TPU v7x, 32 devices: a whole 2x2x4 slice. The times are simulated.
32 devices in a mesh: parts: 2 (over y), gz: 4 (over z), gy: 2 (over x), lc: 2 (over core).
Axes of the slice: x: 2, y: 2, z: 4, core: 2. Of those that a mesh axis runs over, the one named last changes fastest.
Arguments:
- density: float32 [64, 128, 256], P(('parts', 'gz'), 'gy'), parts along dimension 0, may hold values from 0.05 to 1
- void_mask: int32 [64, 128, 256], P(('parts', 'gz'), 'gy'), parts along dimension 0, may hold values 0 or 1
- fixed_mask: int32 [64, 128, 256], P(('parts', 'gz'), 'gy'), parts along dimension 0, may hold values 0 or 1
- displacement: float32 [2, 3, 64, 128, 256], P('lc', None, ('parts', 'gz'), 'gy'), parts along dimension 2, may hold values from -4 to 4
- load_ratio: int32 [4], P('parts'), parts along dimension 0, may hold values from 1 to 8
Outputs:
- gradient: float32 [64, 128, 256], P(('parts', 'gz'), 'gy'), parts along dimension 0
There are 2 independent parts, one for each index of `parts`. A program takes and returns all parts, laid end to end along the dimension named above; each array names one. Nothing has to cross between parts.
All inputs are finite; a program needn't handle non-finite values. No bound on the sum of `void_mask` or of `fixed_mask` on one device may be relied on, other than what follows from the above.
Results may differ from a plain program's by a relative error of at most 0.0001.
Values sent between devices are 32-bit elements; how exact they have to be, the bound alone decides.
No kernel may reach another device: no remote copies, remote signals or barrier semaphores. Data moves between devices by JAX's collectives and lax.ppermute only.
A program may use at most 64 MiB of HBM per device.

v0:
```python
import math

import jax
import jax.numpy as jnp
import numpy as np
from jax import lax
from jax.sharding import PartitionSpec as P


def shifted(block, axis, distance):
    devices = range(lax.axis_size(axis))
    route = [(i - distance, i) for i in devices if i - distance in devices]
    return lax.ppermute(block, axis, route)


def extended_2(array, sides, width):
    for axis, dim in sides:
        peers, length = (lax.axis_size(axis), array.shape[dim])
        up = [(i, (i + 1) % peers) for i in range(peers - 1)]
        down = [(j, i) for i, j in up]
        last = lax.slice_in_dim(array, length - width, length, axis=dim)
        first = lax.slice_in_dim(array, 0, width, axis=dim)
        before = lax.ppermute(last, axis, up)
        after = lax.ppermute(first, axis, down)
        array = jnp.concatenate([before, array, after], axis=dim)
    return array


def element_stiffness():
    poisson = 0.3
    factor = 1.0 / ((1.0 + poisson) * (1.0 - 2.0 * poisson))
    material = np.zeros((6, 6))
    material[:3, :3] = poisson
    for index in range(3):
        material[index, index] = 1.0 - poisson
        material[index + 3, index + 3] = 0.5 - poisson
    material = material * factor
    corners = [(first, second, third) for first in (0, 1) for second in (0, 1) for third in (0, 1)]
    points = [0.5 - 0.5 / math.sqrt(3.0), 0.5 + 0.5 / math.sqrt(3.0)]
    stiffness = np.zeros((24, 24))
    for point_x in points:
        for point_y in points:
            for point_z in points:
                strain = np.zeros((6, 24))
                for corner_index, (first, second, third) in enumerate(corners):
                    along_x = point_x if first else 1.0 - point_x
                    along_y = point_y if second else 1.0 - point_y
                    along_z = point_z if third else 1.0 - point_z
                    sign_x = 1.0 if first else -1.0
                    sign_y = 1.0 if second else -1.0
                    sign_z = 1.0 if third else -1.0
                    deriv_x = sign_x * along_y * along_z
                    deriv_y = along_x * sign_y * along_z
                    deriv_z = along_x * along_y * sign_z
                    column = 3 * corner_index
                    strain[0, column] = deriv_x
                    strain[1, column + 1] = deriv_y
                    strain[2, column + 2] = deriv_z
                    strain[3, column] = deriv_y
                    strain[3, column + 1] = deriv_x
                    strain[4, column + 1] = deriv_z
                    strain[4, column + 2] = deriv_y
                    strain[5, column] = deriv_z
                    strain[5, column + 2] = deriv_x
                stiffness = stiffness + 0.125 * strain.T @ material @ strain
    return stiffness


def cone_offsets():
    result = []
    for shift_x in range(-2, 3):
        for shift_y in range(-2, 3):
            for shift_z in range(-2, 3):
                dist_sq = shift_x * shift_x + shift_y * shift_y + shift_z * shift_z
                if dist_sq < 6.25:
                    result.append((shift_x, shift_y, shift_z, 2.5 - math.sqrt(dist_sq)))
    return result


def shift_depth(field, offset):
    if offset == 0:
        return field
    depth = field.shape[-1]
    position = jnp.arange(depth, dtype=jnp.int32) + offset
    keep = ((position >= 0) & (position < depth)).astype(jnp.float32)
    return jnp.roll(field, -offset, axis=field.ndim - 1) * keep


def cone_filter(padded, shape):
    rows_x, rows_y, depth = shape
    total = jnp.zeros(shape, jnp.float32)
    offsets = cone_offsets()
    for along_depth in range(-2, 3):
        moved_field = shift_depth(padded, along_depth)
        for shift_x, shift_y, shift_z, weight in offsets:
            if shift_z == along_depth:
                total = (
                    total
                    + weight
                    * moved_field[
                        2 + shift_x : 2 + shift_x + rows_x, 2 + shift_y : 2 + shift_y + rows_y
                    ]
                )
    return total


def inside(start, count, total):
    position = start + jnp.arange(-2, count + 2, dtype=jnp.int32)
    return ((position >= 0) & (position < total)).astype(jnp.float32)


def shards(density, void_mask, fixed_mask, displacement, load_ratio):
    rows_x, rows_y, depth = density.shape
    gz_rank = lax.axis_index("gz")
    gy_rank = lax.axis_index("gy")
    case_rank = lax.axis_index("lc")
    total_x = rows_x * lax.axis_size("gz")
    total_y = rows_y * lax.axis_size("gy")
    column_mask = inside(gy_rank * rows_y, rows_y, total_y)[None, :, None]
    free = (1 - fixed_mask).astype(jnp.float32)
    moved = displacement[0] * free[None]
    next_layer = shifted(moved[:, 0:1], "gz", -1)
    extended = jnp.concatenate([moved, next_layer], 1)
    next_column = shifted(extended[:, :, 0:1], "gy", -1)
    extended = jnp.concatenate([extended, next_column], 2)
    stiffness = jnp.asarray(element_stiffness(), jnp.float32)

    def one_layer(layer):
        layers = lax.dynamic_slice_in_dim(extended, layer, 2, 1)
        nodes = []
        for first in (0, 1):
            for second in (0, 1):
                plane = layers[:, first, second : second + rows_y]
                nodes.append(plane)
                nodes.append(shift_depth(plane, 1))
        flat = jnp.stack(nodes, 0).reshape(24, rows_y * depth)
        product = jnp.dot(stiffness, flat, precision=lax.Precision.HIGHEST)
        return jnp.sum(flat * product, 0).reshape(rows_y, depth)

    energy = lax.map(one_layer, jnp.arange(rows_x, dtype=jnp.int32))
    ratios = load_ratio.astype(jnp.float32)
    own_ratio = lax.dynamic_index_in_dim(ratios, case_rank, 0, keepdims=False)
    term = own_ratio / jnp.sum(ratios) * energy
    alive = (1 - void_mask).astype(jnp.float32)
    half = rows_x // 2
    half_shape = (half, rows_y, depth)
    start = case_rank * half
    filled = inside(gz_rank * rows_x + start, half, total_x)[:, None, None] * column_mask
    filled = jnp.broadcast_to(filled, (half + 4, rows_y + 4, depth))
    weight_sum = cone_filter(filled, half_shape)
    density_half = lax.dynamic_slice_in_dim(density, start, half, 0)
    alive_half = lax.dynamic_slice_in_dim(alive, start, half, 0)
    padded_design = extended_2(density_half, ((("gz", "lc"), 0), ("gy", 1)), 2)
    physical = cone_filter(padded_design, half_shape) / weight_sum
    scaling = alive_half * (-3.0 * physical * physical * (1.0 - 0.001)) / weight_sum
    weighted = lax.psum_scatter(term, "lc", scatter_dimension=0, tiled=True)
    sensed = scaling * weighted
    padded_sense = extended_2(sensed, ((("gz", "lc"), 0), ("gy", 1)), 2)
    filtered = alive_half * cone_filter(padded_sense, half_shape)
    gradient = lax.all_gather(filtered, "lc", axis=0, tiled=True)
    return gradient


def solution(mesh):
    placed = (
        P(("parts", "gz"), "gy", None),
        P(("parts", "gz"), "gy", None),
        P(("parts", "gz"), "gy", None),
        P("lc", None, ("parts", "gz"), "gy", None),
        P("parts"),
    )
    return jax.shard_map(
        shards,
        mesh=mesh,
        in_specs=placed,
        out_specs=P(("parts", "gz"), "gy", None),
        check_vma=False,
    )
```

profile of v0, /device:TPU:15, one launch (start us, length us, event | category | flops | bytes accessed | tf_op | source)
XLA Modules:
  0.0 183.5 jit_solution(11901146239948684260)
XLA Ops:
  7.6 1.6 bitcast_multiply_fusion
  10.0 2.1 %collective-permute-start.4 = (f32[3,1,64,256]{3,2,1,0:T(8,128)}, f32[3,1,64,256]{3,2,1,0:T(8,128)S(1)}, u32[]{:S(2)}, u32[]{:S(2)}) collective-permute-start(f32[3,1,64,256]{3,2,1,0:T(8,128)} %slice.1372), channel_id=1, source_target_pairs={{4,0},{8,4},{12,8},{5,1},{9,5},{13,9},{6,2},{10,6},{14,10},{7,3},{... | collective-permute-start | bytes 589832 | tf_op jit(solution)/shard_map/ppermute | solution.py:13
  12.1 2.9 %collective-permute-start.1 = (f32[2,64,256]{2,1,0:T(8,128)S(1)}, f32[2,64,256]{2,1,0:T(8,128)S(1)}, u32[]{:S(2)}, u32[]{:S(2)}) collective-permute-start(f32[2,64,256]{2,1,0:T(8,128)S(1)} %get-tuple-element.109), channel_id=1, source_target_pairs={{1,0},{4,1},{5,4},{8,5},{9,8},{12,9},{13,12},{3,2},{6,3},{7,6},{10... | collective-permute-start | bytes 393224 | tf_op jit(solution)/shard_map/ppermute | solution.py:24
  14.9 3.1 %collective-permute-start = (f32[2,64,256]{2,1,0:T(8,128)S(1)}, f32[2,64,256]{2,1,0:T(8,128)S(1)}, u32[]{:S(2)}, u32[]{:S(2)}) collective-permute-start(f32[2,64,256]{2,1,0:T(8,128)S(1)} %get-tuple-element.108), channel_id=1, source_target_pairs={{0,1},{1,4},{4,5},{5,8},{8,9},{9,12},{12,13},{2,3},{3,6},{6,7},{7,... | collective-permute-start | bytes 393224 | tf_op jit(solution)/shard_map/ppermute | solution.py:23
  20.4 2.2 %collective-permute-start.3 = (f32[8,2,256]{2,1,0:T(2,128)S(1)}, f32[8,2,256]{2,1,0:T(2,128)S(1)}, u32[]{:S(2)}, u32[]{:S(2)}) collective-permute-start(f32[8,2,256]{2,1,0:T(2,128)S(1)} %get-tuple-element.107), channel_id=1, source_target_pairs={{2,0},{3,1},{6,4},{7,5},{10,8},{11,9},{14,12},{15,13},{18,16},{19,... | collective-permute-start | bytes 49160 | tf_op jit(solution)/shard_map/ppermute | solution.py:24
  29.2 2.8 %collective-permute-start.5 = (f32[3,9,1,256]{3,2,1,0:T(1,128)S(1)}, f32[3,9,1,256]{3,2,1,0:T(1,128)S(1)}, u32[]{:S(2)}, u32[]{:S(2)}) collective-permute-start(f32[3,9,1,256]{3,2,1,0:T(1,128)S(1)} %pad_maximum_fusion.9), channel_id=1, source_target_pairs={{2,0},{3,1},{6,4},{7,5},{10,8},{11,9},{14,12},{15,13},{18,16},{19,... | collective-permute-start | bytes 82952 | tf_op jit(solution)/shard_map/ppermute | solution.py:13
  34.7 93.3 %while.11 = (s32[]{:T(128)}, f32[8,64,256]{2,1,0:T(8,128)}, s32[8]{0:T(128)S(1)}, f32[3,9,65,256]{3,2,1,0:T(8,128)}, s32[]{:T(128)}, /*index=5*/s32[]{:T(128)}, s32[]{:T(128)}, s32[]{}, f32[24,24]{1,0:T(8,128)S(1)}) while((s32[]{:T(128)}, f32[8,64,256]{2,1,0:T(8,128)}, s32[8]{0:T(128)S(1)}, f32[3,9,65,256]{3,2,1,0:T(8,128)}, ...), condition=%wide.region_3.4_spmd.clone, body=%wide.region_1.0_spmd.sunk.clone.sunk | while | flops 114410760 | bytes 11738579 | solution.py:140
  44.1 1.6 fusion.281
  55.8 1.6 fusion.281
  67.5 1.6 fusion.281
  79.2 1.6 fusion.281
  90.8 1.6 fusion.281
  102.5 1.6 fusion.281
  125.8 1.6 fusion.281
  128.1 1.9 %broadcast_multiply_fusion = f32[8,64,256]{2,1,0:T(8,128)} fusion(f32[8,64,256]{2,1,0:T(8,128)} %get-tuple-element.32, f32[]{:T(128)S(6)} %div.11), kind=kLoop, calls=%fused_computation.527 | loop fusion | flops 131072 | bytes 1048580 | tf_op jit(solution)/shard_map/mul | solution.py:143
  131.2 1.6 maximum_multiply_fusion.8
  133.5 8.6 %reduce-scatter.2.cloned.1.call-done = f32[4,64,256]{2,1,0:T(8,128)} async-done(((f32[8,64,256]{2,1,0:T(8,128)}), f32[4,64,256]{2,1,0:T(8,128)}) %reduce-scatter.2.cloned.1.call-update) | async-done | bytes 262160 | tf_op jit(solution)/shard_map/reduce_scatter | solution.py:156
  142.1 9.8 %fusion.8 = f32[4,64,256]{2,1,0:T(8,128)S(1)} fusion(f32[4,64,256]{2,1,0:T(8,128)} %reduce-scatter.2.cloned.1.call-done, f32[8,68,256]{2,1,0:T(8,128)} %get-tuple-element.134, f32[8,68,256]{2,1,0:T(8,128)S(1)} %get-tuple-element.133, f32[2,64,256]{2,1,0:T(8,128)} %copy-done.2, f32[4,64,256]{2,1,0:T(8,128)} %copy-done, f32[2,64,256]{2,1,0:T(8,128)} %copy-done.3, ...), kind=kLoop, calls=%fused_computation.61 | loop fusion | flops 20578304 | bytes 36983812 | tf_op jit(solution)/shard_map/mul | solution.py:157
  151.9 2.1 %collective-permute-start.7 = (f32[2,64,256]{2,1,0:T(8,128)S(1)}, f32[2,64,256]{2,1,0:T(8,128)S(1)}, u32[]{:S(2)}, u32[]{:S(2)}) collective-permute-start(f32[2,64,256]{2,1,0:T(8,128)S(1)} %get-tuple-element.111), channel_id=1, source_target_pairs={{1,0},{4,1},{5,4},{8,5},{9,8},{12,9},{13,12},{3,2},{6,3},{7,6},{10... | collective-permute-start | bytes 393224 | tf_op jit(solution)/shard_map/ppermute | solution.py:24
  154.0 3.5 %collective-permute-start.6 = (f32[2,64,256]{2,1,0:T(8,128)S(1)}, f32[2,64,256]{2,1,0:T(8,128)S(1)}, u32[]{:S(2)}, u32[]{:S(2)}) collective-permute-start(f32[2,64,256]{2,1,0:T(8,128)S(1)} %get-tuple-element.110), channel_id=1, source_target_pairs={{0,1},{1,4},{4,5},{5,8},{8,9},{9,12},{12,13},{2,3},{3,6},{6,7},{7,... | collective-permute-start | bytes 393224 | tf_op jit(solution)/shard_map/ppermute | solution.py:23
  159.4 2.2 %collective-permute-start.9 = (f32[8,2,256]{2,1,0:T(2,128)S(1)}, f32[8,2,256]{2,1,0:T(2,128)S(1)}, u32[]{:S(2)}, u32[]{:S(2)}) collective-permute-start(f32[8,2,256]{2,1,0:T(2,128)S(1)} %get-tuple-element.103), channel_id=1, source_target_pairs={{2,0},{3,1},{6,4},{7,5},{10,8},{11,9},{14,12},{15,13},{18,16},{19,... | collective-permute-start | bytes 49160 | tf_op jit(solution)/shard_map/ppermute | solution.py:24
  162.9 3.2 %collective-permute-done.8 = f32[8,2,256]{2,1,0:T(2,128)S(1)} collective-permute-done((f32[8,2,256]{2,1,0:T(2,128)S(1)}, f32[8,2,256]{2,1,0:T(2,128)S(1)}, u32[]{:S(2)}, u32[]{:S(2)}) %collective-permute-start.8) | collective-permute-done | bytes 16416 | tf_op jit(solution)/shard_map/ppermute | solution.py:23
  168.5 2.8 %fusion.88 = f32[4,64,256]{2,1,0:T(8,128)S(1)} fusion(f32[8,68,256]{2,1,0:T(8,128)S(1)} %maximum_multiply_fusion.15, f32[8,68,256]{2,1,0:T(8,128)S(1)} %maximum_multiply_fusion.14, f32[2,64,256]{2,1,0:T(8,128)S(1)} %collective-permute-done.7, f32[4,64,256]{2,1,0:T(8,128)S(1)} %fusion.8, f32[2,64,256]{2,1,0:T(8,128)S(1)} %collective-permute-done.6, ...), kind=kLoop, calls=%fused_computation.142 | loop fusion | flops 11010048 | bytes 20971524 | tf_op jit(solution)/shard_map/mul | solution.py:159
  171.3 4.6 %all_gather.3 = f32[8,64,256]{2,1,0:T(8,128)S(1)} all-gather(f32[4,64,256]{2,1,0:T(8,128)S(1)} %fusion.88), channel_id=1, replica_groups=mesh['parts'=2,'gz'=4,'gy'=2,'lc'=2] {'lc'}, dimensions={0}, use_global_device_ids=true | all-gather | bytes 786432 | tf_op jit(solution)/shard_map/all_gather | solution.py:160
  (222 shorter events, 86.8 us)
Async XLA Ops:
  6.5 135.6 %reduce-scatter.2.cloned.1.call-start = ((), (), s32[]{:S(2)}) async-start(), calls=%async_computation.1 | async-start | bytes 786432 | tf_op jit(solution)/shard_map/reduce_scatter | solution.py:156
  7.6 4.4 %copy-start.8 = (f32[8,64,256]{2,1,0:T(8,128)S(1)}, f32[8,64,256]{2,1,0:T(8,128)}, u32[]{:S(2)}) copy-start(f32[8,64,256]{2,1,0:T(8,128)} %param.8) | copy-start | bytes 1572868
  7.6 12.0 %copy-start.10 = (s32[2]{0:T(128)S(1)}, s32[2]{0:T(128)}, u32[]{:S(2)}) copy-start(s32[2]{0:T(128)} %param.12) | copy-start | bytes 28
  10.0 19.2 %collective-permute-start.4 = (f32[3,1,64,256]{3,2,1,0:T(8,128)}, f32[3,1,64,256]{3,2,1,0:T(8,128)S(1)}, u32[]{:S(2)}, u32[]{:S(2)}) collective-permute-start(f32[3,1,64,256]{3,2,1,0:T(8,128)} %slice.1372), channel_id=1, source_target_pairs={{4,0},{8,4},{12,8},{5,1},{9,5},{13,9},{6,2},{10,6},{14,10},{7,3},{... | collective-permute-start | bytes 589832 | tf_op jit(solution)/shard_map/ppermute | solution.py:13
  12.1 8.3 %collective-permute-start.1 = (f32[2,64,256]{2,1,0:T(8,128)S(1)}, f32[2,64,256]{2,1,0:T(8,128)S(1)}, u32[]{:S(2)}, u32[]{:S(2)}) collective-permute-start(f32[2,64,256]{2,1,0:T(8,128)S(1)} %get-tuple-element.109), channel_id=1, source_target_pairs={{1,0},{4,1},{5,4},{8,5},{9,8},{12,9},{13,12},{3,2},{6,3},{7,6},{10... | collective-permute-start | bytes 393224 | tf_op jit(solution)/shard_map/ppermute | solution.py:24
  14.9 5.4 %collective-permute-start = (f32[2,64,256]{2,1,0:T(8,128)S(1)}, f32[2,64,256]{2,1,0:T(8,128)S(1)}, u32[]{:S(2)}, u32[]{:S(2)}) collective-permute-start(f32[2,64,256]{2,1,0:T(8,128)S(1)} %get-tuple-element.108), channel_id=1, source_target_pairs={{0,1},{1,4},{4,5},{5,8},{8,9},{9,12},{12,13},{2,3},{3,6},{6,7},{7,... | collective-permute-start | bytes 393224 | tf_op jit(solution)/shard_map/ppermute | solution.py:23
  20.2 11.8 %copy-start = (f32[4,64,256]{2,1,0:T(8,128)}, f32[4,64,256]{2,1,0:T(8,128)S(1)}, u32[]{:S(2)}) copy-start(f32[4,64,256]{2,1,0:T(8,128)S(1)} %constant_dynamic-slice_fusion.2) | copy-start | bytes 786436
  20.4 11.6 %copy-start.2 = (f32[2,64,256]{2,1,0:T(8,128)}, f32[2,64,256]{2,1,0:T(8,128)S(1)}, u32[]{:S(2)}) copy-start(f32[2,64,256]{2,1,0:T(8,128)S(1)} %collective-permute-done.1) | copy-start | bytes 393220
  20.4 11.7 %copy-start.3 = (f32[2,64,256]{2,1,0:T(8,128)}, f32[2,64,256]{2,1,0:T(8,128)S(1)}, u32[]{:S(2)}) copy-start(f32[2,64,256]{2,1,0:T(8,128)S(1)} %collective-permute-done) | copy-start | bytes 393220
  20.4 5.4 %collective-permute-start.3 = (f32[8,2,256]{2,1,0:T(2,128)S(1)}, f32[8,2,256]{2,1,0:T(2,128)S(1)}, u32[]{:S(2)}, u32[]{:S(2)}) collective-permute-start(f32[8,2,256]{2,1,0:T(2,128)S(1)} %get-tuple-element.107), channel_id=1, source_target_pairs={{2,0},{3,1},{6,4},{7,5},{10,8},{11,9},{14,12},{15,13},{18,16},{19,... | collective-permute-start | bytes 49160 | tf_op jit(solution)/shard_map/ppermute | solution.py:24
  22.6 4.5 %collective-permute-start.2 = (f32[8,2,256]{2,1,0:T(2,128)S(1)}, f32[8,2,256]{2,1,0:T(2,128)S(1)}, u32[]{:S(2)}, u32[]{:S(2)}) collective-permute-start(f32[8,2,256]{2,1,0:T(2,128)S(1)} %get-tuple-element.106), channel_id=1, source_target_pairs={{0,2},{1,3},{4,6},{5,7},{8,10},{9,11},{12,14},{13,15},{16,18},{17,... | collective-permute-start | bytes 49160 | tf_op jit(solution)/shard_map/ppermute | solution.py:23
  29.2 4.0 %collective-permute-start.5 = (f32[3,9,1,256]{3,2,1,0:T(1,128)S(1)}, f32[3,9,1,256]{3,2,1,0:T(1,128)S(1)}, u32[]{:S(2)}, u32[]{:S(2)}) collective-permute-start(f32[3,9,1,256]{3,2,1,0:T(1,128)S(1)} %pad_maximum_fusion.9), channel_id=1, source_target_pairs={{2,0},{3,1},{6,4},{7,5},{10,8},{11,9},{14,12},{15,13},{18,16},{19,... | collective-permute-start | bytes 82952 | tf_op jit(solution)/shard_map/ppermute | solution.py:13
  33.2 1.5 copy-start.9
  130.1 1.1 copy-start.1
  131.2 1.7 copy-start.4
  131.2 1.7 copy-start.5
  131.2 1.7 copy-start.6
  151.9 6.3 %collective-permute-start.7 = (f32[2,64,256]{2,1,0:T(8,128)S(1)}, f32[2,64,256]{2,1,0:T(8,128)S(1)}, u32[]{:S(2)}, u32[]{:S(2)}) collective-permute-start(f32[2,64,256]{2,1,0:T(8,128)S(1)} %get-tuple-element.111), channel_id=1, source_target_pairs={{1,0},{4,1},{5,4},{8,5},{9,8},{12,9},{13,12},{3,2},{6,3},{7,6},{10... | collective-permute-start | bytes 393224 | tf_op jit(solution)/shard_map/ppermute | solution.py:24
  154.0 5.4 %collective-permute-start.6 = (f32[2,64,256]{2,1,0:T(8,128)S(1)}, f32[2,64,256]{2,1,0:T(8,128)S(1)}, u32[]{:S(2)}, u32[]{:S(2)}) collective-permute-start(f32[2,64,256]{2,1,0:T(8,128)S(1)} %get-tuple-element.110), channel_id=1, source_target_pairs={{0,1},{1,4},{4,5},{5,8},{8,9},{9,12},{12,13},{2,3},{3,6},{6,7},{7,... | collective-permute-start | bytes 393224 | tf_op jit(solution)/shard_map/ppermute | solution.py:23
  159.4 3.5 %collective-permute-start.9 = (f32[8,2,256]{2,1,0:T(2,128)S(1)}, f32[8,2,256]{2,1,0:T(2,128)S(1)}, u32[]{:S(2)}, u32[]{:S(2)}) collective-permute-start(f32[8,2,256]{2,1,0:T(2,128)S(1)} %get-tuple-element.103), channel_id=1, source_target_pairs={{2,0},{3,1},{6,4},{7,5},{10,8},{11,9},{14,12},{15,13},{18,16},{19,... | collective-permute-start | bytes 49160 | tf_op jit(solution)/shard_map/ppermute | solution.py:24
  161.6 4.5 %collective-permute-start.8 = (f32[8,2,256]{2,1,0:T(2,128)S(1)}, f32[8,2,256]{2,1,0:T(2,128)S(1)}, u32[]{:S(2)}, u32[]{:S(2)}) collective-permute-start(f32[8,2,256]{2,1,0:T(2,128)S(1)} %get-tuple-element.102), channel_id=1, source_target_pairs={{0,2},{1,3},{4,6},{5,7},{8,10},{9,11},{12,14},{13,15},{16,18},{17,... | collective-permute-start | bytes 49160 | tf_op jit(solution)/shard_map/ppermute | solution.py:23
  167.4 1.0 copy-start.7
Sparse Core Ops, SparseCore 0:
  130.1 11.9 reduce-scatter.1
where the time goes:
time: 185 us; the launch traced here: 184 us
  local copies, waits for them, and re-layouts  67.7 us (37%)
  other arithmetic  29.2 us (16%)
  starting transfers between devices  23.3 us (13%)
  loops' own time  16.1 us (9%)
  waiting for transfers between devices  15.1 us (8%)
  between operations  15.1 us (8%)
  matrix products  12.4 us (7%)
  blocking collectives  4.59 us (2%)
    while x40, local copies, waits for them, and re-layouts  38 us
    another operation x1, loops' own time, shards(): energy = lax.map(one_layer, jnp.arange(rows_x, dtype=jnp.int32))  16.1 us
    dot_general x8, matrix products, one_layer(): product = jnp.dot(stiffness, flat, precision=lax.Precision.HIGHEST)  12.4 us
    squeeze x8, local copies, waits for them, and re-layouts, one_layer(): plane = layers[:, first, second:second + rows_y]  10.7 us
    mul x1, other arithmetic, shards(): sensed = scaling * weighted  9.76 us
    ppermute x4, starting transfers between devices, extended_2(): after = lax.ppermute(first, axis, down)  9.27 us
    ppermute x4, starting transfers between devices, extended_2(): before = lax.ppermute(last, axis, up)  9.18 us
    reduce_scatter x1, waiting for transfers between devices, shards(): weighted = lax.psum_scatter(term, 'lc', scatter_dimension=0, tiled=True)  8.64 us
  transfers between devices with their start and end apart: 11, of which 6 were waited for; matrix products, arithmetic and copies ran while one was open for 5% of the time, Pallas kernels for 0%

commit v1 on v0

v1 whole, which is shorter than its diff:
```python
import functools
import math

import jax
import jax.numpy as jnp
import numpy as np
from jax import lax
from jax.experimental import pallas as pl
from jax.experimental.pallas import tpu as pltpu
from jax.sharding import PartitionSpec as P

TILE = 8
SLOT = 4
WEIGHT = [2.5 - math.sqrt(squared) for squared in range(7)]


def energy_factors():
    poisson = 0.3
    factor = 1.0 / ((1.0 + poisson) * (1.0 - 2.0 * poisson))
    shear = factor * (0.5 - poisson) / 16.0
    bulk = factor * poisson / 16.0
    twist = factor * (0.5 - poisson) / 48.0
    warp = factor * ((1.0 - poisson) + 2.0 * (0.5 - poisson)) / 144.0
    return shear, bulk, twist, warp


def filled(shape, value=0.0):
    return jnp.full(shape, value, jnp.float32)


def along_depth(field, offset):
    depth = field.shape[-1]
    position = lax.broadcasted_iota(jnp.int32, field.shape, 1)
    keep = position < depth - offset if offset > 0 else position >= -offset
    return jnp.where(keep, pltpu.roll(field, (-offset) % depth, 1), 0.0)


def combined(y0, y1, y2, at):
    plain = y0[at]
    near = (y0[at - 1] + y0[at + 1]) + y1[at]
    corner = y1[at - 1] + y1[at + 1]
    far = (y0[at - 2] + y0[at + 2]) + y2[at]
    knight = (y2[at - 1] + y2[at + 1]) + (y1[at - 2] + y1[at + 2])
    return plain, near, corner, far, knight


def depth_levels(plain, near, corner, far, knight):
    w = WEIGHT
    level0 = w[0] * plain + w[1] * near + w[2] * corner + w[4] * far + w[5] * knight
    level1 = w[1] * plain + w[2] * near + w[3] * corner + w[5] * far + w[6] * knight
    level2 = w[4] * plain + w[5] * near + w[6] * corner
    return level0, level1, level2


def cone_rows(source, row, count):
    y0, y1, y2 = [], [], []
    for layer in range(count + 4):
        here = source[layer, pl.ds(row, TILE), :]
        one = source[layer, pl.ds(row - 1, TILE), :] + source[layer, pl.ds(row + 1, TILE), :]
        y0.append(here)
        y1.append(one)
        if 1 <= layer <= count + 2:
            y2.append(source[layer, pl.ds(row - 2, TILE), :] + source[layer, pl.ds(row + 2, TILE), :])
        else:
            y2.append(None)
        if layer >= 4:
            level0, level1, level2 = depth_levels(*combined(y0, y1, y2, layer - 2))
            total = level0 + (along_depth(level1, 1) + along_depth(level1, -1))
            yield layer - 4, total + (along_depth(level2, 2) + along_depth(level2, -2))


def node_modes(source, layer, row, components=3):
    modes = []
    for component in range(components):
        low = source[component, layer, pl.ds(row, TILE), :]
        high = source[component, layer, pl.ds(row + 1, TILE), :]
        for value in (low + high, high - low):
            after = along_depth(value, 1)
            modes.append(value + after)
            modes.append(after - value)
    return modes


def element_energy(lower, upper):
    shear, bulk, twist, warp = energy_factors()

    def mode(component, first, second, third):
        index = 4 * component + 2 * second + third
        if first:
            return upper[index] - lower[index]
        return upper[index] + lower[index]

    def square(value):
        return value * value

    normal = [mode(0, 1, 0, 0), mode(1, 0, 1, 0), mode(2, 0, 0, 1)]
    trace = normal[0] + normal[1] + normal[2]
    sheared = [
        mode(0, 0, 0, 1) + mode(2, 1, 0, 0),
        mode(1, 0, 0, 1) + mode(2, 0, 1, 0),
        mode(0, 0, 1, 0) + mode(1, 1, 0, 0),
    ]
    bent = [
        (mode(1, 0, 1, 1), mode(0, 1, 0, 1)),
        (mode(2, 0, 1, 1), mode(0, 1, 1, 0)),
        (mode(2, 1, 0, 1), mode(1, 1, 1, 0)),
    ]
    twisted = [mode(0, 0, 1, 1), mode(1, 1, 0, 1), mode(2, 1, 1, 0)]
    warped = [mode(0, 1, 1, 1), mode(1, 1, 1, 1), mode(2, 1, 1, 1)]
    main = 2.0 * (square(normal[0]) + square(normal[1]) + square(normal[2]))
    main = main + (square(sheared[0]) + square(sheared[1]) + square(sheared[2]))
    half = None
    for left, right in bent:
        main = main + (square(left) + square(right))
        term = square(left + right)
        half = term if half is None else half + term
    main = main + 0.5 * half
    twists = square(twisted[0]) + square(twisted[1]) + square(twisted[2])
    twists = twists + square(twisted[0] + twisted[1] + twisted[2])
    warps = square(warped[0]) + square(warped[1]) + square(warped[2])
    return (shear * main + bulk * square(trace)) + (twist * twists + warp * warps)


def flag(condition):
    return jnp.where(condition, 1.0, 0.0).astype(jnp.float32)


def y_flags():
    rank = lax.axis_index("gy")
    return flag(rank > 0), flag(rank < lax.axis_size("gy") - 1)


def edge_rows(first, last, side):
    if side == "first":
        return first[0:SLOT]
    moved_up = pltpu.roll(last, SLOT, 0)
    if side == "last":
        return moved_up[0:SLOT]
    return jnp.where(lax.axis_index("gy") == 0, moved_up, first)[0:SLOT]


def layer_kernel(displacement, fixed, out):
    free = (1 - fixed[0]).astype(jnp.float32)
    for component in range(3):
        out[component] = displacement[0, component, 0] * free


def edge_kernel(sides, layers, *refs):
    (u_first, u_last, f_first, f_last, d_first, d_last, v_first, v_last, d_low, d_high) = refs[:10]
    outs = refs[10:]
    core = lax.axis_index("lc")
    outs[0][...] = jnp.where(core == 0, d_low[...], d_high[...])
    for number, side in enumerate(sides):
        packed, node_corner, design_corner = outs[1 + 3 * number : 4 + 3 * number]
        low, high = [], []
        for layer in range(layers):
            free = edge_rows(
                (1 - f_first[layer]).astype(jnp.float32),
                (1 - f_last[layer]).astype(jnp.float32),
                side,
            )
            for component in range(3):
                moved = free * edge_rows(u_first[0, component, layer], u_last[0, component, layer], side)
                packed[component * layers + layer] = moved
                if layer == 0:
                    node_corner[component] = moved
            design = edge_rows(d_first[layer], d_last[layer], side)
            packed[3 * layers + layer] = design
            if layer < 2:
                low.append(design)
            if layer >= layers - 2:
                high.append(design)
            packed[4 * layers + layer] = edge_rows(
                (1 - v_first[layer]).astype(jnp.float32),
                (1 - v_last[layer]).astype(jnp.float32),
                side,
            )
        for index in range(2):
            design_corner[index] = jnp.where(core == 0, low[index], high[index])


def energy_kernel(count, displacement, fixed, ratio, above, *refs):
    halos, corners = refs[:count], refs[count : 2 * count]
    mine, theirs, nodes, energy = refs[2 * count :]
    layers, rows, depth = fixed.shape
    core = lax.axis_index("lc")
    has_left, has_right = y_flags()
    zero_tile = filled((TILE, depth))
    for component in range(3):
        for layer in range(layers + 1):
            if layer < layers:
                free = (1 - fixed[layer]).astype(jnp.float32)
                nodes[component, layer, TILE : TILE + rows, :] = displacement[0, component, layer] * free
                left, right = (halo[component * layers + layer] for halo in (halos[0], halos[-1]))
            else:
                nodes[component, layer, TILE : TILE + rows, :] = above[component]
                left, right = (corner[component] for corner in (corners[0], corners[-1]))
            nodes[component, layer, 0:TILE, :] = zero_tile
            nodes[component, layer, TILE - SLOT : TILE, :] = left * has_left
            nodes[component, layer, TILE + rows : 2 * TILE + rows, :] = zero_tile
            nodes[component, layer, 2 * TILE + rows : 3 * TILE + rows, :] = zero_tile
            nodes[component, layer, TILE + rows : TILE + rows + SLOT, :] = right * has_right
    total = ratio[0]
    for case in range(1, ratio.shape[0]):
        total = total + ratio[case]
    share = filled((TILE, depth), ratio[core].astype(jnp.float32)) / filled((TILE, depth), total.astype(jnp.float32))
    for row in range(0, rows + 2 * TILE, TILE):
        lower = node_modes(nodes, 0, row)
        for layer in range(layers):
            upper = node_modes(nodes, layer + 1, row)
            energy[layer, row : row + TILE, :] = share * element_energy(lower, upper)
            lower = upper
    half = layers // 2
    mine[...] = energy[pl.ds(core * half, half)]
    theirs[...] = energy[pl.ds((1 - core) * half, half)]


def scaling_kernel(count, density, void, beyond, *refs):
    halos, corners = refs[:count], refs[count : 2 * count]
    scaling, design = refs[2 * count :]
    layers, rows, depth = density.shape
    half = layers // 2
    core = lax.axis_index("lc")
    has_left, has_right = y_flags()
    start = core * half
    zero_tile = filled((TILE, depth))
    origin = 2 * TILE

    def place(slot, middle, left, right):
        design[slot, 0:TILE, :] = zero_tile
        design[slot, TILE : 2 * TILE, :] = zero_tile
        design[slot, origin - SLOT : origin, :] = left * has_left
        design[slot, origin : origin + rows, :] = middle
        design[slot, origin + rows : origin + rows + TILE, :] = zero_tile
        design[slot, origin + rows + TILE : origin + rows + 2 * TILE, :] = zero_tile
        design[slot, origin + rows : origin + rows + SLOT, :] = right * has_right

    for index in range(half + 2):
        source = index + core * (half - 2)
        place(
            index + 2 * (1 - core),
            density[source],
            halos[0][3 * layers + source],
            halos[-1][3 * layers + source],
        )
    for index in range(2):
        place(core * (half + 2) + index, beyond[index], corners[0][index], corners[-1][index])

    total_x = layers * lax.axis_size("gz")
    total_y = rows * lax.axis_size("gy")
    first_layer = lax.axis_index("gz") * layers + start
    first_row = lax.axis_index("gy") * rows
    lane = lax.broadcasted_iota(jnp.int32, (TILE, depth), 1)
    count1 = jnp.where((lane == 0) | (lane == depth - 1), 1.0, 2.0)
    count2 = jnp.where((lane < 2) | (lane >= depth - 2), 1.0, 2.0)
    for row in range(0, rows + 2 * TILE, TILE):
        column = lax.broadcasted_iota(jnp.int32, (TILE, 128), 0) + (first_row + row - TILE)

        def within(offset):
            at = column + offset
            return jnp.where((at >= 0) & (at < total_y), 1.0, 0.0)

        y0, y1, y2 = within(0), within(-1) + within(1), within(-2) + within(2)
        for layer, filtered in cone_rows(design, row + TILE, half):
            at = first_layer + layer

            def inside(offset):
                return flag((at + offset >= 0) & (at + offset < total_x))

            x1 = inside(-1) + inside(1)
            x2 = inside(-2) + inside(2)
            levels = depth_levels(y0, x1 * y0 + y1, x1 * y1, x2 * y0 + y2, x1 * y2 + x2 * y1)
            level0, level1, level2 = (
                jnp.concatenate([level] * (depth // 128), axis=1) for level in levels
            )
            weight_sum = jnp.maximum(level0 + count1 * level1 + count2 * level2, 1.0)
            inverse = 1.0 / weight_sum
            physical = filtered * inverse
            value = (-3.0 * (1.0 - 0.001)) * physical * physical * inverse
            if row == 0:
                alive = has_left * halos[0][4 * layers + start + layer]
                scaling[layer, 0:TILE, :] = zero_tile
                scaling[layer, TILE - SLOT : TILE, :] = value[TILE - SLOT :] * alive
            elif row == rows + TILE:
                alive = has_right * halos[-1][4 * layers + start + layer]
                scaling[layer, row : row + TILE, :] = zero_tile
                scaling[layer, row : row + SLOT, :] = value[0:SLOT] * alive
            else:
                alive = (1 - void[start + layer, row - TILE : row, :]).astype(jnp.float32)
                scaling[layer, row : row + TILE, :] = value * alive


def sensed_kernel(scaling, mine, received, sensed, outgoing):
    half = scaling.shape[0]
    core = lax.axis_index("lc")
    for layer in range(half):
        sensed[layer] = scaling[layer] * (mine[layer] + received[layer])
    outgoing[...] = sensed[pl.ds(core * (half - 2), 2)]


def gradient_kernel(void, own, other, own_beyond, other_beyond, gradient, field):
    layers, rows, depth = void.shape
    half = layers // 2
    core = lax.axis_index("lc")
    field[pl.ds(2 + core * half, half)] = own[...]
    field[pl.ds(2 + (1 - core) * half, half)] = other[...]
    field[pl.ds(core * (layers + 2), 2)] = own_beyond[...]
    field[pl.ds((1 - core) * (layers + 2), 2)] = other_beyond[...]
    for row in range(TILE, TILE + rows, TILE):
        for layer, filtered in cone_rows(field, row, layers):
            alive = (1 - void[layer, row - TILE : row, :]).astype(jnp.float32)
            gradient[layer, row - TILE : row, :] = alive * filtered


def call(kernel, outs, scratch, flops, name, **more):
    return pl.pallas_call(
        kernel,
        out_shape=[jax.ShapeDtypeStruct(shape, jnp.float32) for shape in outs],
        scratch_shapes=[pltpu.VMEM(shape, jnp.float32) for shape in scratch],
        cost_estimate=pl.CostEstimate(flops=flops, bytes_accessed=1 << 20, transcendentals=0),
        compiler_params=pltpu.CompilerParams(vmem_limit_bytes=24 << 20),
        name=name,
        **more,
    )


def whole():
    return pl.BlockSpec(memory_space=pltpu.VMEM)


def shards(density, void_mask, fixed_mask, displacement, load_ratio):
    layers, rows, depth = density.shape
    half = layers // 2
    wide = rows + 2 * TILE
    gz, gy, lc = (lax.axis_size(axis) for axis in ("gz", "gy", "lc"))
    swap = [(0, 1), (1, 0)]
    down = [(z, z - 1) for z in range(1, gz)]
    split = []
    for z in range(gz):
        if z > 0:
            split.append((z * lc, (z - 1) * lc + 1))
        if z < gz - 1:
            split.append((z * lc + 1, (z + 1) * lc))

    def y_pairs(step):
        if gy == 2:
            return [(y, 1 - y) for y in range(gy)]
        return [(y, y + step) for y in range(gy) if 0 <= y + step < gy]

    def node_corner_pairs(step):
        return [(z * gy + y, (z - 1) * gy + peer) for z in range(1, gz) for y, peer in y_pairs(step)]

    def design_corner_pairs(step):
        return [
            ((a // lc * gy + y) * lc + a % lc, (b // lc * gy + peer) * lc + b % lc)
            for a, b in split
            for y, peer in y_pairs(step)
        ]

    block_rows = rows // TILE - 1
    first_u = pl.BlockSpec((1, 3, layers, TILE, depth), lambda i: (0, 0, 0, 0, 0))
    last_u = pl.BlockSpec((1, 3, layers, TILE, depth), lambda i: (0, 0, 0, block_rows, 0))
    first_s = pl.BlockSpec((layers, TILE, depth), lambda i: (0, 0, 0))
    last_s = pl.BlockSpec((layers, TILE, depth), lambda i: (0, block_rows, 0))
    low_s = pl.BlockSpec((2, rows, depth), lambda i: (0, 0, 0))
    high_s = pl.BlockSpec((2, rows, depth), lambda i: (layers // 2 - 1, 0, 0))
    sides = ["both"] if gy == 2 else ["first", "last"]

    (layer_out,) = call(
        layer_kernel,
        [(3, rows, depth)],
        [],
        1 << 18,
        "layer",
        grid=(1,),
        in_specs=[
            pl.BlockSpec((1, 3, 1, rows, depth), lambda i: (0, 0, 0, 0, 0)),
            pl.BlockSpec((1, rows, depth), lambda i: (0, 0, 0)),
        ],
        out_specs=[pl.BlockSpec((3, rows, depth), lambda i: (0, 0, 0))],
    )(displacement, fixed_mask)
    above = lax.ppermute(layer_out, "gz", down)

    out_shapes = [(2, rows, depth)]
    for _ in sides:
        out_shapes += [(5 * layers, SLOT, depth), (3, SLOT, depth), (2, SLOT, depth)]
    edges = call(
        functools.partial(edge_kernel, sides, layers),
        out_shapes,
        [],
        1 << 20,
        "edge",
        grid=(1,),
        in_specs=[first_u, last_u, first_s, last_s, first_s, last_s, first_s, last_s, low_s, high_s],
        out_specs=[pl.BlockSpec(shape, lambda i: (0, 0, 0)) for shape in out_shapes],
    )(
        displacement, displacement, fixed_mask, fixed_mask, density, density,
        void_mask, void_mask, density, density,
    )
    design_out, edges = edges[0], edges[1:]
    packs, node_corners, design_corners = edges[0::3], edges[1::3], edges[2::3]
    steps = [1] if gy == 2 else [-1, 1]
    halos = [lax.ppermute(pack, "gy", y_pairs(step)) for pack, step in zip(packs, steps)]
    corners = [
        lax.ppermute(corner, ("gz", "gy"), node_corner_pairs(step))
        for corner, step in zip(node_corners, steps)
    ]
    beyond = lax.ppermute(design_out, ("gz", "lc"), split)
    outer = [
        lax.ppermute(corner, ("gz", "gy", "lc"), design_corner_pairs(step))
        for corner, step in zip(design_corners, steps)
    ]
    halos, corners, outer = halos[::-1], corners[::-1], outer[::-1]
    count = len(sides)

    (scaling,) = call(
        functools.partial(scaling_kernel, count),
        [(half, wide, depth)],
        [(half + 4, wide + 2 * TILE, depth)],
        1 << 22,
        "scaling",
        in_specs=[whole()] * (3 + 2 * count),
        out_specs=[whole()],
    )(density, void_mask, beyond, *halos, *outer)
    mine, theirs = call(
        functools.partial(energy_kernel, count),
        [(half, wide, depth)] * 2,
        [(3, layers + 1, wide + TILE, depth), (layers, wide, depth)],
        1 << 24,
        "energy",
        in_specs=[whole(), whole(), pl.BlockSpec(memory_space=pltpu.SMEM)] + [whole()] * (1 + 2 * count),
        out_specs=[whole()] * 2,
    )(displacement, fixed_mask, load_ratio, above, *halos, *corners)
    received = lax.ppermute(theirs, "lc", swap)
    sensed, outgoing = call(
        sensed_kernel,
        [(half, wide, depth), (2, wide, depth)],
        [],
        1 << 20,
        "sensed",
        in_specs=[whole()] * 3,
        out_specs=[whole()] * 2,
    )(scaling, mine, received)
    own_beyond = lax.ppermute(outgoing, ("gz", "lc"), split)
    other = lax.ppermute(sensed, "lc", swap)
    other_beyond = lax.ppermute(own_beyond, "lc", swap)
    (gradient,) = call(
        gradient_kernel,
        [(layers, rows, depth)],
        [(layers + 4, wide, depth)],
        1 << 23,
        "gradient",
        in_specs=[whole()] * 5,
        out_specs=[whole()],
    )(void_mask, sensed, other, own_beyond, other_beyond)
    return gradient


def solution(mesh):
    placed = (
        P(("parts", "gz"), "gy", None),
        P(("parts", "gz"), "gy", None),
        P(("parts", "gz"), "gy", None),
        P("lc", None, ("parts", "gz"), "gy", None),
        P("parts"),
    )
    return jax.shard_map(
        shards,
        mesh=mesh,
        in_specs=placed,
        out_specs=P(("parts", "gz"), "gy", None),
        check_vma=False,
    )
```

time: 185 us -> 41.5 us (0.22)
  the two profiles are of different devices: /device:TPU:15 before, /device:TPU:0 now
where the time goes in v1:
time: 41.5 us; the launch traced here: 41.3 us
  starting transfers between devices  22.6 us (54%)
  Pallas kernels  9.49 us (23%)
  waiting for transfers between devices  6.52 us (16%)
  local copies, waits for them, and re-layouts  2.46 us (6%)
    ppermute x1, starting transfers between devices, shards(): other = lax.ppermute(sensed, 'lc', swap)  10.2 us
    ppermute x1, waiting for transfers between devices, shards(): lax.ppermute(corner, ('gz', 'gy'), node_corner_pairs(step))  5.48 us
    pallas_call x1, Pallas kernels, shards(): call(functools.partial(energy_kernel, count), [(half, wide, depth)] * 2,...  5.34 us
    ppermute x1, starting transfers between devices, shards(): other_beyond = lax.ppermute(own_beyond, 'lc', swap)  4.64 us
    ppermute x1, starting transfers between devices, shards(): lax.ppermute(pack, 'gy', y_pairs(step))  3.03 us
    pallas_call x1, Pallas kernels, shards(): call(gradient_kernel, [(layers, rows, depth)], [(layers + 4, wide, depth)...  2.5 us
    unnamed x10, local copies, waits for them, and re-layouts  2.46 us
    pallas_call x1, Pallas kernels, shards(): call(functools.partial(scaling_kernel, count), [(half, wide, depth)], [(h...  1.49 us
  transfers between devices with their start and end apart: 9, of which 2 were waited for; matrix products, arithmetic and copies ran while one was open for 0% of the time, Pallas kernels for 4%

profile of v1, /device:TPU:0, one launch (start us, length us, event | category | flops | bytes accessed | tf_op | source)
XLA Modules:
  0.0 41.3 jit_solution(11929088500937680960)
XLA Ops:
  0.0 1.4 %copy-done = f32[1,3,8,64,256]{4,3,2,1,0:T(8,128)S(1)} copy-done((f32[1,3,8,64,256]{4,3,2,1,0:T(8,128)S(1)}, f32[1,3,8,64,256]{4,3,2,1,0:T(8,128)}, u32[]{:S(2)}) %copy-start) | copy-done | bytes 1572888
  1.4 1.0 %copy-done.3 = s32[8,64,256]{2,1,0:T(8,128)S(1)} copy-done((s32[8,64,256]{2,1,0:T(8,128)S(1)}, s32[8,64,256]{2,1,0:T(8,128)}, u32[]{:S(2)}) %copy-start.3) | copy-done | bytes 524312
  2.5 0.0 copy-start.4
  2.5 1.4 %collective-permute-start.3 = (f32[3,64,256]{2,1,0:T(8,128)S(1)}, f32[3,64,256]{2,1,0:T(8,128)S(1)}, u32[]{:S(2)}, u32[]{:S(2)}) collective-permute-start(f32[3,64,256]{2,1,0:T(8,128)S(1)} %layer.1), channel_id=1, source_target_pairs={{4,0},{8,4},{12,8},{5,1},{9,5},{13,9},{6,2},{10,6},{14,10},{7,3},{... | collective-permute-start | bytes 589832 | tf_op jit(solution)/shard_map/ppermute | solution.py:382
  3.9 0.1 edge.1
  4.0 3.0 %collective-permute-start.1 = (f32[40,4,256]{2,1,0:T(4,128)S(1)}, f32[40,4,256]{2,1,0:T(4,128)S(1)}, u32[]{:S(2)}, u32[]{:S(2)}) collective-permute-start(f32[40,4,256]{2,1,0:T(4,128)S(1)} %get-tuple-element.14), channel_id=1, source_target_pairs={{0,2},{2,0},{1,3},{3,1},{4,6},{6,4},{5,7},{7,5},{8,10},{10,8},{9,1... | collective-permute-start | bytes 491528 | tf_op jit(solution)/shard_map/ppermute | solution.py:403
  7.1 1.3 %collective-permute-start.4 = (f32[3,4,256]{2,1,0:T(4,128)S(1)}, f32[3,4,256]{2,1,0:T(4,128)S(1)}, u32[]{:S(2)}, u32[]{:S(2)}) collective-permute-start(f32[3,4,256]{2,1,0:T(4,128)S(1)} %get-tuple-element.16), channel_id=1, source_target_pairs={{4,2},{6,0},{8,6},{10,4},{12,10},{14,8},{5,3},{7,1},{9,7},{11,5},{... | collective-permute-start | bytes 36872 | tf_op jit(solution)/shard_map/ppermute | solution.py:405
  8.3 5.5 %collective-permute-done.4.refs_1_ = f32[3,4,256]{2,1,0:T(4,128)S(1)} collective-permute-done((f32[3,4,256]{2,1,0:T(4,128)S(1)}, f32[3,4,256]{2,1,0:T(4,128)S(1)}, u32[]{:S(2)}, u32[]{:S(2)}) %collective-permute-start.4) | collective-permute-done | bytes 12320 | tf_op jit(solution)/shard_map/ppermute | solution.py:405
  13.8 0.0 collective-permute-done.1.refs_0_
  13.8 0.0 collective-permute-done.3.above
  13.8 5.3 %energy.1 = (f32[4,80,256]{2,1,0:T(8,128)S(1)}, f32[4,80,256]{2,1,0:T(8,128)S(1)}) custom-call(f32[1,3,8,64,256]{4,3,2,1,0:T(8,128)S(1)} %copy-done, s32[8,64,256]{2,1,0:T(8,128)S(1)} %copy-done.3, s32[2]{0:T(128)S(1)} %copy-done.4, f32[3,64,256]{2,1,0:T(8,128)S(1)} %collective-permute-done.3.above, f32[40,4,256]{2,1,0:T(4,128)S(1)} %collective-permute-done.1.refs_0_, ...), custom_call_target="tpu_custom_call" | custom-call | flops 16777216 | bytes 1048576 | tf_op jit(solution)/shard_map/energy/pallas_call | solution.py:425
  19.2 0.1 collective-permute-start.5
  19.3 0.7 %collective-permute-start = (f32[2,64,256]{2,1,0:T(8,128)S(1)}, f32[2,64,256]{2,1,0:T(8,128)S(1)}, u32[]{:S(2)}, u32[]{:S(2)}) collective-permute-start(f32[2,64,256]{2,1,0:T(8,128)S(1)} %get-tuple-element.13), channel_id=1, source_target_pairs={{1,4},{4,1},{5,8},{8,5},{9,12},{12,9},{3,6},{6,3},{7,10},{10,7},{1... | collective-permute-start | bytes 393224 | tf_op jit(solution)/shard_map/ppermute | solution.py:408
  19.9 0.7 %collective-permute-start.2 = (f32[2,4,256]{2,1,0:T(4,128)S(1)}, f32[2,4,256]{2,1,0:T(4,128)S(1)}, u32[]{:S(2)}, u32[]{:S(2)}) collective-permute-start(f32[2,4,256]{2,1,0:T(4,128)S(1)} %get-tuple-element.15), channel_id=1, source_target_pairs={{1,6},{3,4},{4,3},{6,1},{5,10},{7,8},{8,7},{10,5},{9,14},{11,12},{... | collective-permute-start | bytes 24584 | tf_op jit(solution)/shard_map/ppermute | solution.py:410
  20.6 0.0 collective-permute-done.2.refs_1_
  20.6 1.5 %scaling.1 = f32[4,80,256]{2,1,0:T(8,128)S(1)} custom-call(f32[8,64,256]{2,1,0:T(8,128)S(1)} %copy-done.1, s32[8,64,256]{2,1,0:T(8,128)S(1)} %copy-done.2, f32[2,64,256]{2,1,0:T(8,128)S(1)} %collective-permute-done.beyond, f32[40,4,256]{2,1,0:T(4,128)S(1)} %collective-permute-done.1.refs_0_, f32[2,4,256]{2,1,0:T(4,128)S(1)} %collective-permute-done.2.refs_1_), custom_call_target="tpu_custom_call" | custom-call | flops 4194304 | bytes 1048576 | tf_op jit(solution)/shard_map/scaling/pallas_call | solution.py:416
  22.1 0.0 collective-permute-done.5.received
  22.1 0.1 sensed.1
  22.2 0.7 %collective-permute-start.7 = (f32[2,80,256]{2,1,0:T(8,128)S(1)}, f32[2,80,256]{2,1,0:T(8,128)S(1)}, u32[]{:S(2)}, u32[]{:S(2)}) collective-permute-start(f32[2,80,256]{2,1,0:T(8,128)S(1)} %get-tuple-element.20), channel_id=1, source_target_pairs={{1,4},{4,1},{5,8},{8,5},{9,12},{12,9},{3,6},{6,3},{7,10},{10,7},{1... | collective-permute-start | bytes 491528 | tf_op jit(solution)/shard_map/ppermute | solution.py:444
  22.9 10.2 %collective-permute-start.6 = (f32[4,80,256]{2,1,0:T(8,128)S(1)}, f32[4,80,256]{2,1,0:T(8,128)S(1)}, u32[]{:S(2)}, u32[]{:S(2)}) collective-permute-start(f32[4,80,256]{2,1,0:T(8,128)S(1)} %get-tuple-element.19.own), channel_id=1, source_target_pairs={{0,1},{1,0},{2,3},{3,2},{4,5},{5,4},{6,7},{7,6},{8,9},{9,8},{10,11... | collective-permute-start | bytes 983048 | tf_op jit(solution)/shard_map/ppermute | solution.py:445
  33.1 0.0 collective-permute-done.7.own_beyond
  33.1 4.6 %collective-permute-start.8 = (f32[2,80,256]{2,1,0:T(8,128)S(1)}, f32[2,80,256]{2,1,0:T(8,128)S(1)}, u32[]{:S(2)}, u32[]{:S(2)}) collective-permute-start(f32[2,80,256]{2,1,0:T(8,128)S(1)} %collective-permute-done.7.own_beyond), channel_id=1, source_target_pairs={{0,1},{1,0},{2,3},{3,2},{4,5},{5,4},{6,7},{7,6},{8,9},{9,8},{10,11... | collective-permute-start | bytes 491528 | tf_op jit(solution)/shard_map/ppermute | solution.py:446
  37.7 1.0 %collective-permute-done.8.other_beyond = f32[2,80,256]{2,1,0:T(8,128)S(1)} collective-permute-done((f32[2,80,256]{2,1,0:T(8,128)S(1)}, f32[2,80,256]{2,1,0:T(8,128)S(1)}, u32[]{:S(2)}, u32[]{:S(2)}) %collective-permute-start.8) | collective-permute-done | bytes 163872 | tf_op jit(solution)/shard_map/ppermute | solution.py:446
  38.8 2.5 %gradient.1 = f32[8,64,256]{2,1,0:T(8,128)} custom-call(s32[8,64,256]{2,1,0:T(8,128)S(1)} %copy-done.2, f32[4,80,256]{2,1,0:T(8,128)S(1)} %get-tuple-element.19.own, f32[4,80,256]{2,1,0:T(8,128)S(1)} %collective-permute-done.6.other, f32[2,80,256]{2,1,0:T(8,128)S(1)} %collective-permute-done.7.own_beyond, f32[2,80,256]{2,1,0:T(8,128)S(1)} %collective-permute-done.8.other_beyond), custom_call_target="tpu_custom_call" | custom-call | flops 8388608 | bytes 1048576 | tf_op jit(solution)/shard_map/gradient/pallas_call | solution.py:447
  (10 shorter events, 0.0 us)
Async XLA Ops:
  0.0 1.4 %copy-start = (f32[1,3,8,64,256]{4,3,2,1,0:T(8,128)S(1)}, f32[1,3,8,64,256]{4,3,2,1,0:T(8,128)}, u32[]{:S(2)}) copy-start(f32[1,3,8,64,256]{4,3,2,1,0:T(8,128)} %displacement.3) | copy-start | bytes 4718596
  1.4 1.0 %copy-start.3 = (s32[8,64,256]{2,1,0:T(8,128)S(1)}, s32[8,64,256]{2,1,0:T(8,128)}, u32[]{:S(2)}) copy-start(s32[8,64,256]{2,1,0:T(8,128)} %fixed.3) | copy-start | bytes 1572868
  2.5 1.5 %copy-start.1 = (f32[8,64,256]{2,1,0:T(8,128)S(1)}, f32[8,64,256]{2,1,0:T(8,128)}, u32[]{:S(2)}) copy-start(f32[8,64,256]{2,1,0:T(8,128)} %density.1) | copy-start | bytes 1572868
  2.5 1.5 %copy-start.2 = (s32[8,64,256]{2,1,0:T(8,128)S(1)}, s32[8,64,256]{2,1,0:T(8,128)}, u32[]{:S(2)}) copy-start(s32[8,64,256]{2,1,0:T(8,128)} %void.3) | copy-start | bytes 1572868
  2.5 11.4 %copy-start.4 = (s32[2]{0:T(128)S(1)}, s32[2]{0:T(128)}, u32[]{:S(2)}) copy-start(s32[2]{0:T(128)} %ratio.1) | copy-start | bytes 28
  2.5 11.3 %collective-permute-start.3 = (f32[3,64,256]{2,1,0:T(8,128)S(1)}, f32[3,64,256]{2,1,0:T(8,128)S(1)}, u32[]{:S(2)}, u32[]{:S(2)}) collective-permute-start(f32[3,64,256]{2,1,0:T(8,128)S(1)} %layer.1), channel_id=1, source_target_pairs={{4,0},{8,4},{12,8},{5,1},{9,5},{13,9},{6,2},{10,6},{14,10},{7,3},{... | collective-permute-start | bytes 589832 | tf_op jit(solution)/shard_map/ppermute | solution.py:382
  4.0 9.8 %collective-permute-start.1 = (f32[40,4,256]{2,1,0:T(4,128)S(1)}, f32[40,4,256]{2,1,0:T(4,128)S(1)}, u32[]{:S(2)}, u32[]{:S(2)}) collective-permute-start(f32[40,4,256]{2,1,0:T(4,128)S(1)} %get-tuple-element.14), channel_id=1, source_target_pairs={{0,2},{2,0},{1,3},{3,1},{4,6},{6,4},{5,7},{7,5},{8,10},{10,8},{9,1... | collective-permute-start | bytes 491528 | tf_op jit(solution)/shard_map/ppermute | solution.py:403
  7.1 6.8 %collective-permute-start.4 = (f32[3,4,256]{2,1,0:T(4,128)S(1)}, f32[3,4,256]{2,1,0:T(4,128)S(1)}, u32[]{:S(2)}, u32[]{:S(2)}) collective-permute-start(f32[3,4,256]{2,1,0:T(4,128)S(1)} %get-tuple-element.16), channel_id=1, source_target_pairs={{4,2},{6,0},{8,6},{10,4},{12,10},{14,8},{5,3},{7,1},{9,7},{11,5},{... | collective-permute-start | bytes 36872 | tf_op jit(solution)/shard_map/ppermute | solution.py:405
  19.2 2.9 %collective-permute-start.5 = (f32[4,80,256]{2,1,0:T(8,128)S(1)}, f32[4,80,256]{2,1,0:T(8,128)S(1)}, u32[]{:S(2)}, u32[]{:S(2)}) collective-permute-start(f32[4,80,256]{2,1,0:T(8,128)S(1)} %get-tuple-element.18), channel_id=1, source_target_pairs={{0,1},{1,0},{2,3},{3,2},{4,5},{5,4},{6,7},{7,6},{8,9},{9,8},{10,11... | collective-permute-start | bytes 983048 | tf_op jit(solution)/shard_map/ppermute | solution.py:434
  19.3 1.4 %collective-permute-start = (f32[2,64,256]{2,1,0:T(8,128)S(1)}, f32[2,64,256]{2,1,0:T(8,128)S(1)}, u32[]{:S(2)}, u32[]{:S(2)}) collective-permute-start(f32[2,64,256]{2,1,0:T(8,128)S(1)} %get-tuple-element.13), channel_id=1, source_target_pairs={{1,4},{4,1},{5,8},{8,5},{9,12},{12,9},{3,6},{6,3},{7,10},{10,7},{1... | collective-permute-start | bytes 393224 | tf_op jit(solution)/shard_map/ppermute | solution.py:408
  19.9 0.7 %collective-permute-start.2 = (f32[2,4,256]{2,1,0:T(4,128)S(1)}, f32[2,4,256]{2,1,0:T(4,128)S(1)}, u32[]{:S(2)}, u32[]{:S(2)}) collective-permute-start(f32[2,4,256]{2,1,0:T(4,128)S(1)} %get-tuple-element.15), channel_id=1, source_target_pairs={{1,6},{3,4},{4,3},{6,1},{5,10},{7,8},{8,7},{10,5},{9,14},{11,12},{... | collective-permute-start | bytes 24584 | tf_op jit(solution)/shard_map/ppermute | solution.py:410
  22.2 10.9 %collective-permute-start.7 = (f32[2,80,256]{2,1,0:T(8,128)S(1)}, f32[2,80,256]{2,1,0:T(8,128)S(1)}, u32[]{:S(2)}, u32[]{:S(2)}) collective-permute-start(f32[2,80,256]{2,1,0:T(8,128)S(1)} %get-tuple-element.20), channel_id=1, source_target_pairs={{1,4},{4,1},{5,8},{8,5},{9,12},{12,9},{3,6},{6,3},{7,10},{10,7},{1... | collective-permute-start | bytes 491528 | tf_op jit(solution)/shard_map/ppermute | solution.py:444
  22.9 15.9 %collective-permute-start.6 = (f32[4,80,256]{2,1,0:T(8,128)S(1)}, f32[4,80,256]{2,1,0:T(8,128)S(1)}, u32[]{:S(2)}, u32[]{:S(2)}) collective-permute-start(f32[4,80,256]{2,1,0:T(8,128)S(1)} %get-tuple-element.19.own), channel_id=1, source_target_pairs={{0,1},{1,0},{2,3},{3,2},{4,5},{5,4},{6,7},{7,6},{8,9},{9,8},{10,11... | collective-permute-start | bytes 983048 | tf_op jit(solution)/shard_map/ppermute | solution.py:445
  33.1 5.7 %collective-permute-start.8 = (f32[2,80,256]{2,1,0:T(8,128)S(1)}, f32[2,80,256]{2,1,0:T(8,128)S(1)}, u32[]{:S(2)}, u32[]{:S(2)}) collective-permute-start(f32[2,80,256]{2,1,0:T(8,128)S(1)} %collective-permute-done.7.own_beyond), channel_id=1, source_target_pairs={{0,1},{1,0},{2,3},{3,2},{4,5},{5,4},{6,7},{7,6},{8,9},{9,8},{10,11... | collective-permute-start | bytes 491528 | tf_op jit(solution)/shard_map/ppermute | solution.py:446

commit v2 on v1

v2 whole, which is shorter than its diff:
```python
import functools
import math

import jax
import jax.numpy as jnp
from jax import lax
from jax.experimental import pallas as pl
from jax.experimental.pallas import tpu as pltpu
from jax.sharding import PartitionSpec as P

TILE = 8
SLOT = 4
LANES = 128
VMEM_BYTES = 67043328
WEIGHT = [2.5 - math.sqrt(squared) for squared in range(7)]


def energy_factors():
    poisson = 0.3
    factor = 1.0 / ((1.0 + poisson) * (1.0 - 2.0 * poisson))
    shear = factor * (0.5 - poisson) / 16.0
    bulk = factor * poisson / 16.0
    twist = factor * (0.5 - poisson) / 48.0
    warp = factor * ((1.0 - poisson) + 2.0 * (0.5 - poisson)) / 144.0
    return shear, bulk, twist, warp


def filled(shape, value=0.0):
    return jnp.full(shape, value, jnp.float32)


def lane_index():
    return lax.broadcasted_iota(jnp.int32, (TILE, LANES), 1)


def row_index():
    return lax.broadcasted_iota(jnp.int32, (TILE, LANES), 0)


def parts_of(depth):
    return [slice(at, at + LANES) for at in range(0, depth, LANES)]


def along_depth(values, offset):
    lane = lane_index()
    turned = [pltpu.roll(value, (-offset) % LANES, 1) for value in values]
    zero = filled((TILE, LANES))
    if offset > 0:
        keep, beyond = lane < LANES - offset, turned[1:] + [zero]
    else:
        keep, beyond = lane >= -offset, [zero] + turned[:-1]
    return [jnp.where(keep, own, other) for own, other in zip(turned, beyond)]


def along_rows(tiles, offset):
    turned = [pltpu.roll(tile, (-offset) % TILE, 0) for tile in tiles]
    if offset > 0:
        keep, beyond = row_index() < TILE - offset, turned[1:] + turned[:1]
    else:
        keep, beyond = row_index() >= -offset, turned[-1:] + turned[:-1]
    return [jnp.where(keep, own, other) for own, other in zip(turned, beyond)]


def row_sums(source, sums, layers, wide):
    depth = source.shape[-1]
    for layer in layers:
        for part in parts_of(depth):
            tiles = [source[layer, row : row + TILE, part] for row in range(0, wide, TILE)]
            for number, distance in enumerate((1, 2)):
                ahead, behind = along_rows(tiles, distance), along_rows(tiles, -distance)
                for index, (one, other) in enumerate(zip(ahead, behind)):
                    sums[layer, number, TILE * index : TILE * (index + 1), part] = one + other


def depth_levels(plain, near, corner, far, knight):
    w = WEIGHT
    level0 = w[0] * plain + w[1] * near + w[2] * corner + w[4] * far + w[5] * knight
    level1 = w[1] * plain + w[2] * near + w[3] * corner + w[5] * far + w[6] * knight
    level2 = w[4] * plain + w[5] * near + w[6] * corner
    return level0, level1, level2


def cone_tile(source, sums, layer, row):
    results = []
    for part in parts_of(source.shape[-1]):

        def plane(at):
            return source[layer + at, row : row + TILE, part]

        def summed(at, number):
            return sums[layer + at, number, row : row + TILE, part]

        near = (plane(-1) + plane(1)) + summed(0, 0)
        corner = summed(-1, 0) + summed(1, 0)
        far = (plane(-2) + plane(2)) + summed(0, 1)
        knight = (summed(-1, 1) + summed(1, 1)) + (summed(-2, 0) + summed(2, 0))
        results.append(depth_levels(plane(0), near, corner, far, knight))
    level1 = [levels[1] for levels in results]
    level2 = [levels[2] for levels in results]
    shifted = [along_depth(level1, 1), along_depth(level1, -1), along_depth(level2, 2), along_depth(level2, -2)]
    return [
        levels[0] + ((one + two) + (three + four))
        for levels, one, two, three, four in zip(results, *shifted)
    ]


def row_modes(nodes, modes, layer, slot, wide):
    for component in range(3):
        for part in parts_of(nodes.shape[-1]):
            tiles = [nodes[component, layer, row : row + TILE, part] for row in range(0, wide, TILE)]
            for index, (low, high) in enumerate(zip(tiles, along_rows(tiles, 1))):
                at = slice(TILE * index, TILE * (index + 1))
                modes[slot, 2 * component, at, part] = low + high
                modes[slot, 2 * component + 1, at, part] = high - low


def node_modes(modes, slot, row):
    parts = parts_of(modes.shape[-1])
    found = [[] for _ in parts]
    for number in range(6):
        values = [modes[slot, number, row : row + TILE, part] for part in parts]
        for mine, value, after in zip(found, values, along_depth(values, 1)):
            mine.append(value + after)
            mine.append(after - value)
    return found


def element_energy(lower, upper, scale):
    def mode(component, first, second, third):
        index = 4 * component + 2 * second + third
        if first:
            return upper[index] - lower[index]
        return upper[index] + lower[index]

    def square(value):
        return value * value

    normal = [mode(0, 1, 0, 0), mode(1, 0, 1, 0), mode(2, 0, 0, 1)]
    trace = normal[0] + normal[1] + normal[2]
    main = square(mode(0, 0, 0, 1) + mode(2, 1, 0, 0))
    main = main + square(mode(1, 0, 0, 1) + mode(2, 0, 1, 0))
    main = main + square(mode(0, 0, 1, 0) + mode(1, 1, 0, 0))
    bent = [
        (mode(1, 0, 1, 1), mode(0, 1, 0, 1)),
        (mode(2, 0, 1, 1), mode(0, 1, 1, 0)),
        (mode(2, 1, 0, 1), mode(1, 1, 1, 0)),
    ]
    half = None
    for left, right in bent:
        main = main + square(left + right)
        term = square(left - right)
        half = term if half is None else half + term
    main = main + 2.0 * (square(normal[0]) + square(normal[1]) + square(normal[2]))
    main = main + 0.5 * half
    twisted = [mode(0, 0, 1, 1), mode(1, 1, 0, 1), mode(2, 1, 1, 0)]
    twists = square(twisted[0]) + square(twisted[1]) + square(twisted[2])
    twists = twists + square(twisted[0] + twisted[1] + twisted[2])
    warps = square(mode(0, 1, 1, 1)) + square(mode(1, 1, 1, 1)) + square(mode(2, 1, 1, 1))
    shear, bulk, twist, warp = scale
    return (shear * main + bulk * square(trace)) + (twist * twists + warp * warps)


def shares(ratio):
    total = ratio[0]
    for case in range(1, ratio.shape[0]):
        total = total + ratio[case]
    total = filled((TILE, LANES), total.astype(jnp.float32))

    def scale(case):
        share = filled((TILE, LANES), ratio[case].astype(jnp.float32)) / total
        return [factor * share for factor in energy_factors()]

    return scale


def flag(condition):
    return jnp.where(condition, 1.0, 0.0).astype(jnp.float32)


def y_flags():
    rank = lax.axis_index("gy")
    return flag(rank > 0), flag(rank < lax.axis_size("gy") - 1)


def free_of(mask):
    return (1 - mask).astype(jnp.float32)


def edge_rows(first, last, side):
    if side == "first":
        return first[0:SLOT]
    moved_up = pltpu.roll(last, SLOT, 0)
    if side == "last":
        return moved_up[0:SLOT]
    return jnp.where(lax.axis_index("gy") == 0, moved_up, first)[0:SLOT]


def layer_kernel(displacement, fixed, density, crossing, straight, nodes, mask, sems):
    layers = density.shape[0]
    core = lax.axis_index("lc")
    copies = [
        pltpu.make_async_copy(displacement.at[0, :, 0], nodes, sems.at[0]),
        pltpu.make_async_copy(fixed.at[0], mask, sems.at[1]),
        pltpu.make_async_copy(
            density.at[pl.ds(core * (layers - 2), 2)], crossing.at[pl.ds(3, 2)], sems.at[2]
        ),
    ]
    for copy in copies:
        copy.start()
    for copy in copies:
        copy.wait()
    free = free_of(mask[...])
    for component in range(3):
        moved = nodes[component] * free
        crossing[component] = moved
        straight[component] = moved


def edge_kernel(sides, displacement, fixed, density, void, *outs):
    layers, rows, _ = density.shape
    core = lax.axis_index("lc")
    first, last = slice(0, TILE), slice(rows - TILE, rows)
    for number, side in enumerate(sides):
        packed, crossing, straight = outs[3 * number : 3 * number + 3]
        low, high = [], []
        for layer in range(layers):
            free = edge_rows(free_of(fixed[layer, first]), free_of(fixed[layer, last]), side)
            for component in range(3):
                moved = free * edge_rows(
                    displacement[0, component, layer, first], displacement[0, component, layer, last], side
                )
                packed[component * layers + layer] = moved
                if layer == 0:
                    crossing[component] = moved
                    straight[component] = moved
            design = edge_rows(density[layer, first], density[layer, last], side)
            packed[3 * layers + layer] = design
            if layer < 2:
                low.append(design)
            if layer >= layers - 2:
                high.append(design)
            packed[4 * layers + layer] = edge_rows(
                free_of(void[layer, first]), free_of(void[layer, last]), side
            )
        for index in range(2):
            crossing[3 + index] = jnp.where(core == 0, low[index], high[index])


def energy_kernel(count, displacement, fixed, ratio, *refs):
    halos = refs[:count]
    mine, theirs, last, nodes, modes, energy = refs[count:]
    layers, rows, depth = fixed.shape
    wide = rows + TILE
    half = layers // 2
    core = lax.axis_index("lc")
    has_left, has_right = y_flags()
    for layer in range(layers):
        free = free_of(fixed[layer])
        for component in range(3):
            nodes[component, layer, 0:rows, :] = displacement[0, component, layer] * free
            at = component * layers + layer
            nodes[component, layer, rows : rows + SLOT, :] = halos[-1][at] * has_right
            nodes[component, layer, rows + SLOT : wide, :] = halos[0][at] * has_left
        row_modes(nodes, modes, layer, layer, wide)
    scale = shares(ratio)(core)
    for row in range(0, wide, TILE):
        lower = node_modes(modes, 0, row)
        for layer in range(layers - 1):
            upper = node_modes(modes, layer + 1, row)
            for part, below, above in zip(parts_of(depth), lower, upper):
                energy[layer, row : row + TILE, part] = element_energy(below, above, scale)
            lower = upper
    for component in range(3):
        last[component] = nodes[component, layers - 1]
    mine[0 : half - 1] = energy[pl.ds(core * half, half - 1)]

    @pl.when(core == 0)
    def _():
        mine[half - 1] = energy[half - 1]
        theirs[0 : half - 1] = energy[half : layers - 1]
        theirs[half : half + 3] = nodes[:, layers - 1]

    @pl.when(core == 1)
    def _():
        theirs[0:half] = energy[0:half]


def scaling_kernel(count, density, void, beyond, *refs):
    halos, corners = refs[:count], refs[count : 2 * count]
    scaling, design, sums, halo_alive = refs[2 * count :]
    layers, rows, depth = density.shape
    wide = rows + TILE
    half = layers // 2
    core = lax.axis_index("lc")
    has_left, has_right = y_flags()
    start = core * half

    def place(slot, middle, left, right):
        design[slot, 0:rows, :] = middle
        design[slot, rows : rows + SLOT, :] = right * has_right
        design[slot, rows + SLOT : wide, :] = left * has_left

    for index in range(half + 2):
        source = index + core * (half - 2)
        at = 3 * layers + source
        place(index + 2 * (1 - core), density[source], halos[0][at], halos[-1][at])
    for index in range(2):
        place(core * (half + 2) + index, beyond[3 + index], corners[0][3 + index], corners[-1][3 + index])
    for layer in range(half):
        at = 4 * layers + start + layer
        halo_alive[layer, 0:SLOT, :] = halos[-1][at] * has_right
        halo_alive[layer, SLOT:TILE, :] = halos[0][at] * has_left
    row_sums(design, sums, range(half + 4), wide)

    total_x = layers * lax.axis_size("gz")
    total_y = rows * lax.axis_size("gy")
    first_layer = lax.axis_index("gz") * layers + start
    first_row = lax.axis_index("gy") * rows
    parts = parts_of(depth)
    lane = lane_index()

    def depth_count(number, distance):
        held = filled((TILE, LANES), 2.0)
        if number == 0:
            held = jnp.where(lane < distance, 1.0, held)
        if number == len(parts) - 1:
            held = jnp.where(lane >= LANES - distance, held - 1.0, held)
        return held

    counts = [(depth_count(number, 1), depth_count(number, 2)) for number in range(len(parts))]

    def inside(at):
        return flag((at >= 0) & (at < total_x))

    for row in range(0, wide, TILE):
        column = row_index() + (first_row + row)
        if row == rows:
            column = jnp.where(row_index() >= SLOT, column - (rows + TILE), column)

        def within(offset):
            at = column + offset
            return jnp.where((at >= 0) & (at < total_y), 1.0, 0.0)

        y0, y1, y2 = within(0), within(-1) + within(1), within(-2) + within(2)
        for layer in range(half):
            filtered = cone_tile(design, sums, layer + 2, row)
            at = first_layer + layer
            x1 = inside(at - 1) + inside(at + 1)
            x2 = inside(at - 2) + inside(at + 2)
            level0, level1, level2 = depth_levels(
                y0, x1 * y0 + y1, x1 * y1, x2 * y0 + y2, x1 * y2 + x2 * y1
            )
            for part, value, (count1, count2) in zip(parts, filtered, counts):
                weight_sum = jnp.maximum(level0 + count1 * level1 + count2 * level2, 1.0)
                inverse = 1.0 / weight_sum
                physical = value * inverse
                value = (-3.0 * (1.0 - 0.001)) * physical * physical * inverse
                if row == rows:
                    alive = halo_alive[layer, :, part]
                else:
                    alive = free_of(void[start + layer, row : row + TILE, part])
                scaling[layer, row : row + TILE, part] = value * alive


def sensed_kernel(count, scaling, mine, received, last, ratio, crossing, straight, *refs):
    crossing_corners, straight_corners = refs[:count], refs[count : 2 * count]
    sensed, outgoing, nodes, modes = refs[2 * count :]
    half, wide, depth = scaling.shape
    rows = wide - TILE
    core = lax.axis_index("lc")
    for layer in range(half - 1):
        sensed[layer] = scaling[layer] * (mine[layer] + received[layer])

    @pl.when(core == 0)
    def _():
        sensed[half - 1] = scaling[half - 1] * (mine[half - 1] + received[half - 1])
        outgoing[...] = sensed[0:2]

    @pl.when(core == 1)
    def _():
        has_left, has_right = y_flags()
        scales = shares(ratio)
        cases = ((crossing, crossing_corners), (straight, straight_corners))
        for case, (above, corners) in enumerate(cases):
            for component in range(3):
                if case == 0:
                    nodes[component, 2 * case] = received[half + component]
                else:
                    nodes[component, 2 * case] = last[component]
                nodes[component, 2 * case + 1, 0:rows, :] = above[component]
                nodes[component, 2 * case + 1, rows : rows + SLOT, :] = corners[-1][component] * has_right
                nodes[component, 2 * case + 1, rows + SLOT : wide, :] = corners[0][component] * has_left
            for index in (2 * case, 2 * case + 1):
                row_modes(nodes, modes, index, index, wide)
        for row in range(0, wide, TILE):
            totals = None
            for case in range(2):
                lower, upper = (node_modes(modes, 2 * case + side, row) for side in (0, 1))
                energies = [element_energy(a, b, scales(case)) for a, b in zip(lower, upper)]
                totals = energies if totals is None else [a + b for a, b in zip(totals, energies)]
            for part, value in zip(parts_of(depth), totals):
                sensed[half - 1, row : row + TILE, part] = scaling[half - 1, row : row + TILE, part] * value
        outgoing[...] = sensed[half - 2 : half]


def inner_kernel(void, own, other, gradient, field, sums):
    layers, rows, depth = void.shape
    wide = rows + TILE
    half = layers // 2
    core = lax.axis_index("lc")
    field[pl.ds(core * half, half)] = own[...]
    field[pl.ds((1 - core) * half, half)] = other[...]
    row_sums(field, sums, range(layers), wide)
    for row in range(0, rows, TILE):
        for layer in range(2, layers - 2):
            filtered = cone_tile(field, sums, layer, row)
            for part, value in zip(parts_of(depth), filtered):
                alive = free_of(void[layer, row : row + TILE, part])
                gradient[layer - 2, row : row + TILE, part] = alive * value


def outer_kernel(void, own, other, own_beyond, other_beyond, inner, gradient, field, sums, low, high, sems):
    layers, rows, depth = void.shape
    wide = rows + TILE
    half = layers // 2
    core = lax.axis_index("lc")
    middle = pltpu.make_async_copy(inner, gradient.at[pl.ds(2, layers - 4)], sems.at[0])
    middle.start()
    field[pl.ds(2 + core * half, half)] = own[...]
    field[pl.ds(2 + (1 - core) * half, half)] = other[...]
    field[pl.ds(core * (layers + 2), 2)] = own_beyond[...]
    field[pl.ds((1 - core) * (layers + 2), 2)] = other_beyond[...]
    copies = [middle]
    for number, (result, base) in enumerate(((low, 0), (high, layers - 2))):
        row_sums(field, sums, range(base, base + 6), wide)
        for row in range(0, rows, TILE):
            for layer in range(2):
                filtered = cone_tile(field, sums, base + layer + 2, row)
                for part, value in zip(parts_of(depth), filtered):
                    alive = free_of(void[base + layer, row : row + TILE, part])
                    result[layer, row : row + TILE, part] = alive * value
        copy = pltpu.make_async_copy(result, gradient.at[pl.ds(base, 2)], sems.at[1 + number])
        copy.start()
        copies.append(copy)
    for copy in copies:
        copy.wait()


def vmem():
    return pl.BlockSpec(memory_space=pltpu.VMEM)


def hbm():
    return pl.BlockSpec(memory_space=pltpu.HBM)


def call(kernel, outs, scratch, in_specs, flops, out_specs=None, sems=0, limit=24 << 20):
    scratch = [pltpu.VMEM(shape, kind) for shape, kind in scratch]
    if sems:
        scratch.append(pltpu.SemaphoreType.DMA((sems,)))
    return pl.pallas_call(
        kernel,
        out_shape=[jax.ShapeDtypeStruct(shape, jnp.float32) for shape in outs],
        in_specs=in_specs,
        out_specs=out_specs or [vmem()] * len(outs),
        scratch_shapes=scratch,
        cost_estimate=pl.CostEstimate(flops=flops, bytes_accessed=1 << 20, transcendentals=0),
        compiler_params=pltpu.CompilerParams(vmem_limit_bytes=limit),
    )


def shards(density, void_mask, fixed_mask, displacement, load_ratio):
    layers, rows, depth = density.shape
    half = layers // 2
    wide = rows + TILE
    gz, gy, lc = (lax.axis_size(axis) for axis in ("gz", "gy", "lc"))
    real = jnp.float32
    smem = pl.BlockSpec(memory_space=pltpu.SMEM)
    swap = [(0, 1), (1, 0)]
    crossing, straight = [], []
    for z in range(1, gz):
        crossing.append((z * lc, (z - 1) * lc + 1))
        crossing.append(((z - 1) * lc + 1, z * lc))
        straight.append((z * lc + 1, (z - 1) * lc + 1))

    def y_pairs(step):
        if gy == 2:
            return [(y, 1 - y) for y in range(gy)]
        return [(y, y + step) for y in range(gy) if 0 <= y + step < gy]

    def diagonal(pairs, step):
        return [
            ((a // lc * gy + y) * lc + a % lc, (b // lc * gy + peer) * lc + b % lc)
            for a, b in pairs
            for y, peer in y_pairs(step)
        ]

    sides, steps = (["both"], [1]) if gy == 2 else (["first", "last"], [-1, 1])
    count = len(sides)

    crossing_out, straight_out = call(
        layer_kernel,
        [(5, rows, depth), (3, rows, depth)],
        [((3, rows, depth), real), ((rows, depth), jnp.int32)],
        [hbm()] * 3,
        1 << 18,
        sems=3,
        limit=VMEM_BYTES - 128 * rows * depth * 4,
    )(displacement, fixed_mask, density)
    crossed = lax.ppermute(crossing_out, ("gz", "lc"), crossing)
    straightened = lax.ppermute(straight_out, ("gz", "lc"), straight)
    density, void_mask, fixed_mask, displacement, crossing_out = lax.optimization_barrier(
        (density, void_mask, fixed_mask, displacement, crossing_out)
    )
    edges = call(
        functools.partial(edge_kernel, sides),
        [(5 * layers, SLOT, depth), (5, SLOT, depth), (3, SLOT, depth)] * count,
        [],
        [vmem()] * 4,
        1 << 20,
    )(displacement, fixed_mask, density, void_mask)
    halos = [lax.ppermute(a, "gy", y_pairs(step)) for a, step in zip(edges[0::3], steps)][::-1]
    axes = ("gz", "gy", "lc")
    crossed_corners = [lax.ppermute(a, axes, diagonal(crossing, step)) for a, step in zip(edges[1::3], steps)][::-1]
    straight_corners = [lax.ppermute(a, axes, diagonal(straight, step)) for a, step in zip(edges[2::3], steps)][::-1]

    mine, theirs, last = call(
        functools.partial(energy_kernel, count),
        [(half, wide, depth), (half + 3, wide, depth), (3, wide, depth)],
        [((3, layers, wide, depth), real), ((layers, 6, wide, depth), real), ((layers, wide, depth), real)],
        [vmem(), vmem(), smem] + [vmem()] * count,
        1 << 24,
    )(displacement, fixed_mask, load_ratio, *halos)
    received = lax.ppermute(theirs, "lc", swap)
    (scaling,) = call(
        functools.partial(scaling_kernel, count),
        [(half, wide, depth)],
        [((half + 4, wide, depth), real), ((half + 4, 2, wide, depth), real), ((half, TILE, depth), real)],
        [vmem()] * (3 + 2 * count),
        1 << 22,
    )(density, void_mask, crossed, *halos, *crossed_corners)
    sensed, outgoing = call(
        functools.partial(sensed_kernel, count),
        [(half, wide, depth), (2, wide, depth)],
        [((3, 4, wide, depth), real), ((4, 6, wide, depth), real)],
        [vmem()] * 4 + [smem] + [vmem()] * (2 + 2 * count),
        1 << 22,
    )(scaling, mine, received, last, load_ratio, crossed, straightened, *crossed_corners, *straight_corners)
    own_beyond = lax.ppermute(outgoing, ("gz", "lc"), crossing)
    other = lax.ppermute(sensed, "lc", swap)
    (inner,) = call(
        inner_kernel,
        [(layers - 4, rows, depth)],
        [((layers, wide, depth), real), ((layers, 2, wide, depth), real)],
        [vmem()] * 3,
        1 << 22,
    )(void_mask, sensed, other)
    other_beyond = lax.ppermute(own_beyond, "lc", swap)
    (gradient,) = call(
        outer_kernel,
        [(layers, rows, depth)],
        [
            ((layers + 4, wide, depth), real),
            ((layers + 4, 2, wide, depth), real),
            ((2, rows, depth), real),
            ((2, rows, depth), real),
        ],
        [vmem()] * 6,
        1 << 22,
        out_specs=[hbm()],
        sems=3,
    )(void_mask, sensed, other, own_beyond, other_beyond, inner)
    return gradient


def solution(mesh):
    placed = (
        P(("parts", "gz"), "gy", None),
        P(("parts", "gz"), "gy", None),
        P(("parts", "gz"), "gy", None),
        P("lc", None, ("parts", "gz"), "gy", None),
        P("parts"),
    )
    return jax.shard_map(
        shards,
        mesh=mesh,
        in_specs=placed,
        out_specs=P(("parts", "gz"), "gy", None),
        check_vma=False,
    )
```

time: 41.5 us -> 37.3 us (0.90)
  waiting for transfers between devices: 6.52 us -> 4.57 us
  local copies, waits for them, and re-layouts: 2.46 us -> 1.06 us
  Pallas kernels: 9.49 us -> 8.56 us
    unnamed x10 -> x14, local copies, waits for them, and re-layouts: 2.46 us -> 1.06 us
    ppermute x6, starting transfers between devices: 7.74 us -> 6.37 us  [the longest x1 3.04 us: shards(): lax.ppermute(a, 'gy', y_pairs(step))]
    ppermute x6, waiting for transfers between devices: 5.49 us -> 4.21 us  [the longest x1 4.2 us: shards(): lax.ppermute(a, 'gy', y_pairs(step))]
    ppermute x1, starting transfers between devices: 4.64 us -> 5.8 us  [shards(): other_beyond = lax.ppermute(own_beyond, 'lc', swap)]
    pallas_call x6 -> x7, Pallas kernels: 9.49 us -> 8.56 us  [the longest x1 2.82 us: shards(): call(functools.partial(energy_kernel, count), [(half, wide, depth), (half...]
    ppermute x1, waiting for transfers between devices: 1.03 us -> 0.36 us  [shards(): other_beyond = lax.ppermute(own_beyond, 'lc', swap)]
where the time goes in v2:
time: 37.3 us; the launch traced here: 37 us
  starting transfers between devices  22.6 us (61%)
  Pallas kernels  8.56 us (23%)
  waiting for transfers between devices  4.57 us (12%)
  local copies, waits for them, and re-layouts  1.06 us (3%)
    ppermute x1, starting transfers between devices, shards(): other = lax.ppermute(sensed, 'lc', swap)  10.3 us
    ppermute x1, starting transfers between devices, shards(): other_beyond = lax.ppermute(own_beyond, 'lc', swap)  5.8 us
    ppermute x1, waiting for transfers between devices, shards(): lax.ppermute(a, 'gy', y_pairs(step))  4.2 us
    ppermute x1, starting transfers between devices, shards(): lax.ppermute(a, 'gy', y_pairs(step))  3.04 us
    pallas_call x1, Pallas kernels, shards(): call(functools.partial(energy_kernel, count), [(half, wide, depth), (half...  2.82 us
    pallas_call x1, Pallas kernels, shards(): call(layer_kernel, [(5, rows, depth), (3, rows, depth)], [((3, rows, dept...  2.01 us
    pallas_call x1, Pallas kernels, shards(): call(outer_kernel, [(layers, rows, depth)], [((layers + 4, wide, depth),...  1.44 us
    unnamed x14, local copies, waits for them, and re-layouts  1.06 us
  transfers between devices with their start and end apart: 9, of which 2 were waited for; matrix products, arithmetic and copies ran while one was open for 0% of the time, Pallas kernels for 4%

profile of v2, /device:TPU:0, one launch (start us, length us, event | category | flops | bytes accessed | tf_op | source)
XLA Modules:
  0.0 37.0 jit_solution(17111629674844199080)
XLA Ops:
  0.0 2.0 %shard_map.55 = (f32[5,64,256]{2,1,0:T(8,128)}, f32[3,64,256]{2,1,0:T(8,128)}) custom-call(f32[1,3,8,64,256]{4,3,2,1,0:T(8,128)} %displacement.3, s32[8,64,256]{2,1,0:T(8,128)} %fixed.3, f32[8,64,256]{2,1,0:T(8,128)} %density.3), custom_call_target="tpu_custom_call" | custom-call | flops 262144 | bytes 1048576 | tf_op jit(solution)/shard_map/pallas_call | solution.py:501
  2.1 0.0 copy-start.3
  2.1 1.0 %copy-done.3 = f32[8,64,256]{2,1,0:T(8,128)S(1)} copy-done((f32[8,64,256]{2,1,0:T(8,128)S(1)}, f32[8,64,256]{2,1,0:T(8,128)}, u32[]{:S(2)}) %copy-start.3) | copy-done | bytes 524312
  3.1 0.1 shard_map.56
  3.2 0.0 copy-start.5
  3.2 3.0 %collective-permute-start.1 = (f32[40,4,256]{2,1,0:T(4,128)S(1)}, f32[40,4,256]{2,1,0:T(4,128)S(1)}, u32[]{:S(2)}, u32[]{:S(2)}) collective-permute-start(f32[40,4,256]{2,1,0:T(4,128)S(1)} %get-tuple-element.24), channel_id=1, source_target_pairs={{0,2},{2,0},{1,3},{3,1},{4,6},{6,4},{5,7},{7,5},{8,10},{10,8},{9,1... | collective-permute-start | bytes 491528 | tf_op jit(solution)/shard_map/ppermute | solution.py:522
  6.2 4.2 %collective-permute-done.1.refs_0_ = f32[40,4,256]{2,1,0:T(4,128)S(1)} collective-permute-done((f32[40,4,256]{2,1,0:T(4,128)S(1)}, f32[40,4,256]{2,1,0:T(4,128)S(1)}, u32[]{:S(2)}, u32[]{:S(2)}) %collective-permute-start.1) | collective-permute-done | bytes 163872 | tf_op jit(solution)/shard_map/ppermute | solution.py:522
  10.4 2.8 %shard_map.58 = (f32[4,72,256]{2,1,0:T(8,128)S(1)}, f32[7,72,256]{2,1,0:T(8,128)S(1)}, f32[3,72,256]{2,1,0:T(8,128)S(1)}) custom-call(f32[1,3,8,64,256]{4,3,2,1,0:T(8,128)S(1)} %copy-done, s32[8,64,256]{2,1,0:T(8,128)S(1)} %copy-done.2, s32[2]{0:T(128)S(1)} %copy-done.4, f32[40,4,256]{2,1,0:T(4,128)S(1)} %collective-permute-done.1.refs_0_), custom_call_target="tpu_custom_call" | custom-call | flops 16777216 | bytes 1048576 | tf_op jit(solution)/shard_map/pallas_call | solution.py:527
  13.3 0.1 collective-permute-start.3
  13.3 0.7 %collective-permute-start = (f32[5,64,256]{2,1,0:T(8,128)S(1)}, f32[5,64,256]{2,1,0:T(8,128)S(1)}, u32[]{:S(2)}, u32[]{:S(2)}) collective-permute-start(f32[5,64,256]{2,1,0:T(8,128)S(1)} %copy-done.5), channel_id=1, source_target_pairs={{4,1},{1,4},{8,5},{5,8},{12,9},{9,12},{6,3},{3,6},{10,7},{7,10},{1... | collective-permute-start | bytes 983048 | tf_op jit(solution)/shard_map/ppermute | solution.py:510
  14.0 0.7 %collective-permute-start.4 = (f32[3,64,256]{2,1,0:T(8,128)S(1)}, f32[3,64,256]{2,1,0:T(8,128)S(1)}, u32[]{:S(2)}, u32[]{:S(2)}) collective-permute-start(f32[3,64,256]{2,1,0:T(8,128)S(1)} %copy-done.6), channel_id=1, source_target_pairs={{5,1},{9,5},{13,9},{7,3},{11,7},{15,11},{21,17},{25,21},{29,25},{2... | collective-permute-start | bytes 589832 | tf_op jit(solution)/shard_map/ppermute | solution.py:511
  14.7 0.7 %collective-permute-start.2 = (f32[5,4,256]{2,1,0:T(4,128)S(1)}, f32[5,4,256]{2,1,0:T(4,128)S(1)}, u32[]{:S(2)}, u32[]{:S(2)}) collective-permute-start(f32[5,4,256]{2,1,0:T(4,128)S(1)} %get-tuple-element.25), channel_id=1, source_target_pairs={{4,3},{6,1},{1,6},{3,4},{8,7},{10,5},{5,10},{7,8},{12,11},{14,9},{... | collective-permute-start | bytes 61448 | tf_op jit(solution)/shard_map/ppermute | solution.py:524
  15.4 0.7 %collective-permute-start.5 = (f32[3,4,256]{2,1,0:T(4,128)S(1)}, f32[3,4,256]{2,1,0:T(4,128)S(1)}, u32[]{:S(2)}, u32[]{:S(2)}) collective-permute-start(f32[3,4,256]{2,1,0:T(4,128)S(1)} %get-tuple-element.30), channel_id=1, source_target_pairs={{5,3},{7,1},{9,7},{11,5},{13,11},{15,9},{21,19},{23,17},{25,23},{2... | collective-permute-start | bytes 36872 | tf_op jit(solution)/shard_map/ppermute | solution.py:525
  16.1 0.0 collective-permute-done.2.refs_1_.refs_0_
  16.1 1.0 %shard_map.57.scaling = f32[4,72,256]{2,1,0:T(8,128)S(1)} custom-call(f32[8,64,256]{2,1,0:T(8,128)S(1)} %copy-done.3, s32[8,64,256]{2,1,0:T(8,128)S(1)} %copy-done.1, f32[5,64,256]{2,1,0:T(8,128)S(1)} %collective-permute-done.beyond.crossing, f32[40,4,256]{2,1,0:T(4,128)S(1)} %collective-permute-done.1.refs_0_, ...), custom_call_target="tpu_custom_call" | custom-call | flops 4194304 | bytes 1048576 | tf_op jit(solution)/shard_map/pallas_call | solution.py:535
  17.1 0.0 collective-permute-done.5.refs_1_
  17.1 0.0 collective-permute-done.4.straight
  17.1 0.6 %shard_map.59 = (f32[4,72,256]{2,1,0:T(8,128)S(1)}, f32[2,72,256]{2,1,0:T(8,128)S(1)}) custom-call(f32[4,72,256]{2,1,0:T(8,128)S(1)} %shard_map.57.scaling, f32[4,72,256]{2,1,0:T(8,128)S(1)} %get-tuple-element.26.mine, f32[7,72,256]{2,1,0:T(8,128)S(1)} %collective-permute-done.3.received, f32[3,72,256]{2,1,0:T(8,128)S(1)} %get-tuple-element.28.last, ...), custom_call_target="tpu_custom_call" | custom-call | flops 4194304 | bytes 1048576 | tf_op jit(solution)/shard_map/pallas_call | solution.py:542
  17.7 10.3 %collective-permute-start.6 = (f32[4,72,256]{2,1,0:T(8,128)S(1)}, f32[4,72,256]{2,1,0:T(8,128)S(1)}, u32[]{:S(2)}, u32[]{:S(2)}) collective-permute-start(f32[4,72,256]{2,1,0:T(8,128)S(1)} %get-tuple-element.31.own), channel_id=1, source_target_pairs={{0,1},{1,0},{2,3},{3,2},{4,5},{5,4},{6,7},{7,6},{8,9},{9,8},{10,11... | collective-permute-start | bytes 884744 | tf_op jit(solution)/shard_map/ppermute | solution.py:550
  28.1 0.7 %collective-permute-start.7 = (f32[2,72,256]{2,1,0:T(8,128)S(1)}, f32[2,72,256]{2,1,0:T(8,128)S(1)}, u32[]{:S(2)}, u32[]{:S(2)}) collective-permute-start(f32[2,72,256]{2,1,0:T(8,128)S(1)} %get-tuple-element.32), channel_id=1, source_target_pairs={{4,1},{1,4},{8,5},{5,8},{12,9},{9,12},{6,3},{3,6},{10,7},{7,10},{1... | collective-permute-start | bytes 442376 | tf_op jit(solution)/shard_map/ppermute | solution.py:549
  28.7 5.8 %collective-permute-start.8 = (f32[2,72,256]{2,1,0:T(8,128)S(1)}, f32[2,72,256]{2,1,0:T(8,128)S(1)}, u32[]{:S(2)}, u32[]{:S(2)}) collective-permute-start(f32[2,72,256]{2,1,0:T(8,128)S(1)} %collective-permute-done.7.own_beyond), channel_id=1, source_target_pairs={{0,1},{1,0},{2,3},{3,2},{4,5},{5,4},{6,7},{7,6},{8,9},{9,8},{10,11... | collective-permute-start | bytes 442376 | tf_op jit(solution)/shard_map/ppermute | solution.py:558
  34.5 0.6 %shard_map.60.inner = f32[4,64,256]{2,1,0:T(8,128)S(1)} custom-call(s32[8,64,256]{2,1,0:T(8,128)S(1)} %copy-done.1, f32[4,72,256]{2,1,0:T(8,128)S(1)} %get-tuple-element.31.own, f32[4,72,256]{2,1,0:T(8,128)S(1)} %collective-permute-done.6.other), custom_call_target="tpu_custom_call" | custom-call | flops 4194304 | bytes 1048576 | tf_op jit(solution)/shard_map/pallas_call | solution.py:551
  35.2 0.4 collective-permute-done.8.other_beyond
  35.5 1.4 %shard_map.61 = f32[8,64,256]{2,1,0:T(8,128)} custom-call(s32[8,64,256]{2,1,0:T(8,128)S(1)} %copy-done.1, f32[4,72,256]{2,1,0:T(8,128)S(1)} %get-tuple-element.31.own, f32[4,72,256]{2,1,0:T(8,128)S(1)} %collective-permute-done.6.other, f32[2,72,256]{2,1,0:T(8,128)S(1)} %collective-permute-done.7.own_beyond, ...), custom_call_target="tpu_custom_call" | custom-call | flops 4194304 | bytes 1048576 | tf_op jit(solution)/shard_map/pallas_call | solution.py:559
  (15 shorter events, 0.0 us)
Async XLA Ops:
  0.0 2.0 %copy-start = (f32[1,3,8,64,256]{4,3,2,1,0:T(8,128)S(1)}, f32[1,3,8,64,256]{4,3,2,1,0:T(8,128)}, u32[]{:S(2)}) copy-start(f32[1,3,8,64,256]{4,3,2,1,0:T(8,128)} %displacement.3) | copy-start | bytes 4718596
  0.0 2.0 %copy-start.2 = (s32[8,64,256]{2,1,0:T(8,128)S(1)}, s32[8,64,256]{2,1,0:T(8,128)}, u32[]{:S(2)}) copy-start(s32[8,64,256]{2,1,0:T(8,128)} %fixed.3) | copy-start | bytes 1572868
  0.0 2.0 %copy-start.1 = (s32[8,64,256]{2,1,0:T(8,128)S(1)}, s32[8,64,256]{2,1,0:T(8,128)}, u32[]{:S(2)}) copy-start(s32[8,64,256]{2,1,0:T(8,128)} %void.3) | copy-start | bytes 1572868
  2.1 1.0 %copy-start.3 = (f32[8,64,256]{2,1,0:T(8,128)S(1)}, f32[8,64,256]{2,1,0:T(8,128)}, u32[]{:S(2)}) copy-start(f32[8,64,256]{2,1,0:T(8,128)} %density.3) | copy-start | bytes 1572868
  3.1 7.3 %copy-start.4 = (s32[2]{0:T(128)S(1)}, s32[2]{0:T(128)}, u32[]{:S(2)}) copy-start(s32[2]{0:T(128)} %ratio.3) | copy-start | bytes 28
  3.2 10.2 %copy-start.5 = (f32[5,64,256]{2,1,0:T(8,128)S(1)}, f32[5,64,256]{2,1,0:T(8,128)}, u32[]{:S(2)}) copy-start(f32[5,64,256]{2,1,0:T(8,128)} %get-tuple-element.19) | copy-start | bytes 983044
  3.2 10.9 %copy-start.6 = (f32[3,64,256]{2,1,0:T(8,128)S(1)}, f32[3,64,256]{2,1,0:T(8,128)}, u32[]{:S(2)}) copy-start(f32[3,64,256]{2,1,0:T(8,128)} %get-tuple-element.29) | copy-start | bytes 589828
  3.2 7.2 %collective-permute-start.1 = (f32[40,4,256]{2,1,0:T(4,128)S(1)}, f32[40,4,256]{2,1,0:T(4,128)S(1)}, u32[]{:S(2)}, u32[]{:S(2)}) collective-permute-start(f32[40,4,256]{2,1,0:T(4,128)S(1)} %get-tuple-element.24), channel_id=1, source_target_pairs={{0,2},{2,0},{1,3},{3,1},{4,6},{6,4},{5,7},{7,5},{8,10},{10,8},{9,1... | collective-permute-start | bytes 491528 | tf_op jit(solution)/shard_map/ppermute | solution.py:522
  13.3 3.8 %collective-permute-start.3 = (f32[7,72,256]{2,1,0:T(8,128)S(1)}, f32[7,72,256]{2,1,0:T(8,128)S(1)}, u32[]{:S(2)}, u32[]{:S(2)}) collective-permute-start(f32[7,72,256]{2,1,0:T(8,128)S(1)} %get-tuple-element.27), channel_id=1, source_target_pairs={{0,1},{1,0},{2,3},{3,2},{4,5},{5,4},{6,7},{7,6},{8,9},{9,8},{10,11... | collective-permute-start | bytes 1548296 | tf_op jit(solution)/shard_map/ppermute | solution.py:534
  13.3 2.7 %collective-permute-start = (f32[5,64,256]{2,1,0:T(8,128)S(1)}, f32[5,64,256]{2,1,0:T(8,128)S(1)}, u32[]{:S(2)}, u32[]{:S(2)}) collective-permute-start(f32[5,64,256]{2,1,0:T(8,128)S(1)} %copy-done.5), channel_id=1, source_target_pairs={{4,1},{1,4},{8,5},{5,8},{12,9},{9,12},{6,3},{3,6},{10,7},{7,10},{1... | collective-permute-start | bytes 983048 | tf_op jit(solution)/shard_map/ppermute | solution.py:510
  14.0 3.0 %collective-permute-start.4 = (f32[3,64,256]{2,1,0:T(8,128)S(1)}, f32[3,64,256]{2,1,0:T(8,128)S(1)}, u32[]{:S(2)}, u32[]{:S(2)}) collective-permute-start(f32[3,64,256]{2,1,0:T(8,128)S(1)} %copy-done.6), channel_id=1, source_target_pairs={{5,1},{9,5},{13,9},{7,3},{11,7},{15,11},{21,17},{25,21},{29,25},{2... | collective-permute-start | bytes 589832 | tf_op jit(solution)/shard_map/ppermute | solution.py:511
  14.7 1.3 %collective-permute-start.2 = (f32[5,4,256]{2,1,0:T(4,128)S(1)}, f32[5,4,256]{2,1,0:T(4,128)S(1)}, u32[]{:S(2)}, u32[]{:S(2)}) collective-permute-start(f32[5,4,256]{2,1,0:T(4,128)S(1)} %get-tuple-element.25), channel_id=1, source_target_pairs={{4,3},{6,1},{1,6},{3,4},{8,7},{10,5},{5,10},{7,8},{12,11},{14,9},{... | collective-permute-start | bytes 61448 | tf_op jit(solution)/shard_map/ppermute | solution.py:524
  15.4 1.7 %collective-permute-start.5 = (f32[3,4,256]{2,1,0:T(4,128)S(1)}, f32[3,4,256]{2,1,0:T(4,128)S(1)}, u32[]{:S(2)}, u32[]{:S(2)}) collective-permute-start(f32[3,4,256]{2,1,0:T(4,128)S(1)} %get-tuple-element.30), channel_id=1, source_target_pairs={{5,3},{7,1},{9,7},{11,5},{13,11},{15,9},{21,19},{23,17},{25,23},{2... | collective-permute-start | bytes 36872 | tf_op jit(solution)/shard_map/ppermute | solution.py:525
  17.7 16.8 %collective-permute-start.6 = (f32[4,72,256]{2,1,0:T(8,128)S(1)}, f32[4,72,256]{2,1,0:T(8,128)S(1)}, u32[]{:S(2)}, u32[]{:S(2)}) collective-permute-start(f32[4,72,256]{2,1,0:T(8,128)S(1)} %get-tuple-element.31.own), channel_id=1, source_target_pairs={{0,1},{1,0},{2,3},{3,2},{4,5},{5,4},{6,7},{7,6},{8,9},{9,8},{10,11... | collective-permute-start | bytes 884744 | tf_op jit(solution)/shard_map/ppermute | solution.py:550
  28.1 0.7 %collective-permute-start.7 = (f32[2,72,256]{2,1,0:T(8,128)S(1)}, f32[2,72,256]{2,1,0:T(8,128)S(1)}, u32[]{:S(2)}, u32[]{:S(2)}) collective-permute-start(f32[2,72,256]{2,1,0:T(8,128)S(1)} %get-tuple-element.32), channel_id=1, source_target_pairs={{4,1},{1,4},{8,5},{5,8},{12,9},{9,12},{6,3},{3,6},{10,7},{7,10},{1... | collective-permute-start | bytes 442376 | tf_op jit(solution)/shard_map/ppermute | solution.py:549
  28.7 6.8 %collective-permute-start.8 = (f32[2,72,256]{2,1,0:T(8,128)S(1)}, f32[2,72,256]{2,1,0:T(8,128)S(1)}, u32[]{:S(2)}, u32[]{:S(2)}) collective-permute-start(f32[2,72,256]{2,1,0:T(8,128)S(1)} %collective-permute-done.7.own_beyond), channel_id=1, source_target_pairs={{0,1},{1,0},{2,3},{3,2},{4,5},{5,4},{6,7},{7,6},{8,9},{9,8},{10,11... | collective-permute-start | bytes 442376 | tf_op jit(solution)/shard_map/ppermute | solution.py:558

commit v3 on v2

--- a/solution.py
+++ b/solution.py
@@ -11,7 +11,7 @@
 TILE = 8
 SLOT = 4
 LANES = 128
-VMEM_BYTES = 67043328
+PREPARE_LIMIT = 53 << 20
 WEIGHT = [2.5 - math.sqrt(squared) for squared in range(7)]
 
 
@@ -186,64 +186,81 @@
     return (1 - mask).astype(jnp.float32)
 
 
-def edge_rows(first, last, side):
-    if side == "first":
-        return first[0:SLOT]
-    moved_up = pltpu.roll(last, SLOT, 0)
-    if side == "last":
-        return moved_up[0:SLOT]
-    return jnp.where(lax.axis_index("gy") == 0, moved_up, first)[0:SLOT]
-
-
-def layer_kernel(displacement, fixed, density, crossing, straight, nodes, mask, sems):
-    layers = density.shape[0]
+def prepare_kernel(sides, displacement, fixed, density, void, *refs):
+    count = len(sides)
+    moved, design = refs[:2]
+    packs = refs[2 : 2 + count]
+    nodes, mask, node_edge, mask_edge, design_edge, void_edge, sems = refs[2 + count :]
+    layers, rows, depth = density.shape
     core = lax.axis_index("lc")
     copies = [
         pltpu.make_async_copy(displacement.at[0, :, 0], nodes, sems.at[0]),
         pltpu.make_async_copy(fixed.at[0], mask, sems.at[1]),
         pltpu.make_async_copy(
-            density.at[pl.ds(core * (layers - 2), 2)], crossing.at[pl.ds(3, 2)], sems.at[2]
+            density.at[pl.ds(core * (layers - 2), 2)], design.at[:, pl.ds(0, rows)], sems.at[2]
         ),
     ]
+    for number, side in enumerate(sides):
+        if side == "both":
+            start = pl.multiple_of((1 - lax.axis_index("gy")) * (rows - TILE), TILE)
+        else:
+            start = 0 if side == "first" else rows - TILE
+        at = pl.ds(start, TILE)
+        base = 3 + 4 * number
+        copies += [
+            pltpu.make_async_copy(displacement.at[0, :, :, at], node_edge.at[number], sems.at[base]),
+            pltpu.make_async_copy(fixed.at[:, at], mask_edge.at[number], sems.at[base + 1]),
+            pltpu.make_async_copy(density.at[:, at], design_edge.at[number], sems.at[base + 2]),
+            pltpu.make_async_copy(void.at[:, at], void_edge.at[number], sems.at[base + 3]),
+        ]
     for copy in copies:
         copy.start()
     for copy in copies:
         copy.wait()
     free = free_of(mask[...])
+    front = lax.broadcasted_iota(jnp.int32, (TILE, depth), 0) < SLOT
     for component in range(3):
-        moved = nodes[component] * free
-        crossing[component] = moved
-        straight[component] = moved
-
-
-def edge_kernel(sides, displacement, fixed, density, void, *outs):
-    layers, rows, _ = density.shape
-    core = lax.axis_index("lc")
-    first, last = slice(0, TILE), slice(rows - TILE, rows)
-    for number, side in enumerate(sides):
-        packed, crossing, straight = outs[3 * number : 3 * number + 3]
-        low, high = [], []
+        value = nodes[component] * free
+        moved[component, 0:rows, :] = value
+        moved[component, rows : rows + TILE, :] = jnp.where(front, value[:TILE], value[rows - TILE :])
+    for layer in range(2):
+        first, last = design[layer, 0:TILE, :], design[layer, rows - TILE : rows, :]
+        design[layer, rows : rows + TILE, :] = jnp.where(front, first, last)
+
+    for number, (side, packed) in enumerate(zip(sides, packs)):
+        if side == "both":
+            from_last = lax.axis_index("gy") == 0
+        else:
+            from_last = side == "last"
+
+        def edge(tile):
+            if side == "first":
+                return tile[0:SLOT]
+            turned = pltpu.roll(tile, SLOT, 0)
+            if side == "last":
+                return turned[0:SLOT]
+            return jnp.where(from_last, turned, tile)[0:SLOT]
+
         for layer in range(layers):
-            free = edge_rows(free_of(fixed[layer, first]), free_of(fixed[layer, last]), side)
+            free = free_of(mask_edge[number, layer])
             for component in range(3):
-                moved = free * edge_rows(
-                    displacement[0, component, layer, first], displacement[0, component, layer, last], side
-                )
-                packed[component * layers + layer] = moved
-                if layer == 0:
-                    crossing[component] = moved
-                    straight[component] = moved
-            design = edge_rows(density[layer, first], density[layer, last], side)
-            packed[3 * layers + layer] = design
-            if layer < 2:
-                low.append(design)
-            if layer >= layers - 2:
-                high.append(design)
-            packed[4 * layers + layer] = edge_rows(
-                free_of(void[layer, first]), free_of(void[layer, last]), side
-            )
-        for index in range(2):
-            crossing[3 + index] = jnp.where(core == 0, low[index], high[index])
+                packed[component * layers + layer] = edge(free * node_edge[number, component, layer])
+            packed[3 * layers + layer] = edge(design_edge[number, layer])
+            packed[4 * layers + layer] = edge(free_of(void_edge[number, layer]))
+
+
+def pack_kernel(sides, moved, partner, design, crossing, *corners):
+    rows = crossing.shape[1]
+    for source, base in ((moved, 0), (partner, 3), (design, 6)):
+        for index in range(source.shape[0]):
+            crossing[base + index] = source[index, 0:rows, :]
+            for side, corner in zip(sides, corners):
+                first = source[index, rows : rows + SLOT, :]
+                last = source[index, rows + SLOT : rows + TILE, :]
+                if side == "both":
+                    corner[base + index] = jnp.where(lax.axis_index("gy") == 0, last, first)
+                else:
+                    corner[base + index] = first if side == "first" else last
 
 
 def energy_kernel(count, displacement, fixed, ratio, *refs):
@@ -305,7 +322,7 @@
         at = 3 * layers + source
         place(index + 2 * (1 - core), density[source], halos[0][at], halos[-1][at])
     for index in range(2):
-        place(core * (half + 2) + index, beyond[3 + index], corners[0][3 + index], corners[-1][3 + index])
+        place(core * (half + 2) + index, beyond[6 + index], corners[0][6 + index], corners[-1][6 + index])
     for layer in range(half):
         at = 4 * layers + start + layer
         halo_alive[layer, 0:SLOT, :] = halos[-1][at] * has_right
@@ -362,9 +379,9 @@
                 scaling[layer, row : row + TILE, part] = value * alive
 
 
-def sensed_kernel(count, scaling, mine, received, last, ratio, crossing, straight, *refs):
-    crossing_corners, straight_corners = refs[:count], refs[count : 2 * count]
-    sensed, outgoing, nodes, modes = refs[2 * count :]
+def sensed_kernel(count, scaling, mine, received, last, ratio, above, *refs):
+    corners = refs[:count]
+    sensed, outgoing, nodes, modes = refs[count:]
     half, wide, depth = scaling.shape
     rows = wide - TILE
     core = lax.axis_index("lc")
@@ -380,16 +397,16 @@
     def _():
         has_left, has_right = y_flags()
         scales = shares(ratio)
-        cases = ((crossing, crossing_corners), (straight, straight_corners))
-        for case, (above, corners) in enumerate(cases):
+        for case in range(2):
             for component in range(3):
+                at = 3 * case + component
                 if case == 0:
                     nodes[component, 2 * case] = received[half + component]
                 else:
                     nodes[component, 2 * case] = last[component]
-                nodes[component, 2 * case + 1, 0:rows, :] = above[component]
-                nodes[component, 2 * case + 1, rows : rows + SLOT, :] = corners[-1][component] * has_right
-                nodes[component, 2 * case + 1, rows + SLOT : wide, :] = corners[0][component] * has_left
+                nodes[component, 2 * case + 1, 0:rows, :] = above[at]
+                nodes[component, 2 * case + 1, rows : rows + SLOT, :] = corners[-1][at] * has_right
+                nodes[component, 2 * case + 1, rows + SLOT : wide, :] = corners[0][at] * has_left
             for index in (2 * case, 2 * case + 1):
                 row_modes(nodes, modes, index, index, wide)
         for row in range(0, wide, TILE):
@@ -419,29 +436,37 @@
                 gradient[layer - 2, row : row + TILE, part] = alive * value
 
 
-def outer_kernel(void, own, other, own_beyond, other_beyond, inner, gradient, field, sums, low, high, sems):
+def side_rows(side, void, own, beyond, result, field, sums):
     layers, rows, depth = void.shape
-    wide = rows + TILE
-    half = layers // 2
+    half = own.shape[0]
+    field[pl.ds(side * 4, 2)] = beyond[...]
+    field[pl.ds(2 - 2 * side, 4)] = own[pl.ds(side * (half - 4), 4)]
+    row_sums(field, sums, range(6), rows + TILE)
+    base = side * (layers - 2)
+    for row in range(0, rows, TILE):
+        for layer in range(2):
+            filtered = cone_tile(field, sums, layer + 2, row)
+            for part, value in zip(parts_of(depth), filtered):
+                alive = free_of(void[base + layer, row : row + TILE, part])
+                result[layer, row : row + TILE, part] = alive * value
+
+
+def near_kernel(void, own, beyond, result, field, sums):
+    side_rows(lax.axis_index("lc"), void, own, beyond, result, field, sums)
+
+
+def far_kernel(void, other, beyond, inner, near, gradient, field, sums, far, sems):
+    layers = void.shape[0]
     core = lax.axis_index("lc")
-    middle = pltpu.make_async_copy(inner, gradient.at[pl.ds(2, layers - 4)], sems.at[0])
-    middle.start()
-    field[pl.ds(2 + core * half, half)] = own[...]
-    field[pl.ds(2 + (1 - core) * half, half)] = other[...]
-    field[pl.ds(core * (layers + 2), 2)] = own_beyond[...]
-    field[pl.ds((1 - core) * (layers + 2), 2)] = other_beyond[...]
-    copies = [middle]
-    for number, (result, base) in enumerate(((low, 0), (high, layers - 2))):
-        row_sums(field, sums, range(base, base + 6), wide)
-        for row in range(0, rows, TILE):
-            for layer in range(2):
-                filtered = cone_tile(field, sums, base + layer + 2, row)
-                for part, value in zip(parts_of(depth), filtered):
-                    alive = free_of(void[base + layer, row : row + TILE, part])
-                    result[layer, row : row + TILE, part] = alive * value
-        copy = pltpu.make_async_copy(result, gradient.at[pl.ds(base, 2)], sems.at[1 + number])
+    copies = [
+        pltpu.make_async_copy(inner, gradient.at[pl.ds(2, layers - 4)], sems.at[0]),
+        pltpu.make_async_copy(near, gradient.at[pl.ds(core * (layers - 2), 2)], sems.at[1]),
+        pltpu.make_async_copy(far, gradient.at[pl.ds((1 - core) * (layers - 2), 2)], sems.at[2]),
+    ]
+    for copy in copies[:2]:
         copy.start()
-        copies.append(copy)
+    side_rows(1 - core, void, other, beyond, far, field, sums)
+    copies[2].start()
     for copy in copies:
         copy.wait()
 
@@ -477,11 +502,10 @@
     real = jnp.float32
     smem = pl.BlockSpec(memory_space=pltpu.SMEM)
     swap = [(0, 1), (1, 0)]
-    crossing, straight = [], []
+    crossing = []
     for z in range(1, gz):
         crossing.append((z * lc, (z - 1) * lc + 1))
         crossing.append(((z - 1) * lc + 1, z * lc))
-        straight.append((z * lc + 1, (z - 1) * lc + 1))
 
     def y_pairs(step):
         if gy == 2:
@@ -498,31 +522,37 @@
     sides, steps = (["both"], [1]) if gy == 2 else (["first", "last"], [-1, 1])
     count = len(sides)
 
-    crossing_out, straight_out = call(
-        layer_kernel,
-        [(5, rows, depth), (3, rows, depth)],
-        [((3, rows, depth), real), ((rows, depth), jnp.int32)],
-        [hbm()] * 3,
+    kinds = [
+        ((3, rows, depth), real),
+        ((rows, depth), jnp.int32),
+        ((count, 3, layers, TILE, depth), real),
+        ((count, layers, TILE, depth), jnp.int32),
+        ((count, layers, TILE, depth), real),
+        ((count, layers, TILE, depth), jnp.int32),
+    ]
+    moved, design, *packs = call(
+        functools.partial(prepare_kernel, sides),
+        [(3, wide, depth), (2, wide, depth)] + [(5 * layers, SLOT, depth)] * count,
+        kinds,
+        [hbm()] * 4,
         1 << 18,
-        sems=3,
-        limit=VMEM_BYTES - 128 * rows * depth * 4,
-    )(displacement, fixed_mask, density)
+        sems=3 + 4 * count,
+        limit=PREPARE_LIMIT,
+    )(displacement, fixed_mask, density, void_mask)
+    partner = lax.ppermute(moved, "lc", [(1, 0)])
+    halos = [lax.ppermute(a, "gy", y_pairs(step)) for a, step in zip(packs, steps)][::-1]
+    crossing_out, *corners = call(
+        functools.partial(pack_kernel, sides),
+        [(8, rows, depth)] + [(8, SLOT, depth)] * count,
+        [],
+        [vmem()] * 3,
+        1 << 18,
+    )(moved, partner, design)
     crossed = lax.ppermute(crossing_out, ("gz", "lc"), crossing)
-    straightened = lax.ppermute(straight_out, ("gz", "lc"), straight)
-    density, void_mask, fixed_mask, displacement, crossing_out = lax.optimization_barrier(
-        (density, void_mask, fixed_mask, displacement, crossing_out)
-    )
-    edges = call(
-        functools.partial(edge_kernel, sides),
-        [(5 * layers, SLOT, depth), (5, SLOT, depth), (3, SLOT, depth)] * count,
-        [],
-        [vmem()] * 4,
-        1 << 20,
-    )(displacement, fixed_mask, density, void_mask)
-    halos = [lax.ppermute(a, "gy", y_pairs(step)) for a, step in zip(edges[0::3], steps)][::-1]
-    axes = ("gz", "gy", "lc")
-    crossed_corners = [lax.ppermute(a, axes, diagonal(crossing, step)) for a, step in zip(edges[1::3], steps)][::-1]
-    straight_corners = [lax.ppermute(a, axes, diagonal(straight, step)) for a, step in zip(edges[2::3], steps)][::-1]
+    crossed_corners = [
+        lax.ppermute(a, ("gz", "gy", "lc"), diagonal(crossing, step))
+        for a, step in zip(corners, steps)
+    ][::-1]
 
     mine, theirs, last = call(
         functools.partial(energy_kernel, count),
@@ -543,9 +573,9 @@
         functools.partial(sensed_kernel, count),
         [(half, wide, depth), (2, wide, depth)],
         [((3, 4, wide, depth), real), ((4, 6, wide, depth), real)],
-        [vmem()] * 4 + [smem] + [vmem()] * (2 + 2 * count),
+        [vmem()] * 4 + [smem] + [vmem()] * (1 + count),
         1 << 22,
-    )(scaling, mine, received, last, load_ratio, crossed, straightened, *crossed_corners, *straight_corners)
+    )(scaling, mine, received, last, load_ratio, crossed, *crossed_corners)
     own_beyond = lax.ppermute(outgoing, ("gz", "lc"), crossing)
     other = lax.ppermute(sensed, "lc", swap)
     (inner,) = call(
@@ -556,20 +586,19 @@
         1 << 22,
     )(void_mask, sensed, other)
     other_beyond = lax.ppermute(own_beyond, "lc", swap)
+    ends = [((6, wide, depth), real), ((6, 2, wide, depth), real)]
+    (near,) = call(near_kernel, [(2, rows, depth)], ends, [vmem()] * 3, 1 << 21)(
+        void_mask, sensed, own_beyond
+    )
     (gradient,) = call(
-        outer_kernel,
+        far_kernel,
         [(layers, rows, depth)],
-        [
-            ((layers + 4, wide, depth), real),
-            ((layers + 4, 2, wide, depth), real),
-            ((2, rows, depth), real),
-            ((2, rows, depth), real),
-        ],
-        [vmem()] * 6,
-        1 << 22,
+        ends + [((2, rows, depth), real)],
+        [vmem()] * 5,
+        1 << 21,
         out_specs=[hbm()],
         sems=3,
-    )(void_mask, sensed, other, own_beyond, other_beyond, inner)
+    )(void_mask, other, other_beyond, inner, near)
     return gradient
 
 

time: 37.3 us -> 32.2 us (0.86)
  starting transfers between devices: 22.6 us -> 19.9 us
  local copies, waits for them, and re-layouts: 1.06 us -> 0.02 us
  waiting for transfers between devices: 4.57 us -> 3.87 us
  Pallas kernels: 8.56 us -> 8.11 us
    ppermute x1, starting transfers between devices: 10.3 us -> 7.08 us  [shards(): other = lax.ppermute(sensed, 'lc', swap)]
    unnamed x14 -> x10, local copies, waits for them, and re-layouts: 1.06 us -> 0.02 us
    pallas_call x3 -> x4, Pallas kernels: 3.52 us -> 3.03 us  [the longest x1 1.43 us: shards(): call(functools.partial(prepare_kernel, sides), [(3, wide, depth), (2, wid...]
    ppermute x3 -> x2, starting transfers between devices: 2 us -> 2.07 us  [the longest x1 1.42 us: shards(): partner = lax.ppermute(moved, 'lc', [(1, 0)])]
  transfers between devices with their start and end apart: 9 -> 8, of which waited for: 2 -> 1; matrix products, arithmetic and copies ran while one was open for 0% -> 0% of each run, Pallas kernels for 4% -> 15%
where the time goes in v3:
time: 32.2 us; the launch traced here: 32 us
  starting transfers between devices  19.9 us (62%)
  Pallas kernels  8.11 us (25%)
  waiting for transfers between devices  3.87 us (12%)
    ppermute x1, starting transfers between devices, shards(): other = lax.ppermute(sensed, 'lc', swap)  7.08 us
    ppermute x1, starting transfers between devices, shards(): other_beyond = lax.ppermute(own_beyond, 'lc', swap)  5.93 us
    ppermute x1, waiting for transfers between devices, shards(): lax.ppermute(a, 'gy', y_pairs(step))  3.85 us
    ppermute x1, starting transfers between devices, shards(): lax.ppermute(a, 'gy', y_pairs(step))  3.04 us
    pallas_call x1, Pallas kernels, shards(): call(functools.partial(energy_kernel, count), [(half, wide, depth), (half...  2.84 us
    pallas_call x1, Pallas kernels, shards(): call(functools.partial(prepare_kernel, sides), [(3, wide, depth), (2, wid...  1.43 us
    ppermute x1, starting transfers between devices, shards(): partner = lax.ppermute(moved, 'lc', [(1, 0)])  1.42 us
    pallas_call x1, Pallas kernels, shards(): call(far_kernel, [(layers, rows, depth)], ends + [((2, rows, depth), real...  1.15 us
  transfers between devices with their start and end apart: 8, of which 1 were waited for; matrix products, arithmetic and copies ran while one was open for 0% of the time, Pallas kernels for 15%

profile of v3, /device:TPU:0, one launch (start us, length us, event | category | flops | bytes accessed | tf_op | source)
XLA Modules:
  0.0 32.0 jit_solution(12186282880919143887)
XLA Ops:
  0.0 1.4 %shard_map.55 = (f32[3,72,256]{2,1,0:T(8,128)S(1)}, f32[2,72,256]{2,1,0:T(8,128)S(1)}, f32[40,4,256]{2,1,0:T(4,128)S(1)}) custom-call(f32[1,3,8,64,256]{4,3,2,1,0:T(8,128)} %displacement.3, s32[8,64,256]{2,1,0:T(8,128)} %fixed.3, f32[8,64,256]{2,1,0:T(8,128)} %density.3, s32[8,64,256]{2,1,0:T(8,128)} %void.9), custom_call_target="tpu_custom_call" | custom-call | flops 262144 | bytes 1048576 | tf_op jit(solution)/shard_map/pallas_call | solution.py:533
  1.4 0.0 copy-start
  1.5 0.0 copy-start.3
  1.5 1.4 %collective-permute-start = (f32[3,72,256]{2,1,0:T(8,128)S(1)}, f32[3,72,256]{2,1,0:T(8,128)S(1)}, u32[]{:S(2)}, u32[]{:S(2)}) collective-permute-start(f32[3,72,256]{2,1,0:T(8,128)S(1)} %get-tuple-element.15.moved), channel_id=1, source_target_pairs={{1,0},{3,2},{5,4},{7,6},{9,8},{11,10},{13,12},{15,14},{17,16},{19,... | collective-permute-start | bytes 663560 | tf_op jit(solution)/shard_map/ppermute | solution.py:542
  2.9 3.0 %collective-permute-start.2 = (f32[40,4,256]{2,1,0:T(4,128)S(1)}, f32[40,4,256]{2,1,0:T(4,128)S(1)}, u32[]{:S(2)}, u32[]{:S(2)}) collective-permute-start(f32[40,4,256]{2,1,0:T(4,128)S(1)} %get-tuple-element.18), channel_id=1, source_target_pairs={{0,2},{2,0},{1,3},{3,1},{4,6},{6,4},{5,7},{7,5},{8,10},{10,8},{9,1... | collective-permute-start | bytes 491528 | tf_op jit(solution)/shard_map/ppermute | solution.py:543
  5.9 0.0 collective-permute-done.partner
  6.0 0.7 %collective-permute-start.1 = (f32[8,64,256]{2,1,0:T(8,128)S(1)}, f32[8,64,256]{2,1,0:T(8,128)S(1)}, u32[]{:S(2)}, u32[]{:S(2)}) collective-permute-start(f32[8,64,256]{2,1,0:T(8,128)S(1)} %get-tuple-element.17), channel_id=1, source_target_pairs={{4,1},{1,4},{8,5},{5,8},{12,9},{9,12},{6,3},{3,6},{10,7},{7,10},{1... | collective-permute-start | bytes 1572872 | tf_op jit(solution)/shard_map/ppermute | solution.py:551
  6.7 3.9 %collective-permute-done.2.refs_0_ = f32[40,4,256]{2,1,0:T(4,128)S(1)} collective-permute-done((f32[40,4,256]{2,1,0:T(4,128)S(1)}, f32[40,4,256]{2,1,0:T(4,128)S(1)}, u32[]{:S(2)}, u32[]{:S(2)}) %collective-permute-start.2) | collective-permute-done | bytes 163872 | tf_op jit(solution)/shard_map/ppermute | solution.py:543
  10.6 2.8 %shard_map.58 = (f32[4,72,256]{2,1,0:T(8,128)S(1)}, f32[7,72,256]{2,1,0:T(8,128)S(1)}, f32[3,72,256]{2,1,0:T(8,128)S(1)}) custom-call(f32[1,3,8,64,256]{4,3,2,1,0:T(8,128)S(1)} %copy-done.1, s32[8,64,256]{2,1,0:T(8,128)S(1)} %copy-done.2, s32[2]{0:T(128)S(1)} %copy-done.4, f32[40,4,256]{2,1,0:T(4,128)S(1)} %collective-permute-done.2.refs_0_), custom_call_target="tpu_custom_call" | custom-call | flops 16777216 | bytes 1048576 | tf_op jit(solution)/shard_map/pallas_call | solution.py:557
  13.4 0.4 %collective-permute-start.4 = (f32[7,72,256]{2,1,0:T(8,128)S(1)}, f32[7,72,256]{2,1,0:T(8,128)S(1)}, u32[]{:S(2)}, u32[]{:S(2)}) collective-permute-start(f32[7,72,256]{2,1,0:T(8,128)S(1)} %get-tuple-element.21), channel_id=1, source_target_pairs={{0,1},{1,0},{2,3},{3,2},{4,5},{5,4},{6,7},{7,6},{8,9},{9,8},{10,11... | collective-permute-start | bytes 1548296 | tf_op jit(solution)/shard_map/ppermute | solution.py:564
  13.8 0.7 %collective-permute-start.3 = (f32[8,4,256]{2,1,0:T(4,128)S(1)}, f32[8,4,256]{2,1,0:T(4,128)S(1)}, u32[]{:S(2)}, u32[]{:S(2)}) collective-permute-start(f32[8,4,256]{2,1,0:T(4,128)S(1)} %get-tuple-element.19), channel_id=1, source_target_pairs={{4,3},{6,1},{1,6},{3,4},{8,7},{10,5},{5,10},{7,8},{12,11},{14,9},{... | collective-permute-start | bytes 98312 | tf_op jit(solution)/shard_map/ppermute | solution.py:553
  14.4 0.0 collective-permute-done.3.refs_1_.refs_0_
  14.4 0.0 collective-permute-done.1.beyond.above
  14.5 1.0 %shard_map.57.scaling = f32[4,72,256]{2,1,0:T(8,128)S(1)} custom-call(f32[8,64,256]{2,1,0:T(8,128)S(1)} %copy-done.3, s32[8,64,256]{2,1,0:T(8,128)S(1)} %copy-done, f32[8,64,256]{2,1,0:T(8,128)S(1)} %collective-permute-done.1.beyond.above, f32[40,4,256]{2,1,0:T(4,128)S(1)} %collective-permute-done.2.refs_0_, ...), custom_call_target="tpu_custom_call" | custom-call | flops 4194304 | bytes 1048576 | tf_op jit(solution)/shard_map/pallas_call | solution.py:565
  15.5 0.0 collective-permute-done.4.received
  15.5 0.6 %shard_map.59 = (f32[4,72,256]{2,1,0:T(8,128)S(1)}, f32[2,72,256]{2,1,0:T(8,128)S(1)}) custom-call(f32[4,72,256]{2,1,0:T(8,128)S(1)} %shard_map.57.scaling, f32[4,72,256]{2,1,0:T(8,128)S(1)} %get-tuple-element.20.mine, f32[7,72,256]{2,1,0:T(8,128)S(1)} %collective-permute-done.4.received, f32[3,72,256]{2,1,0:T(8,128)S(1)} %get-tuple-element.22.last, ...), custom_call_target="tpu_custom_call" | custom-call | flops 4194304 | bytes 1048576 | tf_op jit(solution)/shard_map/pallas_call | solution.py:572
  16.1 7.1 %collective-permute-start.5 = (f32[4,72,256]{2,1,0:T(8,128)S(1)}, f32[4,72,256]{2,1,0:T(8,128)S(1)}, u32[]{:S(2)}, u32[]{:S(2)}) collective-permute-start(f32[4,72,256]{2,1,0:T(8,128)S(1)} %get-tuple-element.23.own), channel_id=1, source_target_pairs={{0,1},{1,0},{2,3},{3,2},{4,5},{5,4},{6,7},{7,6},{8,9},{9,8},{10,11... | collective-permute-start | bytes 884744 | tf_op jit(solution)/shard_map/ppermute | solution.py:580
  23.2 0.7 %collective-permute-start.6 = (f32[2,72,256]{2,1,0:T(8,128)S(1)}, f32[2,72,256]{2,1,0:T(8,128)S(1)}, u32[]{:S(2)}, u32[]{:S(2)}) collective-permute-start(f32[2,72,256]{2,1,0:T(8,128)S(1)} %get-tuple-element.24), channel_id=1, source_target_pairs={{4,1},{1,4},{8,5},{5,8},{12,9},{9,12},{6,3},{3,6},{10,7},{7,10},{1... | collective-permute-start | bytes 442376 | tf_op jit(solution)/shard_map/ppermute | solution.py:579
  23.8 0.0 collective-permute-done.6.beyond
  23.8 5.9 %collective-permute-start.7 = (f32[2,72,256]{2,1,0:T(8,128)S(1)}, f32[2,72,256]{2,1,0:T(8,128)S(1)}, u32[]{:S(2)}, u32[]{:S(2)}) collective-permute-start(f32[2,72,256]{2,1,0:T(8,128)S(1)} %collective-permute-done.6.beyond), channel_id=1, source_target_pairs={{0,1},{1,0},{2,3},{3,2},{4,5},{5,4},{6,7},{7,6},{8,9},{9,8},{10,11... | collective-permute-start | bytes 442376 | tf_op jit(solution)/shard_map/ppermute | solution.py:588
  29.8 0.4 %shard_map.61.near = f32[2,64,256]{2,1,0:T(8,128)S(1)} custom-call(s32[8,64,256]{2,1,0:T(8,128)S(1)} %copy-done, f32[4,72,256]{2,1,0:T(8,128)S(1)} %get-tuple-element.23.own, f32[2,72,256]{2,1,0:T(8,128)S(1)} %collective-permute-done.6.beyond), custom_call_target="tpu_custom_call" | custom-call | flops 2097152 | bytes 1048576 | tf_op jit(solution)/shard_map/pallas_call | solution.py:590
  30.2 0.0 collective-permute-done.5.other
  30.2 0.7 %shard_map.60.inner = f32[4,64,256]{2,1,0:T(8,128)S(1)} custom-call(s32[8,64,256]{2,1,0:T(8,128)S(1)} %copy-done, f32[4,72,256]{2,1,0:T(8,128)S(1)} %get-tuple-element.23.own, f32[4,72,256]{2,1,0:T(8,128)S(1)} %collective-permute-done.5.other), custom_call_target="tpu_custom_call" | custom-call | flops 4194304 | bytes 1048576 | tf_op jit(solution)/shard_map/pallas_call | solution.py:581
  30.9 1.1 %shard_map.62 = f32[8,64,256]{2,1,0:T(8,128)} custom-call(s32[8,64,256]{2,1,0:T(8,128)S(1)} %copy-done, f32[4,72,256]{2,1,0:T(8,128)S(1)} %collective-permute-done.5.other, f32[2,72,256]{2,1,0:T(8,128)S(1)} %collective-permute-done.7.beyond, f32[4,64,256]{2,1,0:T(8,128)S(1)} %shard_map.60.inner, f32[2,64,256]{2,1,0:T(8,128)S(1)} %shard_map.61.near), custom_call_target="tpu_custom_call" | custom-call | flops 2097152 | bytes 1048576 | tf_op jit(solution)/shard_map/pallas_call | solution.py:593
  (10 shorter events, 0.1 us)
Async XLA Ops:
  0.0 10.5 %copy-start.1 = (f32[1,3,8,64,256]{4,3,2,1,0:T(8,128)S(1)}, f32[1,3,8,64,256]{4,3,2,1,0:T(8,128)}, u32[]{:S(2)}) copy-start(f32[1,3,8,64,256]{4,3,2,1,0:T(8,128)} %displacement.3) | copy-start | bytes 4718596
  0.0 10.5 %copy-start.2 = (s32[8,64,256]{2,1,0:T(8,128)S(1)}, s32[8,64,256]{2,1,0:T(8,128)}, u32[]{:S(2)}) copy-start(s32[8,64,256]{2,1,0:T(8,128)} %fixed.3) | copy-start | bytes 1572868
  0.0 10.5 %copy-start.4 = (s32[2]{0:T(128)S(1)}, s32[2]{0:T(128)}, u32[]{:S(2)}) copy-start(s32[2]{0:T(128)} %ratio.3) | copy-start | bytes 28
  1.4 13.0 %copy-start = (s32[8,64,256]{2,1,0:T(8,128)S(1)}, s32[8,64,256]{2,1,0:T(8,128)}, u32[]{:S(2)}) copy-start(s32[8,64,256]{2,1,0:T(8,128)} %void.9) | copy-start | bytes 1572868
  1.5 13.0 %copy-start.3 = (f32[8,64,256]{2,1,0:T(8,128)S(1)}, f32[8,64,256]{2,1,0:T(8,128)}, u32[]{:S(2)}) copy-start(f32[8,64,256]{2,1,0:T(8,128)} %density.3) | copy-start | bytes 1572868
  1.5 4.5 %collective-permute-start = (f32[3,72,256]{2,1,0:T(8,128)S(1)}, f32[3,72,256]{2,1,0:T(8,128)S(1)}, u32[]{:S(2)}, u32[]{:S(2)}) collective-permute-start(f32[3,72,256]{2,1,0:T(8,128)S(1)} %get-tuple-element.15.moved), channel_id=1, source_target_pairs={{1,0},{3,2},{5,4},{7,6},{9,8},{11,10},{13,12},{15,14},{17,16},{19,... | collective-permute-start | bytes 663560 | tf_op jit(solution)/shard_map/ppermute | solution.py:542
  2.9 7.6 %collective-permute-start.2 = (f32[40,4,256]{2,1,0:T(4,128)S(1)}, f32[40,4,256]{2,1,0:T(4,128)S(1)}, u32[]{:S(2)}, u32[]{:S(2)}) collective-permute-start(f32[40,4,256]{2,1,0:T(4,128)S(1)} %get-tuple-element.18), channel_id=1, source_target_pairs={{0,2},{2,0},{1,3},{3,1},{4,6},{6,4},{5,7},{7,5},{8,10},{10,8},{9,1... | collective-permute-start | bytes 491528 | tf_op jit(solution)/shard_map/ppermute | solution.py:543
  6.0 8.5 %collective-permute-start.1 = (f32[8,64,256]{2,1,0:T(8,128)S(1)}, f32[8,64,256]{2,1,0:T(8,128)S(1)}, u32[]{:S(2)}, u32[]{:S(2)}) collective-permute-start(f32[8,64,256]{2,1,0:T(8,128)S(1)} %get-tuple-element.17), channel_id=1, source_target_pairs={{4,1},{1,4},{8,5},{5,8},{12,9},{9,12},{6,3},{3,6},{10,7},{7,10},{1... | collective-permute-start | bytes 1572872 | tf_op jit(solution)/shard_map/ppermute | solution.py:551
  13.4 2.1 %collective-permute-start.4 = (f32[7,72,256]{2,1,0:T(8,128)S(1)}, f32[7,72,256]{2,1,0:T(8,128)S(1)}, u32[]{:S(2)}, u32[]{:S(2)}) collective-permute-start(f32[7,72,256]{2,1,0:T(8,128)S(1)} %get-tuple-element.21), channel_id=1, source_target_pairs={{0,1},{1,0},{2,3},{3,2},{4,5},{5,4},{6,7},{7,6},{8,9},{9,8},{10,11... | collective-permute-start | bytes 1548296 | tf_op jit(solution)/shard_map/ppermute | solution.py:564
  13.8 0.7 %collective-permute-start.3 = (f32[8,4,256]{2,1,0:T(4,128)S(1)}, f32[8,4,256]{2,1,0:T(4,128)S(1)}, u32[]{:S(2)}, u32[]{:S(2)}) collective-permute-start(f32[8,4,256]{2,1,0:T(4,128)S(1)} %get-tuple-element.19), channel_id=1, source_target_pairs={{4,3},{6,1},{1,6},{3,4},{8,7},{10,5},{5,10},{7,8},{12,11},{14,9},{... | collective-permute-start | bytes 98312 | tf_op jit(solution)/shard_map/ppermute | solution.py:553
  16.1 14.1 %collective-permute-start.5 = (f32[4,72,256]{2,1,0:T(8,128)S(1)}, f32[4,72,256]{2,1,0:T(8,128)S(1)}, u32[]{:S(2)}, u32[]{:S(2)}) collective-permute-start(f32[4,72,256]{2,1,0:T(8,128)S(1)} %get-tuple-element.23.own), channel_id=1, source_target_pairs={{0,1},{1,0},{2,3},{3,2},{4,5},{5,4},{6,7},{7,6},{8,9},{9,8},{10,11... | collective-permute-start | bytes 884744 | tf_op jit(solution)/shard_map/ppermute | solution.py:580
  23.2 0.7 %collective-permute-start.6 = (f32[2,72,256]{2,1,0:T(8,128)S(1)}, f32[2,72,256]{2,1,0:T(8,128)S(1)}, u32[]{:S(2)}, u32[]{:S(2)}) collective-permute-start(f32[2,72,256]{2,1,0:T(8,128)S(1)} %get-tuple-element.24), channel_id=1, source_target_pairs={{4,1},{1,4},{8,5},{5,8},{12,9},{9,12},{6,3},{3,6},{10,7},{7,10},{1... | collective-permute-start | bytes 442376 | tf_op jit(solution)/shard_map/ppermute | solution.py:579
  23.8 7.0 %collective-permute-start.7 = (f32[2,72,256]{2,1,0:T(8,128)S(1)}, f32[2,72,256]{2,1,0:T(8,128)S(1)}, u32[]{:S(2)}, u32[]{:S(2)}) collective-permute-start(f32[2,72,256]{2,1,0:T(8,128)S(1)} %collective-permute-done.6.beyond), channel_id=1, source_target_pairs={{0,1},{1,0},{2,3},{3,2},{4,5},{5,4},{6,7},{7,6},{8,9},{9,8},{10,11... | collective-permute-start | bytes 442376 | tf_op jit(solution)/shard_map/ppermute | solution.py:588

commit v4 on v3

--- a/solution.py
+++ b/solution.py
@@ -182,22 +182,33 @@
     return flag(rank > 0), flag(rank < lax.axis_size("gy") - 1)
 
 
+def beyond_flag():
+    rank, core = lax.axis_index("gz"), lax.axis_index("lc")
+    return flag((rank > 0) & (core == 0) | (rank < lax.axis_size("gz") - 1) & (core == 1))
+
+
 def free_of(mask):
     return (1 - mask).astype(jnp.float32)
 
 
+def edge_of(first, last, side):
+    if side == "both":
+        return jnp.where(lax.axis_index("gy") == 0, pltpu.roll(last, SLOT, 0), first)[0:SLOT]
+    return first[0:SLOT] if side == "first" else pltpu.roll(last, SLOT, 0)[0:SLOT]
+
+
 def prepare_kernel(sides, displacement, fixed, density, void, *refs):
     count = len(sides)
-    moved, design = refs[:2]
-    packs = refs[2 : 2 + count]
-    nodes, mask, node_edge, mask_edge, design_edge, void_edge, sems = refs[2 + count :]
-    layers, rows, depth = density.shape
+    crossing, corners, packs = refs[0], refs[1 : 1 + count], refs[1 + count : 1 + 2 * count]
+    nodes, mask, node_edge, mask_edge, design_edge, void_edge, sems = refs[1 + 2 * count :]
+    layers, rows, _ = density.shape
     core = lax.axis_index("lc")
+    layer_out = core * (layers - 1)
     copies = [
-        pltpu.make_async_copy(displacement.at[0, :, 0], nodes, sems.at[0]),
-        pltpu.make_async_copy(fixed.at[0], mask, sems.at[1]),
+        pltpu.make_async_copy(displacement.at[0, :, layer_out], nodes, sems.at[0]),
+        pltpu.make_async_copy(fixed.at[layer_out], mask, sems.at[1]),
         pltpu.make_async_copy(
-            density.at[pl.ds(core * (layers - 2), 2)], design.at[:, pl.ds(0, rows)], sems.at[2]
+            density.at[pl.ds(core * (layers - 2), 2)], crossing.at[pl.ds(3, 2)], sems.at[2]
         ),
     ]
     for number, side in enumerate(sides):
@@ -218,54 +229,26 @@
     for copy in copies:
         copy.wait()
     free = free_of(mask[...])
-    front = lax.broadcasted_iota(jnp.int32, (TILE, depth), 0) < SLOT
     for component in range(3):
-        value = nodes[component] * free
-        moved[component, 0:rows, :] = value
-        moved[component, rows : rows + TILE, :] = jnp.where(front, value[:TILE], value[rows - TILE :])
-    for layer in range(2):
-        first, last = design[layer, 0:TILE, :], design[layer, rows - TILE : rows, :]
-        design[layer, rows : rows + TILE, :] = jnp.where(front, first, last)
-
+        crossing[component] = nodes[component] * free
+    for side, corner in zip(sides, corners):
+        for index in range(5):
+            corner[index] = edge_of(crossing[index, 0:TILE, :], crossing[index, rows - TILE : rows, :], side)
     for number, (side, packed) in enumerate(zip(sides, packs)):
-        if side == "both":
-            from_last = lax.axis_index("gy") == 0
-        else:
-            from_last = side == "last"
-
-        def edge(tile):
-            if side == "first":
-                return tile[0:SLOT]
-            turned = pltpu.roll(tile, SLOT, 0)
-            if side == "last":
-                return turned[0:SLOT]
-            return jnp.where(from_last, turned, tile)[0:SLOT]
-
         for layer in range(layers):
             free = free_of(mask_edge[number, layer])
             for component in range(3):
-                packed[component * layers + layer] = edge(free * node_edge[number, component, layer])
-            packed[3 * layers + layer] = edge(design_edge[number, layer])
-            packed[4 * layers + layer] = edge(free_of(void_edge[number, layer]))
-
-
-def pack_kernel(sides, moved, partner, design, crossing, *corners):
-    rows = crossing.shape[1]
-    for source, base in ((moved, 0), (partner, 3), (design, 6)):
-        for index in range(source.shape[0]):
-            crossing[base + index] = source[index, 0:rows, :]
-            for side, corner in zip(sides, corners):
-                first = source[index, rows : rows + SLOT, :]
-                last = source[index, rows + SLOT : rows + TILE, :]
-                if side == "both":
-                    corner[base + index] = jnp.where(lax.axis_index("gy") == 0, last, first)
-                else:
-                    corner[base + index] = first if side == "first" else last
+                moved = free * node_edge[number, component, layer]
+                packed[component * layers + layer] = edge_of(moved, moved, side)
+            design = design_edge[number, layer]
+            packed[3 * layers + layer] = edge_of(design, design, side)
+            alive = free_of(void_edge[number, layer])
+            packed[4 * layers + layer] = edge_of(alive, alive, side)
 
 
 def energy_kernel(count, displacement, fixed, ratio, *refs):
     halos = refs[:count]
-    mine, theirs, last, nodes, modes, energy = refs[count:]
+    mine, theirs, nodes, modes, energy = refs[count:]
     layers, rows, depth = fixed.shape
     wide = rows + TILE
     half = layers // 2
@@ -287,19 +270,26 @@
             for part, below, above in zip(parts_of(depth), lower, upper):
                 energy[layer, row : row + TILE, part] = element_energy(below, above, scale)
             lower = upper
-    for component in range(3):
-        last[component] = nodes[component, layers - 1]
     mine[0 : half - 1] = energy[pl.ds(core * half, half - 1)]
+    theirs[half : half + 3] = nodes[:, (1 - core) * (layers - 1)]
 
     @pl.when(core == 0)
     def _():
         mine[half - 1] = energy[half - 1]
         theirs[0 : half - 1] = energy[half : layers - 1]
-        theirs[half : half + 3] = nodes[:, layers - 1]
+        theirs[half - 1] = energy[half - 1]
 
     @pl.when(core == 1)
     def _():
         theirs[0:half] = energy[0:half]
+        mine[half - 1] = filled((wide, depth))
+
+    @pl.when((core == 1) & (lax.axis_index("gz") == lax.axis_size("gz") - 1))
+    def _():
+        zero = [filled((TILE, LANES))] * 12
+        for row in range(0, wide, TILE):
+            for part, below in zip(parts_of(depth), node_modes(modes, layers - 1, row)):
+                mine[half - 1, row : row + TILE, part] = element_energy(below, zero, scale)
 
 
 def scaling_kernel(count, density, void, beyond, *refs):
@@ -312,17 +302,20 @@
     has_left, has_right = y_flags()
     start = core * half
 
-    def place(slot, middle, left, right):
-        design[slot, 0:rows, :] = middle
-        design[slot, rows : rows + SLOT, :] = right * has_right
-        design[slot, rows + SLOT : wide, :] = left * has_left
+    has_beyond = beyond_flag()
+
+    def place(slot, middle, left, right, keep=1.0):
+        design[slot, 0:rows, :] = middle * keep
+        design[slot, rows : rows + SLOT, :] = right * (keep * has_right)
+        design[slot, rows + SLOT : wide, :] = left * (keep * has_left)
 
     for index in range(half + 2):
         source = index + core * (half - 2)
         at = 3 * layers + source
         place(index + 2 * (1 - core), density[source], halos[0][at], halos[-1][at])
     for index in range(2):
-        place(core * (half + 2) + index, beyond[6 + index], corners[0][6 + index], corners[-1][6 + index])
+        at = 3 + index
+        place(core * (half + 2) + index, beyond[at], corners[0][at], corners[-1][at], has_beyond)
     for layer in range(half):
         at = 4 * layers + start + layer
         halo_alive[layer, 0:SLOT, :] = halos[-1][at] * has_right
@@ -379,93 +372,115 @@
                 scaling[layer, row : row + TILE, part] = value * alive
 
 
-def sensed_kernel(count, scaling, mine, received, last, ratio, above, *refs):
+def sensed_kernel(count, scaling, mine, received, ratio, crossed, *refs):
     corners = refs[:count]
     sensed, outgoing, nodes, modes = refs[count:]
     half, wide, depth = scaling.shape
     rows = wide - TILE
     core = lax.axis_index("lc")
-    for layer in range(half - 1):
+    has_left, has_right = y_flags()
+    has_beyond = beyond_flag()
+    for component in range(3):
+        nodes[component, core, 0:rows, :] = crossed[component] * has_beyond
+        nodes[component, core, rows : rows + SLOT, :] = corners[-1][component] * (has_beyond * has_right)
+        nodes[component, core, rows + SLOT : wide, :] = corners[0][component] * (has_beyond * has_left)
+        nodes[component, 1 - core] = received[half + component]
+    for index in range(2):
+        row_modes(nodes, modes, index, index, wide)
+    scale = shares(ratio)(1 - core)
+    between = 2 - core
+    for row in range(0, wide, TILE):
+        lower, upper = (node_modes(modes, index, row) for index in (0, 1))
+        for part, below, above in zip(parts_of(depth), lower, upper):
+            outgoing[between, row : row + TILE, part] = element_energy(below, above, scale)
+    for layer in range(half):
         sensed[layer] = scaling[layer] * (mine[layer] + received[layer])
 
     @pl.when(core == 0)
     def _():
-        sensed[half - 1] = scaling[half - 1] * (mine[half - 1] + received[half - 1])
-        outgoing[...] = sensed[0:2]
+        outgoing[0:2] = sensed[0:2]
 
     @pl.when(core == 1)
     def _():
-        has_left, has_right = y_flags()
-        scales = shares(ratio)
-        for case in range(2):
-            for component in range(3):
-                at = 3 * case + component
-                if case == 0:
-                    nodes[component, 2 * case] = received[half + component]
-                else:
-                    nodes[component, 2 * case] = last[component]
-                nodes[component, 2 * case + 1, 0:rows, :] = above[at]
-                nodes[component, 2 * case + 1, rows : rows + SLOT, :] = corners[-1][at] * has_right
-                nodes[component, 2 * case + 1, rows + SLOT : wide, :] = corners[0][at] * has_left
-            for index in (2 * case, 2 * case + 1):
-                row_modes(nodes, modes, index, index, wide)
-        for row in range(0, wide, TILE):
-            totals = None
-            for case in range(2):
-                lower, upper = (node_modes(modes, 2 * case + side, row) for side in (0, 1))
-                energies = [element_energy(a, b, scales(case)) for a, b in zip(lower, upper)]
-                totals = energies if totals is None else [a + b for a, b in zip(totals, energies)]
-            for part, value in zip(parts_of(depth), totals):
-                sensed[half - 1, row : row + TILE, part] = scaling[half - 1, row : row + TILE, part] * value
-        outgoing[...] = sensed[half - 2 : half]
+        outgoing[0] = sensed[half - 2]
+        outgoing[2] = scaling[half - 1]
+
+
+def ends_kernel(scaling, mine, outgoing, received, ends):
+    half = scaling.shape[0]
+    core = lax.axis_index("lc")
+
+    has_beyond = beyond_flag()
+
+    @pl.when(core == 0)
+    def _():
+        ends[0] = has_beyond * received[0]
+        ends[1] = has_beyond * (received[2] * (received[1] + outgoing[2]))
+        ends[2] = received[0]
+
+    @pl.when(core == 1)
+    def _():
+        ends[0] = scaling[half - 1] * ((outgoing[1] + mine[half - 1]) + has_beyond * received[2])
+        ends[1] = has_beyond * received[0]
+        ends[2] = has_beyond * received[1]
 
 
 def inner_kernel(void, own, other, gradient, field, sums):
     layers, rows, depth = void.shape
-    wide = rows + TILE
     half = layers // 2
     core = lax.axis_index("lc")
     field[pl.ds(core * half, half)] = own[...]
     field[pl.ds((1 - core) * half, half)] = other[...]
-    row_sums(field, sums, range(layers), wide)
+    row_sums(field, sums, range(1, layers - 1), rows + TILE)
     for row in range(0, rows, TILE):
-        for layer in range(2, layers - 2):
+        for layer in range(3, layers - 3):
             filtered = cone_tile(field, sums, layer, row)
             for part, value in zip(parts_of(depth), filtered):
                 alive = free_of(void[layer, row : row + TILE, part])
-                gradient[layer - 2, row : row + TILE, part] = alive * value
-
-
-def side_rows(side, void, own, beyond, result, field, sums):
+                gradient[layer - 3, row : row + TILE, part] = alive * value
+
+
+def side_rows(side, void, own, other, ends, result, field, sums):
     layers, rows, depth = void.shape
     half = own.shape[0]
-    field[pl.ds(side * 4, 2)] = beyond[...]
-    field[pl.ds(2 - 2 * side, 4)] = own[pl.ds(side * (half - 4), 4)]
-    row_sums(field, sums, range(6), rows + TILE)
-    base = side * (layers - 2)
+
+    @pl.when(side == 0)
+    def _():
+        field[0:2] = ends[0:2]
+        field[2:6] = own[0:4]
+        field[6] = own[4] if half > 4 else other[0]
+
+    @pl.when(side == 1)
+    def _():
+        field[0] = own[half - 5] if half > 4 else other[half - 1]
+        field[1:4] = own[half - 4 : half - 1]
+        field[4:7] = ends[...]
+
+    row_sums(field, sums, range(7), rows + TILE)
+    base = side * (layers - 3)
     for row in range(0, rows, TILE):
-        for layer in range(2):
+        for layer in range(3):
             filtered = cone_tile(field, sums, layer + 2, row)
             for part, value in zip(parts_of(depth), filtered):
                 alive = free_of(void[base + layer, row : row + TILE, part])
                 result[layer, row : row + TILE, part] = alive * value
 
 
-def near_kernel(void, own, beyond, result, field, sums):
-    side_rows(lax.axis_index("lc"), void, own, beyond, result, field, sums)
-
-
-def far_kernel(void, other, beyond, inner, near, gradient, field, sums, far, sems):
+def near_kernel(void, own, other, ends, result, field, sums):
+    side_rows(lax.axis_index("lc"), void, own, other, ends, result, field, sums)
+
+
+def far_kernel(void, own, other, ends, inner, near, gradient, field, sums, far, sems):
     layers = void.shape[0]
     core = lax.axis_index("lc")
     copies = [
-        pltpu.make_async_copy(inner, gradient.at[pl.ds(2, layers - 4)], sems.at[0]),
-        pltpu.make_async_copy(near, gradient.at[pl.ds(core * (layers - 2), 2)], sems.at[1]),
-        pltpu.make_async_copy(far, gradient.at[pl.ds((1 - core) * (layers - 2), 2)], sems.at[2]),
+        pltpu.make_async_copy(inner, gradient.at[pl.ds(3, layers - 6)], sems.at[0]),
+        pltpu.make_async_copy(near, gradient.at[pl.ds(core * (layers - 3), 3)], sems.at[1]),
+        pltpu.make_async_copy(far, gradient.at[pl.ds((1 - core) * (layers - 3), 3)], sems.at[2]),
     ]
     for copy in copies[:2]:
         copy.start()
-    side_rows(1 - core, void, other, beyond, far, field, sums)
+    side_rows(1 - core, void, other, own, ends, far, field, sums)
     copies[2].start()
     for copy in copies:
         copy.wait()
@@ -502,22 +517,28 @@
     real = jnp.float32
     smem = pl.BlockSpec(memory_space=pltpu.SMEM)
     swap = [(0, 1), (1, 0)]
-    crossing = []
+    across = []
     for z in range(1, gz):
-        crossing.append((z * lc, (z - 1) * lc + 1))
-        crossing.append(((z - 1) * lc + 1, z * lc))
+        across.append((z * lc, (z - 1) * lc + 1))
+        across.append(((z - 1) * lc + 1, z * lc))
 
     def y_pairs(step):
         if gy == 2:
             return [(y, 1 - y) for y in range(gy)]
         return [(y, y + step) for y in range(gy) if 0 <= y + step < gy]
 
-    def diagonal(pairs, step):
-        return [
-            ((a // lc * gy + y) * lc + a % lc, (b // lc * gy + peer) * lc + b % lc)
-            for a, b in pairs
-            for y, peer in y_pairs(step)
-        ]
+    outermost = [0, gz * lc - 1] if gy % 2 == 0 else []
+
+    def at(place, y):
+        return (place // lc * gy + y) * lc + place % lc
+
+    axes = ("gz", "gy", "lc")
+    swaps = [(at(place, y), at(place, y ^ 1)) for place in outermost for y in range(gy)]
+    crossing = [(at(a, y), at(b, y)) for a, b in across for y in range(gy)] + swaps
+
+    def diagonal(step):
+        pairs = [(at(a, y), at(b, peer)) for a, b in across for y, peer in y_pairs(step)]
+        return pairs + swaps if gy == 2 else pairs
 
     sides, steps = (["both"], [1]) if gy == 2 else (["first", "last"], [-1, 1])
     count = len(sides)
@@ -530,33 +551,22 @@
         ((count, layers, TILE, depth), real),
         ((count, layers, TILE, depth), jnp.int32),
     ]
-    moved, design, *packs = call(
+    crossing_out, *edges = call(
         functools.partial(prepare_kernel, sides),
-        [(3, wide, depth), (2, wide, depth)] + [(5 * layers, SLOT, depth)] * count,
+        [(5, rows, depth)] + [(5, SLOT, depth)] * count + [(5 * layers, SLOT, depth)] * count,
         kinds,
         [hbm()] * 4,
         1 << 18,
         sems=3 + 4 * count,
         limit=PREPARE_LIMIT,
     )(displacement, fixed_mask, density, void_mask)
-    partner = lax.ppermute(moved, "lc", [(1, 0)])
-    halos = [lax.ppermute(a, "gy", y_pairs(step)) for a, step in zip(packs, steps)][::-1]
-    crossing_out, *corners = call(
-        functools.partial(pack_kernel, sides),
-        [(8, rows, depth)] + [(8, SLOT, depth)] * count,
-        [],
-        [vmem()] * 3,
-        1 << 18,
-    )(moved, partner, design)
-    crossed = lax.ppermute(crossing_out, ("gz", "lc"), crossing)
-    crossed_corners = [
-        lax.ppermute(a, ("gz", "gy", "lc"), diagonal(crossing, step))
-        for a, step in zip(corners, steps)
-    ][::-1]
-
-    mine, theirs, last = call(
+    crossed = lax.ppermute(crossing_out, axes, crossing)
+    corners = [lax.ppermute(a, axes, diagonal(step)) for a, step in zip(edges[:count], steps)][::-1]
+    halos = [lax.ppermute(a, "gy", y_pairs(step)) for a, step in zip(edges[count:], steps)][::-1]
+
+    mine, theirs = call(
         functools.partial(energy_kernel, count),
-        [(half, wide, depth), (half + 3, wide, depth), (3, wide, depth)],
+        [(half, wide, depth), (half + 3, wide, depth)],
         [((3, layers, wide, depth), real), ((layers, 6, wide, depth), real), ((layers, wide, depth), real)],
         [vmem(), vmem(), smem] + [vmem()] * count,
         1 << 24,
@@ -568,37 +578,40 @@
         [((half + 4, wide, depth), real), ((half + 4, 2, wide, depth), real), ((half, TILE, depth), real)],
         [vmem()] * (3 + 2 * count),
         1 << 22,
-    )(density, void_mask, crossed, *halos, *crossed_corners)
+    )(density, void_mask, crossed, *halos, *corners)
     sensed, outgoing = call(
         functools.partial(sensed_kernel, count),
-        [(half, wide, depth), (2, wide, depth)],
-        [((3, 4, wide, depth), real), ((4, 6, wide, depth), real)],
-        [vmem()] * 4 + [smem] + [vmem()] * (1 + count),
+        [(half, wide, depth), (3, wide, depth)],
+        [((3, 2, wide, depth), real), ((2, 6, wide, depth), real)],
+        [vmem()] * 3 + [smem] + [vmem()] * (1 + count),
         1 << 22,
-    )(scaling, mine, received, last, load_ratio, crossed, *crossed_corners)
-    own_beyond = lax.ppermute(outgoing, ("gz", "lc"), crossing)
+    )(scaling, mine, received, load_ratio, crossed, *corners)
+    beyond = lax.ppermute(outgoing, axes, crossing)
     other = lax.ppermute(sensed, "lc", swap)
     (inner,) = call(
         inner_kernel,
-        [(layers - 4, rows, depth)],
+        [(layers - 6, rows, depth)],
         [((layers, wide, depth), real), ((layers, 2, wide, depth), real)],
         [vmem()] * 3,
         1 << 22,
     )(void_mask, sensed, other)
-    other_beyond = lax.ppermute(own_beyond, "lc", swap)
-    ends = [((6, wide, depth), real), ((6, 2, wide, depth), real)]
-    (near,) = call(near_kernel, [(2, rows, depth)], ends, [vmem()] * 3, 1 << 21)(
-        void_mask, sensed, own_beyond
+    (own_ends,) = call(ends_kernel, [(3, wide, depth)], [], [vmem()] * 4, 1 << 18)(
+        scaling, mine, outgoing, beyond
+    )
+    other_ends = lax.ppermute(own_ends, "lc", swap)
+    held = [((7, wide, depth), real), ((7, 2, wide, depth), real)]
+    (near,) = call(near_kernel, [(3, rows, depth)], held, [vmem()] * 4, 1 << 21)(
+        void_mask, sensed, other, own_ends
     )
     (gradient,) = call(
         far_kernel,
         [(layers, rows, depth)],
-        ends + [((2, rows, depth), real)],
-        [vmem()] * 5,
+        held + [((3, rows, depth), real)],
+        [vmem()] * 6,
         1 << 21,
         out_specs=[hbm()],
         sems=3,
-    )(void_mask, other, other_beyond, inner, near)
+    )(void_mask, sensed, other, other_ends, inner, near)
     return gradient
 
 

time: 32.2 us -> 30.2 us (0.938)
  starting transfers between devices: 19.9 us -> 8.08 us
  waiting for transfers between devices: 3.87 us -> 13.3 us
  Pallas kernels: 8.11 us -> 8.56 us
    ppermute x5 -> x4, waiting for transfers between devices: 0.01 us -> 9.08 us  [the longest x1 5.27 us: shards(): lax.ppermute(a, axes, diagonal(step))]
    ppermute x1, starting transfers between devices: 7.08 us -> 0.33 us  [shards(): other = lax.ppermute(sensed, 'lc', swap)]
    ppermute x5 -> x4, starting transfers between devices: 9.36 us -> 4.63 us  [the longest x1 2.02 us: shards(): beyond = lax.ppermute(outgoing, axes, crossing)]
    ppermute x1, waiting for transfers between devices: 3.85 us -> 4.2 us  [shards(): lax.ppermute(a, 'gy', y_pairs(step))]
    pallas_call x6, Pallas kernels: 4.29 us -> 4.63 us  [the longest x1 1.43 us: shards(): call(functools.partial(prepare_kernel, sides), [(5, rows, depth)] + [(5,...]
  transfers between devices with their start and end apart: 8 -> 7, of which waited for: 1 -> 4; matrix products, arithmetic and copies ran while one was open for 0% -> 0% of each run, Pallas kernels for 15% -> 7%
where the time goes in v4:
time: 30.2 us; the launch traced here: 30 us
  waiting for transfers between devices  13.3 us (44%)
  Pallas kernels  8.56 us (28%)
  starting transfers between devices  8.08 us (27%)
    ppermute x1, waiting for transfers between devices, shards(): lax.ppermute(a, axes, diagonal(step))  5.27 us
    ppermute x1, waiting for transfers between devices, shards(): lax.ppermute(a, 'gy', y_pairs(step))  4.2 us
    ppermute x1, waiting for transfers between devices, shards(): beyond = lax.ppermute(outgoing, axes, crossing)  3.64 us
    ppermute x1, starting transfers between devices, shards(): lax.ppermute(a, 'gy', y_pairs(step))  3.04 us
    pallas_call x1, Pallas kernels, shards(): call(functools.partial(energy_kernel, count), [(half, wide, depth), (half...  2.91 us
    ppermute x1, starting transfers between devices, shards(): beyond = lax.ppermute(outgoing, axes, crossing)  2.02 us
    ppermute x1, starting transfers between devices, shards(): crossed = lax.ppermute(crossing_out, axes, crossing)  1.8 us
    pallas_call x1, Pallas kernels, shards(): call(functools.partial(prepare_kernel, sides), [(5, rows, depth)] + [(5,...  1.43 us
  transfers between devices with their start and end apart: 7, of which 4 were waited for; matrix products, arithmetic and copies ran while one was open for 0% of the time, Pallas kernels for 7%

profile of v4, /device:TPU:0, one launch (start us, length us, event | category | flops | bytes accessed | tf_op | source)
XLA Modules:
  0.0 30.0 jit_solution(9478453823999765656)
XLA Ops:
  0.0 1.4 %shard_map.55 = (f32[5,64,256]{2,1,0:T(8,128)S(1)}, f32[5,4,256]{2,1,0:T(4,128)S(1)}, f32[40,4,256]{2,1,0:T(4,128)S(1)}) custom-call(f32[1,3,8,64,256]{4,3,2,1,0:T(8,128)} %displacement.3, s32[8,64,256]{2,1,0:T(8,128)} %fixed.3, f32[8,64,256]{2,1,0:T(8,128)} %density.3, s32[8,64,256]{2,1,0:T(8,128)} %void.9), custom_call_target="tpu_custom_call" | custom-call | flops 262144 | bytes 1048576 | tf_op jit(solution)/shard_map/pallas_call | solution.py:554
  1.4 0.0 copy-start
  1.5 0.0 copy-start.3
  1.5 3.0 %collective-permute-start.1 = (f32[40,4,256]{2,1,0:T(4,128)S(1)}, f32[40,4,256]{2,1,0:T(4,128)S(1)}, u32[]{:S(2)}, u32[]{:S(2)}) collective-permute-start(f32[40,4,256]{2,1,0:T(4,128)S(1)} %get-tuple-element.13), channel_id=1, source_target_pairs={{0,2},{2,0},{1,3},{3,1},{4,6},{6,4},{5,7},{7,5},{8,10},{10,8},{9,1... | collective-permute-start | bytes 491528 | tf_op jit(solution)/shard_map/ppermute | solution.py:565
  4.5 4.2 %collective-permute-done.1.refs_0_ = f32[40,4,256]{2,1,0:T(4,128)S(1)} collective-permute-done((f32[40,4,256]{2,1,0:T(4,128)S(1)}, f32[40,4,256]{2,1,0:T(4,128)S(1)}, u32[]{:S(2)}, u32[]{:S(2)}) %collective-permute-start.1) | collective-permute-done | bytes 163872 | tf_op jit(solution)/shard_map/ppermute | solution.py:565
  8.7 2.9 %shard_map.57 = (f32[4,72,256]{2,1,0:T(8,128)S(1)}, f32[7,72,256]{2,1,0:T(8,128)S(1)}) custom-call(f32[1,3,8,64,256]{4,3,2,1,0:T(8,128)S(1)} %copy-done.1, s32[8,64,256]{2,1,0:T(8,128)S(1)} %copy-done.2, s32[2]{0:T(128)S(1)} %copy-done.4, f32[40,4,256]{2,1,0:T(4,128)S(1)} %collective-permute-done.1.refs_0_), custom_call_target="tpu_custom_call" | custom-call | flops 16777216 | bytes 1048576 | tf_op jit(solution)/shard_map/pallas_call | solution.py:567
  11.6 0.1 collective-permute-start.3
  11.7 1.8 %collective-permute-start = (f32[5,64,256]{2,1,0:T(8,128)S(1)}, f32[5,64,256]{2,1,0:T(8,128)S(1)}, u32[]{:S(2)}, u32[]{:S(2)}) collective-permute-start(f32[5,64,256]{2,1,0:T(8,128)S(1)} %get-tuple-element.12), channel_id=1, source_target_pairs={{4,1},{6,3},{1,4},{3,6},{8,5},{10,7},{5,8},{7,10},{12,9},{14,11},{... | collective-permute-start | bytes 983048 | tf_op jit(solution)/shard_map/ppermute | solution.py:563
  13.5 0.3 collective-permute-start.2
  13.8 5.3 %collective-permute-done.2.refs_1_.refs_0_ = f32[5,4,256]{2,1,0:T(4,128)S(1)} collective-permute-done((f32[5,4,256]{2,1,0:T(4,128)S(1)}, f32[5,4,256]{2,1,0:T(4,128)S(1)}, u32[]{:S(2)}, u32[]{:S(2)}) %collective-permute-start.2) | collective-permute-done | bytes 20512 | tf_op jit(solution)/shard_map/ppermute | solution.py:564
  19.1 0.0 collective-permute-done.beyond.crossed
  19.1 0.0 copy-done.3
  19.1 1.0 %shard_map.56.scaling = f32[4,72,256]{2,1,0:T(8,128)S(1)} custom-call(f32[8,64,256]{2,1,0:T(8,128)S(1)} %copy-done.3, s32[8,64,256]{2,1,0:T(8,128)S(1)} %copy-done, f32[5,64,256]{2,1,0:T(8,128)S(1)} %collective-permute-done.beyond.crossed, f32[40,4,256]{2,1,0:T(4,128)S(1)} %collective-permute-done.1.refs_0_, ...), custom_call_target="tpu_custom_call" | custom-call | flops 4194304 | bytes 1048576 | tf_op jit(solution)/shard_map/pallas_call | solution.py:575
  20.1 0.0 collective-permute-done.3.received
  20.1 1.0 %shard_map.58 = (f32[4,72,256]{2,1,0:T(8,128)S(1)}, f32[3,72,256]{2,1,0:T(8,128)S(1)}) custom-call(f32[4,72,256]{2,1,0:T(8,128)S(1)} %shard_map.56.scaling, f32[4,72,256]{2,1,0:T(8,128)S(1)} %get-tuple-element.15.mine, f32[7,72,256]{2,1,0:T(8,128)S(1)} %collective-permute-done.3.received, s32[2]{0:T(128)S(1)} %copy-done.4, ...), custom_call_target="tpu_custom_call" | custom-call | flops 4194304 | bytes 1048576 | tf_op jit(solution)/shard_map/pallas_call | solution.py:582
  21.2 2.0 %collective-permute-start.5 = (f32[3,72,256]{2,1,0:T(8,128)S(1)}, f32[3,72,256]{2,1,0:T(8,128)S(1)}, u32[]{:S(2)}, u32[]{:S(2)}) collective-permute-start(f32[3,72,256]{2,1,0:T(8,128)S(1)} %get-tuple-element.18.outgoing), channel_id=1, source_target_pairs={{4,1},{6,3},{1,4},{3,6},{8,5},{10,7},{5,8},{7,10},{12,9},{14,11},{... | collective-permute-start | bytes 663560 | tf_op jit(solution)/shard_map/ppermute | solution.py:589
  23.2 0.3 %collective-permute-start.4 = (f32[4,72,256]{2,1,0:T(8,128)S(1)}, f32[4,72,256]{2,1,0:T(8,128)S(1)}, u32[]{:S(2)}, u32[]{:S(2)}) collective-permute-start(f32[4,72,256]{2,1,0:T(8,128)S(1)} %get-tuple-element.17.own), channel_id=1, source_target_pairs={{0,1},{1,0},{2,3},{3,2},{4,5},{5,4},{6,7},{7,6},{8,9},{9,8},{10,11... | collective-permute-start | bytes 884744 | tf_op jit(solution)/shard_map/ppermute | solution.py:590
  23.5 3.6 %collective-permute-done.5.received = f32[3,72,256]{2,1,0:T(8,128)S(1)} collective-permute-done((f32[3,72,256]{2,1,0:T(8,128)S(1)}, f32[3,72,256]{2,1,0:T(8,128)S(1)}, u32[]{:S(2)}, u32[]{:S(2)}) %collective-permute-start.5) | collective-permute-done | bytes 221216 | tf_op jit(solution)/shard_map/ppermute | solution.py:589
  27.2 0.5 %collective-permute-start.6 = (f32[3,72,256]{2,1,0:T(8,128)S(1)}, f32[3,72,256]{2,1,0:T(8,128)S(1)}, u32[]{:S(2)}, u32[]{:S(2)}) collective-permute-start(f32[3,72,256]{2,1,0:T(8,128)S(1)} %shard_map.59.ends), channel_id=1, source_target_pairs={{0,1},{1,0},{2,3},{3,2},{4,5},{5,4},{6,7},{7,6},{8,9},{9,8},{10,11... | collective-permute-start | bytes 663560 | tf_op jit(solution)/shard_map/ppermute | solution.py:601
  27.7 0.0 collective-permute-done.4.other
  27.7 0.5 %shard_map.61.near = f32[3,64,256]{2,1,0:T(8,128)S(1)} custom-call(s32[8,64,256]{2,1,0:T(8,128)S(1)} %copy-done, f32[4,72,256]{2,1,0:T(8,128)S(1)} %get-tuple-element.17.own, f32[4,72,256]{2,1,0:T(8,128)S(1)} %collective-permute-done.4.other, f32[3,72,256]{2,1,0:T(8,128)S(1)} %shard_map.59.ends), custom_call_target="tpu_custom_call" | custom-call | flops 2097152 | bytes 1048576 | tf_op jit(solution)/shard_map/pallas_call | solution.py:603
  28.2 0.4 %shard_map.60.inner = f32[2,64,256]{2,1,0:T(8,128)S(1)} custom-call(s32[8,64,256]{2,1,0:T(8,128)S(1)} %copy-done, f32[4,72,256]{2,1,0:T(8,128)S(1)} %get-tuple-element.17.own, f32[4,72,256]{2,1,0:T(8,128)S(1)} %collective-permute-done.4.other), custom_call_target="tpu_custom_call" | custom-call | flops 4194304 | bytes 1048576 | tf_op jit(solution)/shard_map/pallas_call | solution.py:591
  28.7 0.2 collective-permute-done.6.ends
  28.8 1.2 %shard_map.62 = f32[8,64,256]{2,1,0:T(8,128)} custom-call(s32[8,64,256]{2,1,0:T(8,128)S(1)} %copy-done, f32[4,72,256]{2,1,0:T(8,128)S(1)} %get-tuple-element.17.own, f32[4,72,256]{2,1,0:T(8,128)S(1)} %collective-permute-done.4.other, f32[3,72,256]{2,1,0:T(8,128)S(1)} %collective-permute-done.6.ends, f32[2,64,256]{2,1,0:T(8,128)S(1)} %shard_map.60.inner, ...), custom_call_target="tpu_custom_call" | custom-call | flops 2097152 | bytes 1048576 | tf_op jit(solution)/shard_map/pallas_call | solution.py:606
  (8 shorter events, 0.0 us)
Async XLA Ops:
  0.0 8.7 %copy-start.1 = (f32[1,3,8,64,256]{4,3,2,1,0:T(8,128)S(1)}, f32[1,3,8,64,256]{4,3,2,1,0:T(8,128)}, u32[]{:S(2)}) copy-start(f32[1,3,8,64,256]{4,3,2,1,0:T(8,128)} %displacement.3) | copy-start | bytes 4718596
  0.0 8.7 %copy-start.2 = (s32[8,64,256]{2,1,0:T(8,128)S(1)}, s32[8,64,256]{2,1,0:T(8,128)}, u32[]{:S(2)}) copy-start(s32[8,64,256]{2,1,0:T(8,128)} %fixed.3) | copy-start | bytes 1572868
  0.0 8.7 %copy-start.4 = (s32[2]{0:T(128)S(1)}, s32[2]{0:T(128)}, u32[]{:S(2)}) copy-start(s32[2]{0:T(128)} %ratio.3) | copy-start | bytes 28
  1.4 17.6 %copy-start = (s32[8,64,256]{2,1,0:T(8,128)S(1)}, s32[8,64,256]{2,1,0:T(8,128)}, u32[]{:S(2)}) copy-start(s32[8,64,256]{2,1,0:T(8,128)} %void.9) | copy-start | bytes 1572868
  1.5 17.6 %copy-start.3 = (f32[8,64,256]{2,1,0:T(8,128)S(1)}, f32[8,64,256]{2,1,0:T(8,128)}, u32[]{:S(2)}) copy-start(f32[8,64,256]{2,1,0:T(8,128)} %density.3) | copy-start | bytes 1572868
  1.5 7.2 %collective-permute-start.1 = (f32[40,4,256]{2,1,0:T(4,128)S(1)}, f32[40,4,256]{2,1,0:T(4,128)S(1)}, u32[]{:S(2)}, u32[]{:S(2)}) collective-permute-start(f32[40,4,256]{2,1,0:T(4,128)S(1)} %get-tuple-element.13), channel_id=1, source_target_pairs={{0,2},{2,0},{1,3},{3,1},{4,6},{6,4},{5,7},{7,5},{8,10},{10,8},{9,1... | collective-permute-start | bytes 491528 | tf_op jit(solution)/shard_map/ppermute | solution.py:565
  11.6 8.5 %collective-permute-start.3 = (f32[7,72,256]{2,1,0:T(8,128)S(1)}, f32[7,72,256]{2,1,0:T(8,128)S(1)}, u32[]{:S(2)}, u32[]{:S(2)}) collective-permute-start(f32[7,72,256]{2,1,0:T(8,128)S(1)} %get-tuple-element.16), channel_id=1, source_target_pairs={{0,1},{1,0},{2,3},{3,2},{4,5},{5,4},{6,7},{7,6},{8,9},{9,8},{10,11... | collective-permute-start | bytes 1548296 | tf_op jit(solution)/shard_map/ppermute | solution.py:574
  11.7 7.4 %collective-permute-start = (f32[5,64,256]{2,1,0:T(8,128)S(1)}, f32[5,64,256]{2,1,0:T(8,128)S(1)}, u32[]{:S(2)}, u32[]{:S(2)}) collective-permute-start(f32[5,64,256]{2,1,0:T(8,128)S(1)} %get-tuple-element.12), channel_id=1, source_target_pairs={{4,1},{6,3},{1,4},{3,6},{8,5},{10,7},{5,8},{7,10},{12,9},{14,11},{... | collective-permute-start | bytes 983048 | tf_op jit(solution)/shard_map/ppermute | solution.py:563
  13.5 5.6 %collective-permute-start.2 = (f32[5,4,256]{2,1,0:T(4,128)S(1)}, f32[5,4,256]{2,1,0:T(4,128)S(1)}, u32[]{:S(2)}, u32[]{:S(2)}) collective-permute-start(f32[5,4,256]{2,1,0:T(4,128)S(1)} %get-tuple-element.14), channel_id=1, source_target_pairs={{4,3},{6,1},{1,6},{3,4},{8,7},{10,5},{5,10},{7,8},{12,11},{14,9},{... | collective-permute-start | bytes 61448 | tf_op jit(solution)/shard_map/ppermute | solution.py:564
  21.2 6.0 %collective-permute-start.5 = (f32[3,72,256]{2,1,0:T(8,128)S(1)}, f32[3,72,256]{2,1,0:T(8,128)S(1)}, u32[]{:S(2)}, u32[]{:S(2)}) collective-permute-start(f32[3,72,256]{2,1,0:T(8,128)S(1)} %get-tuple-element.18.outgoing), channel_id=1, source_target_pairs={{4,1},{6,3},{1,4},{3,6},{8,5},{10,7},{5,8},{7,10},{12,9},{14,11},{... | collective-permute-start | bytes 663560 | tf_op jit(solution)/shard_map/ppermute | solution.py:589
  23.2 4.5 %collective-permute-start.4 = (f32[4,72,256]{2,1,0:T(8,128)S(1)}, f32[4,72,256]{2,1,0:T(8,128)S(1)}, u32[]{:S(2)}, u32[]{:S(2)}) collective-permute-start(f32[4,72,256]{2,1,0:T(8,128)S(1)} %get-tuple-element.17.own), channel_id=1, source_target_pairs={{0,1},{1,0},{2,3},{3,2},{4,5},{5,4},{6,7},{7,6},{8,9},{9,8},{10,11... | collective-permute-start | bytes 884744 | tf_op jit(solution)/shard_map/ppermute | solution.py:590
  27.2 1.6 %collective-permute-start.6 = (f32[3,72,256]{2,1,0:T(8,128)S(1)}, f32[3,72,256]{2,1,0:T(8,128)S(1)}, u32[]{:S(2)}, u32[]{:S(2)}) collective-permute-start(f32[3,72,256]{2,1,0:T(8,128)S(1)} %shard_map.59.ends), channel_id=1, source_target_pairs={{0,1},{1,0},{2,3},{3,2},{4,5},{5,4},{6,7},{7,6},{8,9},{9,8},{10,11... | collective-permute-start | bytes 663560 | tf_op jit(solution)/shard_map/ppermute | solution.py:601

commit v5 on v4

--- a/solution.py
+++ b/solution.py
@@ -161,13 +161,17 @@
 
 
 def shares(ratio):
-    total = ratio[0]
-    for case in range(1, ratio.shape[0]):
-        total = total + ratio[case]
-    total = filled((TILE, LANES), total.astype(jnp.float32))
+    values = [jnp.broadcast_to(ratio[case : case + 1, :], (TILE, LANES)) for case in range(ratio.shape[0])]
+    values = [value.astype(jnp.float32) for value in values]
+    total = values[0]
+    for value in values[1:]:
+        total = total + value
 
     def scale(case):
-        share = filled((TILE, LANES), ratio[case].astype(jnp.float32)) / total
+        chosen = values[0]
+        for number, value in enumerate(values[1:], 1):
+            chosen = jnp.where(case == number, value, chosen)
+        share = chosen / total
         return [factor * share for factor in energy_factors()]
 
     return scale
@@ -199,8 +203,8 @@
 
 def prepare_kernel(sides, displacement, fixed, density, void, *refs):
     count = len(sides)
-    crossing, corners, packs = refs[0], refs[1 : 1 + count], refs[1 + count : 1 + 2 * count]
-    nodes, mask, node_edge, mask_edge, design_edge, void_edge, sems = refs[1 + 2 * count :]
+    crossing, corners, firsts, rests = (refs[0], *(refs[1 + at * count : 1 + (at + 1) * count] for at in range(3)))
+    nodes, mask, node_edge, mask_edge, design_edge, void_edge, sems = refs[1 + 3 * count :]
     layers, rows, _ = density.shape
     core = lax.axis_index("lc")
     layer_out = core * (layers - 1)
@@ -234,90 +238,201 @@
     for side, corner in zip(sides, corners):
         for index in range(5):
             corner[index] = edge_of(crossing[index, 0:TILE, :], crossing[index, rows - TILE : rows, :], side)
-    for number, (side, packed) in enumerate(zip(sides, packs)):
+    early = first_layers(layers)
+    for number, (side, first, rest) in enumerate(zip(sides, firsts, rests)):
+        base = 3 * (layers - FIRST)
         for layer in range(layers):
             free = free_of(mask_edge[number, layer])
             for component in range(3):
                 moved = free * node_edge[number, component, layer]
-                packed[component * layers + layer] = edge_of(moved, moved, side)
+                if layer in early:
+                    first[component * FIRST + early.index(layer)] = edge_of(moved, moved, side)
+                else:
+                    rest[component * (layers - FIRST) + layer - 3] = edge_of(moved, moved, side)
             design = design_edge[number, layer]
-            packed[3 * layers + layer] = edge_of(design, design, side)
+            rest[base + layer] = edge_of(design, design, side)
             alive = free_of(void_edge[number, layer])
-            packed[4 * layers + layer] = edge_of(alive, alive, side)
-
-
-def energy_kernel(count, displacement, fixed, ratio, *refs):
+            rest[base + layers + layer] = edge_of(alive, alive, side)
+
+
+FIRST = 5
+
+
+def first_layers(layers):
+    return (0, 1, 2, layers - 2, layers - 1)
+
+
+def node_halo(firsts, rests, component, layer, layers):
+    early = first_layers(layers)
+    if layer in early:
+        at, packs = component * FIRST + early.index(layer), firsts
+    else:
+        at, packs = component * (layers - FIRST) + layer - 3, rests
+    return packs[0][at], packs[-1][at]
+
+
+def load_nodes(displacement, fixed, firsts, rests, layer, nodes, modes, slot):
+    layers, rows, _ = fixed.shape
+    wide = rows + TILE
+    has_left, has_right = y_flags()
+    free = free_of(fixed[layer])
+    for component in range(3):
+        nodes[component, slot, 0:rows, :] = displacement[0, component, layer] * free
+        left, right = node_halo(firsts, rests, component, layer, layers)
+        nodes[component, slot, rows : rows + SLOT, :] = right * has_right
+        nodes[component, slot, rows + SLOT : wide, :] = left * has_left
+    row_modes(nodes, modes, slot, slot, wide)
+
+
+def first_energy(modes, energy, tiles, scale):
+    depth = energy.shape[-1]
+    for row in range(0, TILE * tiles, TILE):
+        found = [node_modes(modes, slot, row) for slot in range(FIRST)]
+        for index, slot in enumerate((0, 1, 3)):
+            for part, below, above in zip(parts_of(depth), found[slot], found[slot + 1]):
+                energy[index, row : row + TILE, part] = element_energy(below, above, scale)
+
+
+def energy_bulk_kernel(displacement, fixed, ratio, energy, nodes, modes):
+    layers, rows, _ = fixed.shape
+    for slot, layer in enumerate(first_layers(layers)):
+        free = free_of(fixed[layer])
+        for component in range(3):
+            nodes[component, slot] = displacement[0, component, layer] * free
+        row_modes(nodes, modes, slot, slot, rows)
+    scale = shares(ratio)(lax.axis_index("lc"))
+    first_energy(modes, energy, rows // TILE - 1, scale)
+
+
+def energy_first_kernel(count, displacement, fixed, ratio, bulk, *refs):
     halos = refs[:count]
     mine, theirs, nodes, modes, energy = refs[count:]
+    layers, rows, _ = fixed.shape
+    last = rows - TILE
+    core = lax.axis_index("lc")
+    has_left, has_right = y_flags()
+    for slot, layer in enumerate(first_layers(layers)):
+        free = free_of(fixed[layer, last:rows])
+        free_next = free_of(fixed[layer, 0:TILE])
+        for component in range(3):
+            left, right = node_halo(halos, None, component, layer, layers)
+            nodes[component, slot, 0:TILE, :] = displacement[0, component, layer, last:rows] * free
+            nodes[component, slot, TILE : TILE + SLOT, :] = right * has_right
+            nodes[component, slot, TILE + SLOT : 2 * TILE, :] = left * has_left
+            nodes[component, slot, 2 * TILE : 3 * TILE, :] = displacement[0, component, layer, 0:TILE] * free_next
+        row_modes(nodes, modes, slot, slot, 3 * TILE)
+    first_energy(modes, energy, 2, shares(ratio)(core))
+
+    def whole_layer(target, index, source):
+        target[index, 0:last, :] = bulk[source]
+        target[index, last : rows + TILE, :] = energy[source]
+
+    def node_layer(layer, slot):
+        free = free_of(fixed[layer])
+        for component in range(3):
+            theirs[2 + component, 0:rows, :] = displacement[0, component, layer] * free
+            theirs[2 + component, rows : rows + TILE, :] = nodes[component, slot, TILE : 2 * TILE, :]
+
+    @pl.when(core == 0)
+    def _():
+        whole_layer(mine, 0, 0)
+        whole_layer(mine, 1, 1)
+        whole_layer(theirs, 0, 2)
+        whole_layer(theirs, 1, 2)
+        node_layer(layers - 1, FIRST - 1)
+
+    @pl.when(core == 1)
+    def _():
+        whole_layer(mine, 0, 2)
+        whole_layer(mine, 1, 2)
+        whole_layer(theirs, 0, 0)
+        whole_layer(theirs, 1, 1)
+        node_layer(0, 0)
+
+
+def energy_rest_kernel(count, displacement, fixed, ratio, *refs):
+    firsts, rests = refs[:count], refs[count : 2 * count]
+    mine, theirs, nodes, modes, energy = refs[2 * count :]
     layers, rows, depth = fixed.shape
     wide = rows + TILE
-    half = layers // 2
-    core = lax.axis_index("lc")
-    has_left, has_right = y_flags()
-    for layer in range(layers):
-        free = free_of(fixed[layer])
-        for component in range(3):
-            nodes[component, layer, 0:rows, :] = displacement[0, component, layer] * free
-            at = component * layers + layer
-            nodes[component, layer, rows : rows + SLOT, :] = halos[-1][at] * has_right
-            nodes[component, layer, rows + SLOT : wide, :] = halos[0][at] * has_left
-        row_modes(nodes, modes, layer, layer, wide)
+    core = lax.axis_index("lc")
+    for slot in range(layers - 3):
+        load_nodes(displacement, fixed, firsts, rests, slot + 2, nodes, modes, slot)
     scale = shares(ratio)(core)
     for row in range(0, wide, TILE):
         lower = node_modes(modes, 0, row)
-        for layer in range(layers - 1):
+        for layer in range(layers - 4):
             upper = node_modes(modes, layer + 1, row)
             for part, below, above in zip(parts_of(depth), lower, upper):
                 energy[layer, row : row + TILE, part] = element_energy(below, above, scale)
             lower = upper
-    mine[0 : half - 1] = energy[pl.ds(core * half, half - 1)]
-    theirs[half : half + 3] = nodes[:, (1 - core) * (layers - 1)]
-
-    @pl.when(core == 0)
-    def _():
-        mine[half - 1] = energy[half - 1]
-        theirs[0 : half - 1] = energy[half : layers - 1]
-        theirs[half - 1] = energy[half - 1]
-
-    @pl.when(core == 1)
-    def _():
-        theirs[0:half] = energy[0:half]
-        mine[half - 1] = filled((wide, depth))
+    held = layers // 2 - 2
+    mine[...] = energy[pl.ds(core * held, held)]
+    theirs[...] = energy[pl.ds((1 - core) * held, held)]
+
+
+def crown_kernel(count, displacement, fixed, ratio, *refs):
+    firsts = refs[:count]
+    crown, nodes, modes = refs[count:]
+    layers, rows, depth = fixed.shape
+    wide = rows + TILE
+    core = lax.axis_index("lc")
+    crown[0] = filled((wide, depth))
 
     @pl.when((core == 1) & (lax.axis_index("gz") == lax.axis_size("gz") - 1))
     def _():
+        scale = shares(ratio)(core)
+        load_nodes(displacement, fixed, firsts, None, layers - 1, nodes, modes, 0)
         zero = [filled((TILE, LANES))] * 12
         for row in range(0, wide, TILE):
-            for part, below in zip(parts_of(depth), node_modes(modes, layers - 1, row)):
-                mine[half - 1, row : row + TILE, part] = element_energy(below, zero, scale)
-
-
-def scaling_kernel(count, density, void, beyond, *refs):
+            for part, below in zip(parts_of(depth), node_modes(modes, 0, row)):
+                crown[0, row : row + TILE, part] = element_energy(below, zero, scale)
+
+
+def place(design, slot, middle, left, right, keep=1.0):
+    rows = middle.shape[0]
+    has_left, has_right = y_flags()
+    design[slot, 0:rows, :] = middle * keep
+    design[slot, rows : rows + SLOT, :] = right * (keep * has_right)
+    design[slot, rows + SLOT : rows + TILE, :] = left * (keep * has_left)
+
+
+def scaling_first_kernel(count, density, void, beyond, *refs):
     halos, corners = refs[:count], refs[count : 2 * count]
     scaling, design, sums, halo_alive = refs[2 * count :]
-    layers, rows, depth = density.shape
-    wide = rows + TILE
-    half = layers // 2
-    core = lax.axis_index("lc")
-    has_left, has_right = y_flags()
-    start = core * half
-
+    layers = density.shape[0]
+    core = lax.axis_index("lc")
     has_beyond = beyond_flag()
-
-    def place(slot, middle, left, right, keep=1.0):
-        design[slot, 0:rows, :] = middle * keep
-        design[slot, rows : rows + SLOT, :] = right * (keep * has_right)
-        design[slot, rows + SLOT : wide, :] = left * (keep * has_left)
-
-    for index in range(half + 2):
-        source = index + core * (half - 2)
-        at = 3 * layers + source
-        place(index + 2 * (1 - core), density[source], halos[0][at], halos[-1][at])
+    for index in range(4):
+        source = index + core * (layers - 4)
+        at = 3 * (layers - FIRST) + source
+        place(design, index + 2 * (1 - core), density[source], halos[0][at], halos[-1][at])
     for index in range(2):
         at = 3 + index
-        place(core * (half + 2) + index, beyond[at], corners[0][at], corners[-1][at], has_beyond)
+        place(design, 4 * core + index, beyond[at], corners[0][at], corners[-1][at], has_beyond)
+    scale_layers(core * (layers - 2), void, halos, scaling, design, sums, halo_alive)
+
+
+def scaling_rest_kernel(count, density, void, *refs):
+    halos = refs[:count]
+    scaling, design, sums, halo_alive = refs[count:]
+    layers = density.shape[0]
+    half = layers // 2
+    start = 2 + lax.axis_index("lc") * (half - 2)
+    for index in range(half + 2):
+        source = start - 2 + index
+        at = 3 * (layers - FIRST) + source
+        place(design, index, density[source], halos[0][at], halos[-1][at])
+    scale_layers(start, void, halos, scaling, design, sums, halo_alive)
+
+
+def scale_layers(start, void, halos, scaling, design, sums, halo_alive):
+    layers, rows, depth = void.shape
+    half = scaling.shape[0]
+    wide = rows + TILE
+    has_left, has_right = y_flags()
     for layer in range(half):
-        at = 4 * layers + start + layer
+        at = 3 * (layers - FIRST) + layers + start + layer
         halo_alive[layer, 0:SLOT, :] = halos[-1][at] * has_right
         halo_alive[layer, SLOT:TILE, :] = halos[0][at] * has_left
     row_sums(design, sums, range(half + 4), wide)
@@ -372,10 +487,10 @@
                 scaling[layer, row : row + TILE, part] = value * alive
 
 
-def sensed_kernel(count, scaling, mine, received, ratio, crossed, *refs):
+def sensed_first_kernel(count, scaling, mine, received, ratio, crossed, *refs):
     corners = refs[:count]
     sensed, outgoing, nodes, modes = refs[count:]
-    half, wide, depth = scaling.shape
+    _, wide, depth = scaling.shape
     rows = wide - TILE
     core = lax.axis_index("lc")
     has_left, has_right = y_flags()
@@ -384,7 +499,7 @@
         nodes[component, core, 0:rows, :] = crossed[component] * has_beyond
         nodes[component, core, rows : rows + SLOT, :] = corners[-1][component] * (has_beyond * has_right)
         nodes[component, core, rows + SLOT : wide, :] = corners[0][component] * (has_beyond * has_left)
-        nodes[component, 1 - core] = received[half + component]
+        nodes[component, 1 - core] = received[2 + component]
     for index in range(2):
         row_modes(nodes, modes, index, index, wide)
     scale = shares(ratio)(1 - core)
@@ -393,7 +508,7 @@
         lower, upper = (node_modes(modes, index, row) for index in (0, 1))
         for part, below, above in zip(parts_of(depth), lower, upper):
             outgoing[between, row : row + TILE, part] = element_energy(below, above, scale)
-    for layer in range(half):
+    for layer in range(2):
         sensed[layer] = scaling[layer] * (mine[layer] + received[layer])
 
     @pl.when(core == 0)
@@ -402,12 +517,19 @@
 
     @pl.when(core == 1)
     def _():
-        outgoing[0] = sensed[half - 2]
-        outgoing[2] = scaling[half - 1]
-
-
-def ends_kernel(scaling, mine, outgoing, received, ends):
-    half = scaling.shape[0]
+        outgoing[0] = sensed[0]
+        outgoing[2] = scaling[1]
+
+
+def sensed_rest_kernel(scaling, mine, received, first, sensed):
+    core = lax.axis_index("lc")
+    held = scaling.shape[0]
+    sensed[pl.ds(core * held, 2)] = first[...]
+    for layer in range(held):
+        sensed[2 * (1 - core) + layer] = scaling[layer] * (mine[layer] + received[layer])
+
+
+def ends_kernel(scaling, crown, outgoing, received, ends):
     core = lax.axis_index("lc")
 
     has_beyond = beyond_flag()
@@ -420,7 +542,7 @@
 
     @pl.when(core == 1)
     def _():
-        ends[0] = scaling[half - 1] * ((outgoing[1] + mine[half - 1]) + has_beyond * received[2])
+        ends[0] = scaling[1] * ((outgoing[1] + crown[0]) + has_beyond * received[2])
         ends[1] = has_beyond * received[0]
         ends[2] = has_beyond * received[1]
 
@@ -515,7 +637,7 @@
     wide = rows + TILE
     gz, gy, lc = (lax.axis_size(axis) for axis in ("gz", "gy", "lc"))
     real = jnp.float32
-    smem = pl.BlockSpec(memory_space=pltpu.SMEM)
+    load_ratio = load_ratio.reshape(-1, 1)
     swap = [(0, 1), (1, 0)]
     across = []
     for z in range(1, gz):
@@ -527,17 +649,27 @@
             return [(y, 1 - y) for y in range(gy)]
         return [(y, y + step) for y in range(gy) if 0 <= y + step < gy]
 
-    outermost = [0, gz * lc - 1] if gy % 2 == 0 else []
-
-    def at(place, y):
-        return (place // lc * gy + y) * lc + place % lc
-
-    axes = ("gz", "gy", "lc")
-    swaps = [(at(place, y), at(place, y ^ 1)) for place in outermost for y in range(gy)]
-    crossing = [(at(a, y), at(b, y)) for a, b in across for y in range(gy)] + swaps
+    parts = lax.axis_size("parts")
+    axes = ("parts", "gz", "gy", "lc")
+
+    def at(part, place, y):
+        return ((part * gz + place // lc) * gy + y) * lc + place % lc
+
+    swaps = []
+    if parts % 2 == 0:
+        for part in range(parts):
+            for place in (0, gz * lc - 1):
+                swaps += [(at(part, place, y), at(part ^ 1, place, y)) for y in range(gy)]
+
+    def across_pairs(peers):
+        return [
+            (at(part, a, y), at(part, b, peer)) for part in range(parts) for a, b in across for y, peer in peers
+        ]
+
+    crossing = across_pairs([(y, y) for y in range(gy)]) + swaps
 
     def diagonal(step):
-        pairs = [(at(a, y), at(b, peer)) for a, b in across for y, peer in y_pairs(step)]
+        pairs = across_pairs(y_pairs(step))
         return pairs + swaps if gy == 2 else pairs
 
     sides, steps = (["both"], [1]) if gy == 2 else (["first", "last"], [-1, 1])
@@ -553,7 +685,8 @@
     ]
     crossing_out, *edges = call(
         functools.partial(prepare_kernel, sides),
-        [(5, rows, depth)] + [(5, SLOT, depth)] * count + [(5 * layers, SLOT, depth)] * count,
+        [(5, rows, depth)]
+        + [(size, SLOT, depth) for size in (5, 3 * FIRST, 5 * layers - 3 * FIRST) for _ in sides],
         kinds,
         [hbm()] * 4,
         1 << 18,
@@ -562,30 +695,66 @@
     )(displacement, fixed_mask, density, void_mask)
     crossed = lax.ppermute(crossing_out, axes, crossing)
     corners = [lax.ppermute(a, axes, diagonal(step)) for a, step in zip(edges[:count], steps)][::-1]
-    halos = [lax.ppermute(a, "gy", y_pairs(step)) for a, step in zip(edges[count:], steps)][::-1]
-
-    mine, theirs = call(
-        functools.partial(energy_kernel, count),
-        [(half, wide, depth), (half + 3, wide, depth)],
-        [((3, layers, wide, depth), real), ((layers, 6, wide, depth), real), ((layers, wide, depth), real)],
-        [vmem(), vmem(), smem] + [vmem()] * count,
-        1 << 24,
-    )(displacement, fixed_mask, load_ratio, *halos)
+    halos, rests = (
+        [lax.ppermute(a, "gy", y_pairs(step)) for a, step in zip(packs, steps)][::-1]
+        for packs in (edges[count : 2 * count], edges[2 * count :])
+    )
+
+    def energy(kernel, held, high, low, outs, *more):
+        return call(
+            kernel,
+            outs,
+            [((3, held, high, depth), real), ((held, 6, high, depth), real)] + low,
+            [vmem()] * (3 + len(more)),
+            1 << 23,
+        )(displacement, fixed_mask, load_ratio, *more)
+
+    def scaling(kernel, held, *more):
+        (made,) = call(
+            functools.partial(kernel, count),
+            [(held, wide, depth)],
+            [((held + 4, wide, depth), real), ((held + 4, 2, wide, depth), real), ((held, TILE, depth), real)],
+            [vmem()] * (2 + len(more)),
+            1 << 21,
+        )(density, void_mask, *more)
+        return made
+
+    (bulk,) = energy(energy_bulk_kernel, FIRST, rows, [], [(3, rows - TILE, depth)])
+    mine, theirs = energy(
+        functools.partial(energy_first_kernel, count),
+        FIRST,
+        3 * TILE,
+        [((3, 2 * TILE, depth), real)],
+        [(2, wide, depth), (5, wide, depth)],
+        bulk,
+        *halos,
+    )
     received = lax.ppermute(theirs, "lc", swap)
-    (scaling,) = call(
-        functools.partial(scaling_kernel, count),
-        [(half, wide, depth)],
-        [((half + 4, wide, depth), real), ((half + 4, 2, wide, depth), real), ((half, TILE, depth), real)],
-        [vmem()] * (3 + 2 * count),
+    scaling_rest = scaling(scaling_rest_kernel, half - 2, *rests)
+    mine_rest, theirs_rest = energy(
+        functools.partial(energy_rest_kernel, count),
+        layers - 3,
+        wide,
+        [((layers - 4, wide, depth), real)],
+        [(half - 2, wide, depth), (half - 2, wide, depth)],
+        *halos,
+        *rests,
+    )
+    (crown,) = energy(
+        functools.partial(crown_kernel, count), 1, wide, [], [(1, wide, depth)], *halos
+    )
+    received_rest = lax.ppermute(theirs_rest, "lc", swap)
+    scaling_first = scaling(scaling_first_kernel, 2, crossed, *rests, *corners)
+    first, outgoing = call(
+        functools.partial(sensed_first_kernel, count),
+        [(2, wide, depth), (3, wide, depth)],
+        [((3, 2, wide, depth), real), ((2, 6, wide, depth), real)],
+        [vmem()] * (5 + count),
         1 << 22,
-    )(density, void_mask, crossed, *halos, *corners)
-    sensed, outgoing = call(
-        functools.partial(sensed_kernel, count),
-        [(half, wide, depth), (3, wide, depth)],
-        [((3, 2, wide, depth), real), ((2, 6, wide, depth), real)],
-        [vmem()] * 3 + [smem] + [vmem()] * (1 + count),
-        1 << 22,
-    )(scaling, mine, received, load_ratio, crossed, *corners)
+    )(scaling_first, mine, received, load_ratio, crossed, *corners)
+    (sensed,) = call(sensed_rest_kernel, [(half, wide, depth)], [], [vmem()] * 4, 1 << 18)(
+        scaling_rest, mine_rest, received_rest, first
+    )
     beyond = lax.ppermute(outgoing, axes, crossing)
     other = lax.ppermute(sensed, "lc", swap)
     (inner,) = call(
@@ -596,7 +765,7 @@
         1 << 22,
     )(void_mask, sensed, other)
     (own_ends,) = call(ends_kernel, [(3, wide, depth)], [], [vmem()] * 4, 1 << 18)(
-        scaling, mine, outgoing, beyond
+        scaling_first, crown, outgoing, beyond
     )
     other_ends = lax.ppermute(own_ends, "lc", swap)
     held = [((7, wide, depth), real), ((7, 2, wide, depth), real)]

time: 30.2 us -> 25.8 us (0.85)
  waiting for transfers between devices: 13.3 us -> 8.5 us
  starting transfers between devices: 8.08 us -> 8.96 us
  Pallas kernels: 8.56 us -> 7.92 us
    ppermute x1, waiting for transfers between devices: 5.27 us -> 0.01 us  [shards(): lax.ppermute(a, axes, diagonal(step))]
    ppermute x1 -> x2, starting transfers between devices: 3.04 us -> 4.52 us  [shards(): lax.ppermute(a, 'gy', y_pairs(step))]
    ppermute x1, starting transfers between devices: 2.02 us -> 1.03 us  [shards(): beyond = lax.ppermute(outgoing, axes, crossing)]
    pallas_call x4 -> x9, Pallas kernels: 6.41 us -> 5.77 us  [the longest x4 2.6 us: energy(): call(kernel, outs, [((3, held, high, depth), real), ((held, 6, high, dept...]
    ppermute x1, starting transfers between devices: 0.52 us -> 0.18 us  [shards(): other_ends = lax.ppermute(own_ends, 'lc', swap)]
    ppermute x1, starting transfers between devices: 1.8 us -> 2.11 us  [shards(): crossed = lax.ppermute(crossing_out, axes, crossing)]
    ppermute x1 -> x2, waiting for transfers between devices: 4.2 us -> 4.17 us  [shards(): lax.ppermute(a, 'gy', y_pairs(step))]
  transfers between devices with their start and end apart: 7 -> 9, of which waited for: 4 -> 4; matrix products, arithmetic and copies ran while one was open for 0% -> 0% of each run, Pallas kernels for 7% -> 19%
where the time goes in v5:
time: 25.8 us; the launch traced here: 25.6 us
  starting transfers between devices  8.96 us (35%)
  waiting for transfers between devices  8.5 us (33%)
  Pallas kernels  7.92 us (31%)
    ppermute x2, starting transfers between devices, shards(): lax.ppermute(a, 'gy', y_pairs(step))  4.52 us
    ppermute x2, waiting for transfers between devices, shards(): lax.ppermute(a, 'gy', y_pairs(step))  4.17 us
    ppermute x1, waiting for transfers between devices, shards(): beyond = lax.ppermute(outgoing, axes, crossing)  3.89 us
    pallas_call x4, Pallas kernels, energy(): call(kernel, outs, [((3, held, high, depth), real), ((held, 6, high, dept...  2.6 us
    ppermute x1, starting transfers between devices, shards(): crossed = lax.ppermute(crossing_out, axes, crossing)  2.11 us
    pallas_call x1, Pallas kernels, shards(): call(functools.partial(prepare_kernel, sides), [(5, rows, depth)] + [(siz...  1.45 us
    pallas_call x1, Pallas kernels, shards(): call(far_kernel, [(layers, rows, depth)], held + [((3, rows, depth), real...  1.2 us
    pallas_call x2, Pallas kernels, scaling(): call(functools.partial(kernel, count), [(held, wide, depth)], [((held + 4...  1.2 us
  transfers between devices with their start and end apart: 9, of which 4 were waited for; matrix products, arithmetic and copies ran while one was open for 0% of the time, Pallas kernels for 19%

profile of v5, /device:TPU:0, one launch (start us, length us, event | category | flops | bytes accessed | tf_op | source)
XLA Modules:
  0.0 25.6 jit_solution(7460787042985134012)
XLA Ops:
  0.0 1.4 %shard_map.55 = (f32[5,64,256]{2,1,0:T(8,128)S(1)}, f32[5,4,256]{2,1,0:T(4,128)S(1)}, f32[15,4,256]{2,1,0:T(4,128)S(1)}, f32[25,4,256]{2,1,0:T(4,128)S(1)}) custom-call(f32[1,3,8,64,256]{4,3,2,1,0:T(8,128)} %displacement.9, s32[8,64,256]{2,1,0:T(8,128)} %fixed.9, f32[8,64,256]{2,1,0:T(8,128)} %density.5, s32[8,64,256]{2,1,0:T(8,128)} %void.11), custom_call_target="tpu_custom_call" | custom-call | flops 262144 | bytes 1048576 | tf_op jit(solution)/shard_map/pallas_call | solution.py:686
  1.5 3.0 %collective-permute-start.1 = (f32[15,4,256]{2,1,0:T(4,128)S(1)}, f32[15,4,256]{2,1,0:T(4,128)S(1)}, u32[]{:S(2)}, u32[]{:S(2)}) collective-permute-start(f32[15,4,256]{2,1,0:T(4,128)S(1)} %get-tuple-element.16), channel_id=1, source_target_pairs={{0,2},{2,0},{1,3},{3,1},{4,6},{6,4},{5,7},{7,5},{8,10},{10,8},{9,1... | collective-permute-start | bytes 184328 | tf_op jit(solution)/shard_map/ppermute | solution.py:699
  4.5 0.1 copy.6.ratio
  4.6 0.9 %shard_map.59.bulk = f32[3,56,256]{2,1,0:T(8,128)S(1)} custom-call(f32[1,3,8,64,256]{4,3,2,1,0:T(8,128)S(1)} %copy-done, s32[8,64,256]{2,1,0:T(8,128)S(1)} %copy-done.2, s32[2,1]{1,0:T(2,128)S(1)} %copy.6.ratio), custom_call_target="tpu_custom_call" | custom-call | flops 8388608 | bytes 1048576 | tf_op jit(solution)/shard_map/pallas_call | solution.py:704
  5.5 1.2 %collective-permute-done.1.refs_0_ = f32[15,4,256]{2,1,0:T(4,128)S(1)} collective-permute-done((f32[15,4,256]{2,1,0:T(4,128)S(1)}, f32[15,4,256]{2,1,0:T(4,128)S(1)}, u32[]{:S(2)}, u32[]{:S(2)}) %collective-permute-start.1) | collective-permute-done | bytes 61472 | tf_op jit(solution)/shard_map/ppermute | solution.py:699
  6.7 0.3 %shard_map.60 = (f32[2,72,256]{2,1,0:T(8,128)S(1)}, f32[5,72,256]{2,1,0:T(8,128)S(1)}) custom-call(f32[1,3,8,64,256]{4,3,2,1,0:T(8,128)S(1)} %copy-done, s32[8,64,256]{2,1,0:T(8,128)S(1)} %copy-done.2, s32[2,1]{1,0:T(2,128)S(1)} %copy.6.ratio, f32[3,56,256]{2,1,0:T(8,128)S(1)} %shard_map.59.bulk, f32[15,4,256]{2,1,0:T(4,128)S(1)} %collective-permute-done.1.refs_0_), custom_call_target="tpu_custom_call" | custom-call | flops 8388608 | bytes 1048576 | tf_op jit(solution)/shard_map/pallas_call | solution.py:704
  7.0 0.1 collective-permute-start.5
  7.1 2.1 %collective-permute-start.3 = (f32[5,64,256]{2,1,0:T(8,128)S(1)}, f32[5,64,256]{2,1,0:T(8,128)S(1)}, u32[]{:S(2)}, u32[]{:S(2)}) collective-permute-start(f32[5,64,256]{2,1,0:T(8,128)S(1)} %get-tuple-element.19), channel_id=1, source_target_pairs={{4,1},{6,3},{1,4},{3,6},{8,5},{10,7},{5,8},{7,10},{12,9},{14,11},{... | collective-permute-start | bytes 983048 | tf_op jit(solution)/shard_map/ppermute | solution.py:696
  9.2 1.5 %collective-permute-start = (f32[25,4,256]{2,1,0:T(4,128)S(1)}, f32[25,4,256]{2,1,0:T(4,128)S(1)}, u32[]{:S(2)}, u32[]{:S(2)}) collective-permute-start(f32[25,4,256]{2,1,0:T(4,128)S(1)} %get-tuple-element.15), channel_id=1, source_target_pairs={{0,2},{2,0},{1,3},{3,1},{4,6},{6,4},{5,7},{7,5},{8,10},{10,8},{9,1... | collective-permute-start | bytes 307208 | tf_op jit(solution)/shard_map/ppermute | solution.py:699
  10.7 0.5 %collective-permute-start.4 = (f32[5,4,256]{2,1,0:T(4,128)S(1)}, f32[5,4,256]{2,1,0:T(4,128)S(1)}, u32[]{:S(2)}, u32[]{:S(2)}) collective-permute-start(f32[5,4,256]{2,1,0:T(4,128)S(1)} %get-tuple-element.20), channel_id=1, source_target_pairs={{4,3},{6,1},{1,6},{3,4},{8,7},{10,5},{5,10},{7,8},{12,11},{14,9},{... | collective-permute-start | bytes 61448 | tf_op jit(solution)/shard_map/ppermute | solution.py:697
  11.2 3.0 %collective-permute-done.refs_0_.refs_1_ = f32[25,4,256]{2,1,0:T(4,128)S(1)} collective-permute-done((f32[25,4,256]{2,1,0:T(4,128)S(1)}, f32[25,4,256]{2,1,0:T(4,128)S(1)}, u32[]{:S(2)}, u32[]{:S(2)}) %collective-permute-start) | collective-permute-done | bytes 102432 | tf_op jit(solution)/shard_map/ppermute | solution.py:699
  14.2 1.4 %shard_map.57 = (f32[2,72,256]{2,1,0:T(8,128)S(1)}, f32[2,72,256]{2,1,0:T(8,128)S(1)}) custom-call(f32[1,3,8,64,256]{4,3,2,1,0:T(8,128)S(1)} %copy-done, s32[8,64,256]{2,1,0:T(8,128)S(1)} %copy-done.2, s32[2,1]{1,0:T(2,128)S(1)} %copy.6.ratio, f32[15,4,256]{2,1,0:T(4,128)S(1)} %collective-permute-done.1.refs_0_, ...), custom_call_target="tpu_custom_call" | custom-call | flops 8388608 | bytes 1048576 | tf_op jit(solution)/shard_map/pallas_call | solution.py:704
  15.6 0.1 collective-permute-start.2
  15.7 0.6 %shard_map.58.scaling = f32[2,72,256]{2,1,0:T(8,128)S(1)} custom-call(f32[8,64,256]{2,1,0:T(8,128)S(1)} %copy-done.3, s32[8,64,256]{2,1,0:T(8,128)S(1)} %copy-done.1, f32[5,64,256]{2,1,0:T(8,128)S(1)} %collective-permute-done.3.beyond.crossed, f32[25,4,256]{2,1,0:T(4,128)S(1)} %collective-permute-done.refs_0_.refs_1_, ...), custom_call_target="tpu_custom_call" | custom-call | flops 2097152 | bytes 1048576 | tf_op jit(solution)/shard_map/pallas_call | solution.py:713
  16.4 0.5 %shard_map.61 = (f32[2,72,256]{2,1,0:T(8,128)S(1)}, f32[3,72,256]{2,1,0:T(8,128)S(1)}) custom-call(f32[2,72,256]{2,1,0:T(8,128)S(1)} %shard_map.58.scaling, f32[2,72,256]{2,1,0:T(8,128)S(1)} %get-tuple-element.21.mine, f32[5,72,256]{2,1,0:T(8,128)S(1)} %collective-permute-done.5.received, s32[2,1]{1,0:T(2,128)S(1)} %copy.6.ratio, ...), custom_call_target="tpu_custom_call" | custom-call | flops 4194304 | bytes 1048576 | tf_op jit(solution)/shard_map/pallas_call | solution.py:748
  16.9 1.0 %collective-permute-start.7 = (f32[3,72,256]{2,1,0:T(8,128)S(1)}, f32[3,72,256]{2,1,0:T(8,128)S(1)}, u32[]{:S(2)}, u32[]{:S(2)}) collective-permute-start(f32[3,72,256]{2,1,0:T(8,128)S(1)} %get-tuple-element.24.outgoing), channel_id=1, source_target_pairs={{4,1},{6,3},{1,4},{3,6},{8,5},{10,7},{5,8},{7,10},{12,9},{14,11},{... | collective-permute-start | bytes 663560 | tf_op jit(solution)/shard_map/ppermute | solution.py:758
  17.9 0.6 %shard_map.56.scaling = f32[2,72,256]{2,1,0:T(8,128)S(1)} custom-call(f32[8,64,256]{2,1,0:T(8,128)S(1)} %copy-done.3, s32[8,64,256]{2,1,0:T(8,128)S(1)} %copy-done.1, f32[25,4,256]{2,1,0:T(4,128)S(1)} %collective-permute-done.refs_0_.refs_1_), custom_call_target="tpu_custom_call" | custom-call | flops 2097152 | bytes 1048576 | tf_op jit(solution)/shard_map/pallas_call | solution.py:713
  18.5 0.5 %collective-permute-start.6 = (f32[4,72,256]{2,1,0:T(8,128)S(1)}, f32[4,72,256]{2,1,0:T(8,128)S(1)}, u32[]{:S(2)}, u32[]{:S(2)}) collective-permute-start(f32[4,72,256]{2,1,0:T(8,128)S(1)} %shard_map.62.own), channel_id=1, source_target_pairs={{0,1},{1,0},{2,3},{3,2},{4,5},{5,4},{6,7},{7,6},{8,9},{9,8},{10,11... | collective-permute-start | bytes 884744 | tf_op jit(solution)/shard_map/ppermute | solution.py:759
  19.0 3.9 %collective-permute-done.7.received = f32[3,72,256]{2,1,0:T(8,128)S(1)} collective-permute-done((f32[3,72,256]{2,1,0:T(8,128)S(1)}, f32[3,72,256]{2,1,0:T(8,128)S(1)}, u32[]{:S(2)}, u32[]{:S(2)}) %collective-permute-start.7) | collective-permute-done | bytes 221216 | tf_op jit(solution)/shard_map/ppermute | solution.py:758
  22.9 0.2 collective-permute-start.8
  23.1 0.5 %shard_map.66.near = f32[3,64,256]{2,1,0:T(8,128)S(1)} custom-call(s32[8,64,256]{2,1,0:T(8,128)S(1)} %copy-done.1, f32[4,72,256]{2,1,0:T(8,128)S(1)} %shard_map.62.own, f32[4,72,256]{2,1,0:T(8,128)S(1)} %collective-permute-done.6.other, f32[3,72,256]{2,1,0:T(8,128)S(1)} %shard_map.64.ends), custom_call_target="tpu_custom_call" | custom-call | flops 2097152 | bytes 1048576 | tf_op jit(solution)/shard_map/pallas_call | solution.py:772
  23.6 0.4 %shard_map.65.inner = f32[2,64,256]{2,1,0:T(8,128)S(1)} custom-call(s32[8,64,256]{2,1,0:T(8,128)S(1)} %copy-done.1, f32[4,72,256]{2,1,0:T(8,128)S(1)} %shard_map.62.own, f32[4,72,256]{2,1,0:T(8,128)S(1)} %collective-permute-done.6.other), custom_call_target="tpu_custom_call" | custom-call | flops 4194304 | bytes 1048576 | tf_op jit(solution)/shard_map/pallas_call | solution.py:760
  24.0 0.4 %collective-permute-done.8.ends = f32[3,72,256]{2,1,0:T(8,128)S(1)} collective-permute-done((f32[3,72,256]{2,1,0:T(8,128)S(1)}, f32[3,72,256]{2,1,0:T(8,128)S(1)}, u32[]{:S(2)}, u32[]{:S(2)}) %collective-permute-start.8) | collective-permute-done | bytes 221216 | tf_op jit(solution)/shard_map/ppermute | solution.py:770
  24.4 1.2 %shard_map.67 = f32[8,64,256]{2,1,0:T(8,128)} custom-call(s32[8,64,256]{2,1,0:T(8,128)S(1)} %copy-done.1, f32[4,72,256]{2,1,0:T(8,128)S(1)} %shard_map.62.own, f32[4,72,256]{2,1,0:T(8,128)S(1)} %collective-permute-done.6.other, f32[3,72,256]{2,1,0:T(8,128)S(1)} %collective-permute-done.8.ends, f32[2,64,256]{2,1,0:T(8,128)S(1)} %shard_map.65.inner, ...), custom_call_target="tpu_custom_call" | custom-call | flops 2097152 | bytes 1048576 | tf_op jit(solution)/shard_map/pallas_call | solution.py:775
  (18 shorter events, 0.1 us)
Async XLA Ops:
  0.0 4.6 %copy-start.2 = (s32[8,64,256]{2,1,0:T(8,128)S(1)}, s32[8,64,256]{2,1,0:T(8,128)}, u32[]{:S(2)}) copy-start(s32[8,64,256]{2,1,0:T(8,128)} %fixed.9) | copy-start | bytes 1572868
  0.0 4.6 %copy-start = (f32[1,3,8,64,256]{4,3,2,1,0:T(8,128)S(1)}, f32[1,3,8,64,256]{4,3,2,1,0:T(8,128)}, u32[]{:S(2)}) copy-start(f32[1,3,8,64,256]{4,3,2,1,0:T(8,128)} %displacement.9) | copy-start | bytes 4718596
  0.0 4.5 %copy-start.4 = (s32[2]{0:T(128)S(1)}, s32[2]{0:T(128)}, u32[]{:S(2)}) copy-start(s32[2]{0:T(128)} %param.9) | copy-start | bytes 28
  1.5 5.2 %collective-permute-start.1 = (f32[15,4,256]{2,1,0:T(4,128)S(1)}, f32[15,4,256]{2,1,0:T(4,128)S(1)}, u32[]{:S(2)}, u32[]{:S(2)}) collective-permute-start(f32[15,4,256]{2,1,0:T(4,128)S(1)} %get-tuple-element.16), channel_id=1, source_target_pairs={{0,2},{2,0},{1,3},{3,1},{4,6},{6,4},{5,7},{7,5},{8,10},{10,8},{9,1... | collective-permute-start | bytes 184328 | tf_op jit(solution)/shard_map/ppermute | solution.py:699
  7.0 8.7 %copy-start.1 = (s32[8,64,256]{2,1,0:T(8,128)S(1)}, s32[8,64,256]{2,1,0:T(8,128)}, u32[]{:S(2)}) copy-start(s32[8,64,256]{2,1,0:T(8,128)} %void.11) | copy-start | bytes 1572868
  7.0 8.7 %copy-start.3 = (f32[8,64,256]{2,1,0:T(8,128)S(1)}, f32[8,64,256]{2,1,0:T(8,128)}, u32[]{:S(2)}) copy-start(f32[8,64,256]{2,1,0:T(8,128)} %density.5) | copy-start | bytes 1572868
  7.0 9.3 %collective-permute-start.5 = (f32[5,72,256]{2,1,0:T(8,128)S(1)}, f32[5,72,256]{2,1,0:T(8,128)S(1)}, u32[]{:S(2)}, u32[]{:S(2)}) collective-permute-start(f32[5,72,256]{2,1,0:T(8,128)S(1)} %get-tuple-element.22), channel_id=1, source_target_pairs={{0,1},{1,0},{2,3},{3,2},{4,5},{5,4},{6,7},{7,6},{8,9},{9,8},{10,11... | collective-permute-start | bytes 1105928 | tf_op jit(solution)/shard_map/ppermute | solution.py:732
  7.1 8.6 %collective-permute-start.3 = (f32[5,64,256]{2,1,0:T(8,128)S(1)}, f32[5,64,256]{2,1,0:T(8,128)S(1)}, u32[]{:S(2)}, u32[]{:S(2)}) collective-permute-start(f32[5,64,256]{2,1,0:T(8,128)S(1)} %get-tuple-element.19), channel_id=1, source_target_pairs={{4,1},{6,3},{1,4},{3,6},{8,5},{10,7},{5,8},{7,10},{12,9},{14,11},{... | collective-permute-start | bytes 983048 | tf_op jit(solution)/shard_map/ppermute | solution.py:696
  9.2 5.0 %collective-permute-start = (f32[25,4,256]{2,1,0:T(4,128)S(1)}, f32[25,4,256]{2,1,0:T(4,128)S(1)}, u32[]{:S(2)}, u32[]{:S(2)}) collective-permute-start(f32[25,4,256]{2,1,0:T(4,128)S(1)} %get-tuple-element.15), channel_id=1, source_target_pairs={{0,2},{2,0},{1,3},{3,1},{4,6},{6,4},{5,7},{7,5},{8,10},{10,8},{9,1... | collective-permute-start | bytes 307208 | tf_op jit(solution)/shard_map/ppermute | solution.py:699
  10.7 4.9 %collective-permute-start.4 = (f32[5,4,256]{2,1,0:T(4,128)S(1)}, f32[5,4,256]{2,1,0:T(4,128)S(1)}, u32[]{:S(2)}, u32[]{:S(2)}) collective-permute-start(f32[5,4,256]{2,1,0:T(4,128)S(1)} %get-tuple-element.20), channel_id=1, source_target_pairs={{4,3},{6,1},{1,6},{3,4},{8,7},{10,5},{5,10},{7,8},{12,11},{14,9},{... | collective-permute-start | bytes 61448 | tf_op jit(solution)/shard_map/ppermute | solution.py:697
  15.6 2.9 %collective-permute-start.2 = (f32[2,72,256]{2,1,0:T(8,128)S(1)}, f32[2,72,256]{2,1,0:T(8,128)S(1)}, u32[]{:S(2)}, u32[]{:S(2)}) collective-permute-start(f32[2,72,256]{2,1,0:T(8,128)S(1)} %get-tuple-element.18), channel_id=1, source_target_pairs={{0,1},{1,0},{2,3},{3,2},{4,5},{5,4},{6,7},{7,6},{8,9},{9,8},{10,11... | collective-permute-start | bytes 442376 | tf_op jit(solution)/shard_map/ppermute | solution.py:746
  16.9 6.0 %collective-permute-start.7 = (f32[3,72,256]{2,1,0:T(8,128)S(1)}, f32[3,72,256]{2,1,0:T(8,128)S(1)}, u32[]{:S(2)}, u32[]{:S(2)}) collective-permute-start(f32[3,72,256]{2,1,0:T(8,128)S(1)} %get-tuple-element.24.outgoing), channel_id=1, source_target_pairs={{4,1},{6,3},{1,4},{3,6},{8,5},{10,7},{5,8},{7,10},{12,9},{14,11},{... | collective-permute-start | bytes 663560 | tf_op jit(solution)/shard_map/ppermute | solution.py:758
  18.5 4.6 %collective-permute-start.6 = (f32[4,72,256]{2,1,0:T(8,128)S(1)}, f32[4,72,256]{2,1,0:T(8,128)S(1)}, u32[]{:S(2)}, u32[]{:S(2)}) collective-permute-start(f32[4,72,256]{2,1,0:T(8,128)S(1)} %shard_map.62.own), channel_id=1, source_target_pairs={{0,1},{1,0},{2,3},{3,2},{4,5},{5,4},{6,7},{7,6},{8,9},{9,8},{10,11... | collective-permute-start | bytes 884744 | tf_op jit(solution)/shard_map/ppermute | solution.py:759
  22.9 1.5 %collective-permute-start.8 = (f32[3,72,256]{2,1,0:T(8,128)S(1)}, f32[3,72,256]{2,1,0:T(8,128)S(1)}, u32[]{:S(2)}, u32[]{:S(2)}) collective-permute-start(f32[3,72,256]{2,1,0:T(8,128)S(1)} %shard_map.64.ends), channel_id=1, source_target_pairs={{0,1},{1,0},{2,3},{3,2},{4,5},{5,4},{6,7},{7,6},{8,9},{9,8},{10,11... | collective-permute-start | bytes 663560 | tf_op jit(solution)/shard_map/ppermute | solution.py:770

commit v6 on v5

--- a/solution.py
+++ b/solution.py
@@ -352,7 +352,7 @@
 
 def energy_rest_kernel(count, displacement, fixed, ratio, *refs):
     firsts, rests = refs[:count], refs[count : 2 * count]
-    mine, theirs, nodes, modes, energy = refs[2 * count :]
+    energy, nodes, modes = refs[2 * count :]
     layers, rows, depth = fixed.shape
     wide = rows + TILE
     core = lax.axis_index("lc")
@@ -366,9 +366,6 @@
             for part, below, above in zip(parts_of(depth), lower, upper):
                 energy[layer, row : row + TILE, part] = element_energy(below, above, scale)
             lower = upper
-    held = layers // 2 - 2
-    mine[...] = energy[pl.ds(core * held, held)]
-    theirs[...] = energy[pl.ds((1 - core) * held, held)]
 
 
 def crown_kernel(count, displacement, fixed, ratio, *refs):
@@ -417,13 +414,10 @@
     halos = refs[:count]
     scaling, design, sums, halo_alive = refs[count:]
     layers = density.shape[0]
-    half = layers // 2
-    start = 2 + lax.axis_index("lc") * (half - 2)
-    for index in range(half + 2):
-        source = start - 2 + index
-        at = 3 * (layers - FIRST) + source
-        place(design, index, density[source], halos[0][at], halos[-1][at])
-    scale_layers(start, void, halos, scaling, design, sums, halo_alive)
+    for layer in range(layers):
+        at = 3 * (layers - FIRST) + layer
+        place(design, layer, density[layer], halos[0][at], halos[-1][at])
+    scale_layers(2, void, halos, scaling, design, sums, halo_alive)
 
 
 def scale_layers(start, void, halos, scaling, design, sums, halo_alive):
@@ -521,12 +515,9 @@
         outgoing[2] = scaling[1]
 
 
-def sensed_rest_kernel(scaling, mine, received, first, sensed):
-    core = lax.axis_index("lc")
-    held = scaling.shape[0]
-    sensed[pl.ds(core * held, 2)] = first[...]
-    for layer in range(held):
-        sensed[2 * (1 - core) + layer] = scaling[layer] * (mine[layer] + received[layer])
+def sensed_rest_kernel(scaling, mine, received, sensed):
+    for layer in range(scaling.shape[0]):
+        sensed[layer] = scaling[layer] * (mine[layer] + received[layer])
 
 
 def ends_kernel(scaling, crown, outgoing, received, ends):
@@ -547,12 +538,12 @@
         ends[2] = has_beyond * received[1]
 
 
-def inner_kernel(void, own, other, gradient, field, sums):
+def inner_kernel(void, own, other, middle, gradient, field, sums):
     layers, rows, depth = void.shape
-    half = layers // 2
-    core = lax.axis_index("lc")
-    field[pl.ds(core * half, half)] = own[...]
-    field[pl.ds((1 - core) * half, half)] = other[...]
+    core = lax.axis_index("lc")
+    field[pl.ds(core * (layers - 2), 2)] = own[...]
+    field[pl.ds((1 - core) * (layers - 2), 2)] = other[...]
+    field[2 : layers - 2] = middle[...]
     row_sums(field, sums, range(1, layers - 1), rows + TILE)
     for row in range(0, rows, TILE):
         for layer in range(3, layers - 3):
@@ -562,20 +553,20 @@
                 gradient[layer - 3, row : row + TILE, part] = alive * value
 
 
-def side_rows(side, void, own, other, ends, result, field, sums):
+def side_rows(side, void, first, middle, ends, result, field, sums):
     layers, rows, depth = void.shape
-    half = own.shape[0]
+    held = middle.shape[0]
 
     @pl.when(side == 0)
     def _():
         field[0:2] = ends[0:2]
-        field[2:6] = own[0:4]
-        field[6] = own[4] if half > 4 else other[0]
+        field[2:4] = first[...]
+        field[4:7] = middle[0:3]
 
     @pl.when(side == 1)
     def _():
-        field[0] = own[half - 5] if half > 4 else other[half - 1]
-        field[1:4] = own[half - 4 : half - 1]
+        field[0:3] = middle[held - 3 : held]
+        field[3] = first[0]
         field[4:7] = ends[...]
 
     row_sums(field, sums, range(7), rows + TILE)
@@ -588,11 +579,11 @@
                 result[layer, row : row + TILE, part] = alive * value
 
 
-def near_kernel(void, own, other, ends, result, field, sums):
-    side_rows(lax.axis_index("lc"), void, own, other, ends, result, field, sums)
-
-
-def far_kernel(void, own, other, ends, inner, near, gradient, field, sums, far, sems):
+def near_kernel(void, first, middle, ends, result, field, sums):
+    side_rows(lax.axis_index("lc"), void, first, middle, ends, result, field, sums)
+
+
+def far_kernel(void, first, middle, ends, inner, near, gradient, field, sums, far, sems):
     layers = void.shape[0]
     core = lax.axis_index("lc")
     copies = [
@@ -602,7 +593,7 @@
     ]
     for copy in copies[:2]:
         copy.start()
-    side_rows(1 - core, void, other, own, ends, far, field, sums)
+    side_rows(1 - core, void, first, middle, ends, far, field, sums)
     copies[2].start()
     for copy in copies:
         copy.wait()
@@ -633,7 +624,6 @@
 
 def shards(density, void_mask, fixed_mask, displacement, load_ratio):
     layers, rows, depth = density.shape
-    half = layers // 2
     wide = rows + TILE
     gz, gy, lc = (lax.axis_size(axis) for axis in ("gz", "gy", "lc"))
     real = jnp.float32
@@ -730,20 +720,20 @@
         *halos,
     )
     received = lax.ppermute(theirs, "lc", swap)
-    scaling_rest = scaling(scaling_rest_kernel, half - 2, *rests)
-    mine_rest, theirs_rest = energy(
+    scaling_rest = scaling(scaling_rest_kernel, layers - 4, *rests)
+    (mine_rest,) = energy(
         functools.partial(energy_rest_kernel, count),
         layers - 3,
         wide,
-        [((layers - 4, wide, depth), real)],
-        [(half - 2, wide, depth), (half - 2, wide, depth)],
+        [],
+        [(layers - 4, wide, depth)],
         *halos,
         *rests,
     )
     (crown,) = energy(
         functools.partial(crown_kernel, count), 1, wide, [], [(1, wide, depth)], *halos
     )
-    received_rest = lax.ppermute(theirs_rest, "lc", swap)
+    received_rest = lax.ppermute(mine_rest, "lc", swap)
     scaling_first = scaling(scaling_first_kernel, 2, crossed, *rests, *corners)
     first, outgoing = call(
         functools.partial(sensed_first_kernel, count),
@@ -752,25 +742,25 @@
         [vmem()] * (5 + count),
         1 << 22,
     )(scaling_first, mine, received, load_ratio, crossed, *corners)
-    (sensed,) = call(sensed_rest_kernel, [(half, wide, depth)], [], [vmem()] * 4, 1 << 18)(
-        scaling_rest, mine_rest, received_rest, first
-    )
+    (middle,) = call(
+        sensed_rest_kernel, [(layers - 4, wide, depth)], [], [vmem()] * 3, 1 << 18
+    )(scaling_rest, mine_rest, received_rest)
     beyond = lax.ppermute(outgoing, axes, crossing)
-    other = lax.ppermute(sensed, "lc", swap)
+    other = lax.ppermute(first, "lc", swap)
     (inner,) = call(
         inner_kernel,
         [(layers - 6, rows, depth)],
         [((layers, wide, depth), real), ((layers, 2, wide, depth), real)],
-        [vmem()] * 3,
+        [vmem()] * 4,
         1 << 22,
-    )(void_mask, sensed, other)
+    )(void_mask, first, other, middle)
     (own_ends,) = call(ends_kernel, [(3, wide, depth)], [], [vmem()] * 4, 1 << 18)(
         scaling_first, crown, outgoing, beyond
     )
     other_ends = lax.ppermute(own_ends, "lc", swap)
     held = [((7, wide, depth), real), ((7, 2, wide, depth), real)]
     (near,) = call(near_kernel, [(3, rows, depth)], held, [vmem()] * 4, 1 << 21)(
-        void_mask, sensed, other, own_ends
+        void_mask, first, middle, own_ends
     )
     (gradient,) = call(
         far_kernel,
@@ -780,7 +770,7 @@
         1 << 21,
         out_specs=[hbm()],
         sems=3,
-    )(void_mask, sensed, other, other_ends, inner, near)
+    )(void_mask, other, middle, other_ends, inner, near)
     return gradient
 
 

time: 25.8 us -> 26.1 us (1.012)
  waiting for transfers between devices: 8.5 us -> 6.74 us
  starting transfers between devices: 8.96 us -> 10.7 us
  Pallas kernels: 7.92 us -> 8.26 us
    ppermute x1, waiting for transfers between devices: 0.01 us -> 3.28 us  [shards(): lax.ppermute(a, axes, diagonal(step))]
    ppermute x2, waiting for transfers between devices: 4.17 us -> 1.19 us  [shards(): lax.ppermute(a, 'gy', y_pairs(step))]
    ppermute x1, waiting for transfers between devices: 3.89 us -> 1.97 us  [shards(): beyond = lax.ppermute(outgoing, axes, crossing)]
    ppermute x1, starting transfers between devices: 1.03 us -> 2.08 us  [shards(): beyond = lax.ppermute(outgoing, axes, crossing)]
    ppermute x1, starting transfers between devices: 0.18 us -> 0.77 us  [shards(): other_ends = lax.ppermute(own_ends, 'lc', swap)]
    ppermute x1, waiting for transfers between devices: 0.42 us -> 0.01 us  [shards(): other_ends = lax.ppermute(own_ends, 'lc', swap)]
    pallas_call x2, Pallas kernels: 1.2 us -> 1.57 us  [scaling(): call(functools.partial(kernel, count), [(held, wide, depth)], [((held + 4...]
    ppermute x2, waiting for transfers between devices: 0.01 us -> 0.3 us  [the longest x1 0.29 us: shards(): other = lax.ppermute(first, 'lc', swap)]
  transfers between devices with their start and end apart: 9 -> 9, of which waited for: 4 -> 4; matrix products, arithmetic and copies ran while one was open for 0% -> 0% of each run, Pallas kernels for 19% -> 18%
where the time goes in v6:
time: 26.1 us; the launch traced here: 26 us
  starting transfers between devices  10.7 us (41%)
  Pallas kernels  8.26 us (32%)
  waiting for transfers between devices  6.74 us (26%)
    ppermute x2, starting transfers between devices, shards(): lax.ppermute(a, 'gy', y_pairs(step))  4.52 us
    ppermute x1, waiting for transfers between devices, shards(): lax.ppermute(a, axes, diagonal(step))  3.28 us
    pallas_call x4, Pallas kernels, energy(): call(kernel, outs, [((3, held, high, depth), real), ((held, 6, high, dept...  2.55 us
    ppermute x1, starting transfers between devices, shards(): crossed = lax.ppermute(crossing_out, axes, crossing)  2.11 us
    ppermute x1, starting transfers between devices, shards(): beyond = lax.ppermute(outgoing, axes, crossing)  2.08 us
    ppermute x1, waiting for transfers between devices, shards(): beyond = lax.ppermute(outgoing, axes, crossing)  1.97 us
    pallas_call x2, Pallas kernels, scaling(): call(functools.partial(kernel, count), [(held, wide, depth)], [((held + 4...  1.57 us
    pallas_call x1, Pallas kernels, shards(): call(functools.partial(prepare_kernel, sides), [(5, rows, depth)] + [(siz...  1.45 us
  transfers between devices with their start and end apart: 9, of which 4 were waited for; matrix products, arithmetic and copies ran while one was open for 0% of the time, Pallas kernels for 18%

profile of v6, /device:TPU:0, one launch (start us, length us, event | category | flops | bytes accessed | tf_op | source)
XLA Modules:
  0.0 26.0 jit_solution(18180712360802979513)
XLA Ops:
  0.0 1.4 %shard_map.55 = (f32[5,64,256]{2,1,0:T(8,128)S(1)}, f32[5,4,256]{2,1,0:T(4,128)S(1)}, f32[15,4,256]{2,1,0:T(4,128)S(1)}, f32[25,4,256]{2,1,0:T(4,128)S(1)}) custom-call(f32[1,3,8,64,256]{4,3,2,1,0:T(8,128)} %displacement.9, s32[8,64,256]{2,1,0:T(8,128)} %fixed.9, f32[8,64,256]{2,1,0:T(8,128)} %density.5, s32[8,64,256]{2,1,0:T(8,128)} %void.11), custom_call_target="tpu_custom_call" | custom-call | flops 262144 | bytes 1048576 | tf_op jit(solution)/shard_map/pallas_call | solution.py:676
  1.5 3.0 %collective-permute-start.3 = (f32[15,4,256]{2,1,0:T(4,128)S(1)}, f32[15,4,256]{2,1,0:T(4,128)S(1)}, u32[]{:S(2)}, u32[]{:S(2)}) collective-permute-start(f32[15,4,256]{2,1,0:T(4,128)S(1)} %get-tuple-element.16), channel_id=1, source_target_pairs={{0,2},{2,0},{1,3},{3,1},{4,6},{6,4},{5,7},{7,5},{8,10},{10,8},{9,1... | collective-permute-start | bytes 184328 | tf_op jit(solution)/shard_map/ppermute | solution.py:689
  4.5 0.1 copy.7.ratio
  4.6 0.9 %shard_map.57.bulk = f32[3,56,256]{2,1,0:T(8,128)S(1)} custom-call(f32[1,3,8,64,256]{4,3,2,1,0:T(8,128)S(1)} %copy-done, s32[8,64,256]{2,1,0:T(8,128)S(1)} %copy-done.2, s32[2,1]{1,0:T(2,128)S(1)} %copy.7.ratio), custom_call_target="tpu_custom_call" | custom-call | flops 8388608 | bytes 1048576 | tf_op jit(solution)/shard_map/pallas_call | solution.py:694
  5.5 1.2 %collective-permute-done.3.refs_0_ = f32[15,4,256]{2,1,0:T(4,128)S(1)} collective-permute-done((f32[15,4,256]{2,1,0:T(4,128)S(1)}, f32[15,4,256]{2,1,0:T(4,128)S(1)}, u32[]{:S(2)}, u32[]{:S(2)}) %collective-permute-start.3) | collective-permute-done | bytes 61472 | tf_op jit(solution)/shard_map/ppermute | solution.py:689
  6.7 0.3 %shard_map.58 = (f32[2,72,256]{2,1,0:T(8,128)S(1)}, f32[5,72,256]{2,1,0:T(8,128)S(1)}) custom-call(f32[1,3,8,64,256]{4,3,2,1,0:T(8,128)S(1)} %copy-done, s32[8,64,256]{2,1,0:T(8,128)S(1)} %copy-done.2, s32[2,1]{1,0:T(2,128)S(1)} %copy.7.ratio, f32[3,56,256]{2,1,0:T(8,128)S(1)} %shard_map.57.bulk, f32[15,4,256]{2,1,0:T(4,128)S(1)} %collective-permute-done.3.refs_0_), custom_call_target="tpu_custom_call" | custom-call | flops 8388608 | bytes 1048576 | tf_op jit(solution)/shard_map/pallas_call | solution.py:694
  7.0 0.1 collective-permute-start.4
  7.1 2.1 %collective-permute-start = (f32[5,64,256]{2,1,0:T(8,128)S(1)}, f32[5,64,256]{2,1,0:T(8,128)S(1)}, u32[]{:S(2)}, u32[]{:S(2)}) collective-permute-start(f32[5,64,256]{2,1,0:T(8,128)S(1)} %get-tuple-element.13), channel_id=1, source_target_pairs={{4,1},{6,3},{1,4},{3,6},{8,5},{10,7},{5,8},{7,10},{12,9},{14,11},{... | collective-permute-start | bytes 983048 | tf_op jit(solution)/shard_map/ppermute | solution.py:686
  9.2 1.5 %collective-permute-start.1 = (f32[25,4,256]{2,1,0:T(4,128)S(1)}, f32[25,4,256]{2,1,0:T(4,128)S(1)}, u32[]{:S(2)}, u32[]{:S(2)}) collective-permute-start(f32[25,4,256]{2,1,0:T(4,128)S(1)} %get-tuple-element.14), channel_id=1, source_target_pairs={{0,2},{2,0},{1,3},{3,1},{4,6},{6,4},{5,7},{7,5},{8,10},{10,8},{9,1... | collective-permute-start | bytes 307208 | tf_op jit(solution)/shard_map/ppermute | solution.py:689
  10.7 0.5 %collective-permute-start.2 = (f32[5,4,256]{2,1,0:T(4,128)S(1)}, f32[5,4,256]{2,1,0:T(4,128)S(1)}, u32[]{:S(2)}, u32[]{:S(2)}) collective-permute-start(f32[5,4,256]{2,1,0:T(4,128)S(1)} %get-tuple-element.15), channel_id=1, source_target_pairs={{4,3},{6,1},{1,6},{3,4},{8,7},{10,5},{5,10},{7,8},{12,11},{14,9},{... | collective-permute-start | bytes 61448 | tf_op jit(solution)/shard_map/ppermute | solution.py:687
  11.2 3.3 %collective-permute-done.2.refs_1_.refs_0_ = f32[5,4,256]{2,1,0:T(4,128)S(1)} collective-permute-done((f32[5,4,256]{2,1,0:T(4,128)S(1)}, f32[5,4,256]{2,1,0:T(4,128)S(1)}, u32[]{:S(2)}, u32[]{:S(2)}) %collective-permute-start.2) | collective-permute-done | bytes 20512 | tf_op jit(solution)/shard_map/ppermute | solution.py:687
  14.5 0.6 %shard_map.56.scaling = f32[2,72,256]{2,1,0:T(8,128)S(1)} custom-call(f32[8,64,256]{2,1,0:T(8,128)S(1)} %copy-done.3, s32[8,64,256]{2,1,0:T(8,128)S(1)} %copy-done.1, f32[5,64,256]{2,1,0:T(8,128)S(1)} %collective-permute-done.beyond.crossed, f32[25,4,256]{2,1,0:T(4,128)S(1)} %collective-permute-done.1.refs_0_.refs_1_, ...), custom_call_target="tpu_custom_call" | custom-call | flops 2097152 | bytes 1048576 | tf_op jit(solution)/shard_map/pallas_call | solution.py:703
  15.2 0.5 %shard_map.59 = (f32[2,72,256]{2,1,0:T(8,128)S(1)}, f32[3,72,256]{2,1,0:T(8,128)S(1)}) custom-call(f32[2,72,256]{2,1,0:T(8,128)S(1)} %shard_map.56.scaling, f32[2,72,256]{2,1,0:T(8,128)S(1)} %get-tuple-element.17.mine, f32[5,72,256]{2,1,0:T(8,128)S(1)} %collective-permute-done.4.received, s32[2,1]{1,0:T(2,128)S(1)} %copy.7.ratio, ...), custom_call_target="tpu_custom_call" | custom-call | flops 4194304 | bytes 1048576 | tf_op jit(solution)/shard_map/pallas_call | solution.py:738
  15.7 2.1 %collective-permute-start.7 = (f32[3,72,256]{2,1,0:T(8,128)S(1)}, f32[3,72,256]{2,1,0:T(8,128)S(1)}, u32[]{:S(2)}, u32[]{:S(2)}) collective-permute-start(f32[3,72,256]{2,1,0:T(8,128)S(1)} %get-tuple-element.20.outgoing), channel_id=1, source_target_pairs={{4,1},{6,3},{1,4},{3,6},{8,5},{10,7},{5,8},{7,10},{12,9},{14,11},{... | collective-permute-start | bytes 663560 | tf_op jit(solution)/shard_map/ppermute | solution.py:748
  17.8 1.3 %shard_map.61.mine = f32[4,72,256]{2,1,0:T(8,128)S(1)} custom-call(f32[1,3,8,64,256]{4,3,2,1,0:T(8,128)S(1)} %copy-done, s32[8,64,256]{2,1,0:T(8,128)S(1)} %copy-done.2, s32[2,1]{1,0:T(2,128)S(1)} %copy.7.ratio, f32[15,4,256]{2,1,0:T(4,128)S(1)} %collective-permute-done.3.refs_0_, f32[25,4,256]{2,1,0:T(4,128)S(1)} %collective-permute-done.1.refs_0_.refs_1_), custom_call_target="tpu_custom_call" | custom-call | flops 8388608 | bytes 1048576 | tf_op jit(solution)/shard_map/pallas_call | solution.py:694
  19.1 0.6 %collective-permute-start.6 = (f32[4,72,256]{2,1,0:T(8,128)S(1)}, f32[4,72,256]{2,1,0:T(8,128)S(1)}, u32[]{:S(2)}, u32[]{:S(2)}) collective-permute-start(f32[4,72,256]{2,1,0:T(8,128)S(1)} %shard_map.61.mine), channel_id=1, source_target_pairs={{0,1},{1,0},{2,3},{3,2},{4,5},{5,4},{6,7},{7,6},{8,9},{9,8},{10,11... | collective-permute-start | bytes 884744 | tf_op jit(solution)/shard_map/ppermute | solution.py:736
  19.7 2.0 %collective-permute-done.7.received = f32[3,72,256]{2,1,0:T(8,128)S(1)} collective-permute-done((f32[3,72,256]{2,1,0:T(8,128)S(1)}, f32[3,72,256]{2,1,0:T(8,128)S(1)}, u32[]{:S(2)}, u32[]{:S(2)}) %collective-permute-start.7) | collective-permute-done | bytes 221216 | tf_op jit(solution)/shard_map/ppermute | solution.py:748
  21.7 0.8 %collective-permute-start.8 = (f32[3,72,256]{2,1,0:T(8,128)S(1)}, f32[3,72,256]{2,1,0:T(8,128)S(1)}, u32[]{:S(2)}, u32[]{:S(2)}) collective-permute-start(f32[3,72,256]{2,1,0:T(8,128)S(1)} %shard_map.64.ends), channel_id=1, source_target_pairs={{0,1},{1,0},{2,3},{3,2},{4,5},{5,4},{6,7},{7,6},{8,9},{9,8},{10,11... | collective-permute-start | bytes 663560 | tf_op jit(solution)/shard_map/ppermute | solution.py:760
  22.5 0.1 collective-permute-start.5
  22.6 0.9 %shard_map.60.scaling = f32[4,72,256]{2,1,0:T(8,128)S(1)} custom-call(f32[8,64,256]{2,1,0:T(8,128)S(1)} %copy-done.3, s32[8,64,256]{2,1,0:T(8,128)S(1)} %copy-done.1, f32[25,4,256]{2,1,0:T(4,128)S(1)} %collective-permute-done.1.refs_0_.refs_1_), custom_call_target="tpu_custom_call" | custom-call | flops 2097152 | bytes 1048576 | tf_op jit(solution)/shard_map/pallas_call | solution.py:703
  23.5 0.3 %collective-permute-done.5.other.first = f32[2,72,256]{2,1,0:T(8,128)S(1)} collective-permute-done((f32[2,72,256]{2,1,0:T(8,128)S(1)}, f32[2,72,256]{2,1,0:T(8,128)S(1)}, u32[]{:S(2)}, u32[]{:S(2)}) %collective-permute-start.5) | collective-permute-done | bytes 147488 | tf_op jit(solution)/shard_map/ppermute | solution.py:749
  23.8 0.4 %shard_map.65.inner = f32[2,64,256]{2,1,0:T(8,128)S(1)} custom-call(s32[8,64,256]{2,1,0:T(8,128)S(1)} %copy-done.1, f32[2,72,256]{2,1,0:T(8,128)S(1)} %get-tuple-element.19.own.first, f32[2,72,256]{2,1,0:T(8,128)S(1)} %collective-permute-done.5.other.first, f32[4,72,256]{2,1,0:T(8,128)S(1)} %shard_map.62.middle), custom_call_target="tpu_custom_call" | custom-call | flops 4194304 | bytes 1048576 | tf_op jit(solution)/shard_map/pallas_call | solution.py:750
  24.2 0.5 %shard_map.66.near = f32[3,64,256]{2,1,0:T(8,128)S(1)} custom-call(s32[8,64,256]{2,1,0:T(8,128)S(1)} %copy-done.1, f32[2,72,256]{2,1,0:T(8,128)S(1)} %get-tuple-element.19.own.first, f32[4,72,256]{2,1,0:T(8,128)S(1)} %shard_map.62.middle, f32[3,72,256]{2,1,0:T(8,128)S(1)} %shard_map.64.ends), custom_call_target="tpu_custom_call" | custom-call | flops 2097152 | bytes 1048576 | tf_op jit(solution)/shard_map/pallas_call | solution.py:762
  24.8 1.2 %shard_map.67 = f32[8,64,256]{2,1,0:T(8,128)} custom-call(s32[8,64,256]{2,1,0:T(8,128)S(1)} %copy-done.1, f32[2,72,256]{2,1,0:T(8,128)S(1)} %collective-permute-done.5.other.first, f32[4,72,256]{2,1,0:T(8,128)S(1)} %shard_map.62.middle, f32[3,72,256]{2,1,0:T(8,128)S(1)} %collective-permute-done.8.ends, f32[2,64,256]{2,1,0:T(8,128)S(1)} %shard_map.65.inner, ...), custom_call_target="tpu_custom_call" | custom-call | flops 2097152 | bytes 1048576 | tf_op jit(solution)/shard_map/pallas_call | solution.py:765
  (18 shorter events, 0.1 us)
Async XLA Ops:
  0.0 4.6 %copy-start.2 = (s32[8,64,256]{2,1,0:T(8,128)S(1)}, s32[8,64,256]{2,1,0:T(8,128)}, u32[]{:S(2)}) copy-start(s32[8,64,256]{2,1,0:T(8,128)} %fixed.9) | copy-start | bytes 1572868
  0.0 4.6 %copy-start = (f32[1,3,8,64,256]{4,3,2,1,0:T(8,128)S(1)}, f32[1,3,8,64,256]{4,3,2,1,0:T(8,128)}, u32[]{:S(2)}) copy-start(f32[1,3,8,64,256]{4,3,2,1,0:T(8,128)} %displacement.9) | copy-start | bytes 4718596
  0.0 4.5 %copy-start.4 = (s32[2]{0:T(128)S(1)}, s32[2]{0:T(128)}, u32[]{:S(2)}) copy-start(s32[2]{0:T(128)} %param.9) | copy-start | bytes 28
  1.5 5.2 %collective-permute-start.3 = (f32[15,4,256]{2,1,0:T(4,128)S(1)}, f32[15,4,256]{2,1,0:T(4,128)S(1)}, u32[]{:S(2)}, u32[]{:S(2)}) collective-permute-start(f32[15,4,256]{2,1,0:T(4,128)S(1)} %get-tuple-element.16), channel_id=1, source_target_pairs={{0,2},{2,0},{1,3},{3,1},{4,6},{6,4},{5,7},{7,5},{8,10},{10,8},{9,1... | collective-permute-start | bytes 184328 | tf_op jit(solution)/shard_map/ppermute | solution.py:689
  5.5 9.0 %copy-start.1 = (s32[8,64,256]{2,1,0:T(8,128)S(1)}, s32[8,64,256]{2,1,0:T(8,128)}, u32[]{:S(2)}) copy-start(s32[8,64,256]{2,1,0:T(8,128)} %void.11) | copy-start | bytes 1572868
  5.5 9.0 %copy-start.3 = (f32[8,64,256]{2,1,0:T(8,128)S(1)}, f32[8,64,256]{2,1,0:T(8,128)}, u32[]{:S(2)}) copy-start(f32[8,64,256]{2,1,0:T(8,128)} %density.5) | copy-start | bytes 1572868
  7.0 8.1 %collective-permute-start.4 = (f32[5,72,256]{2,1,0:T(8,128)S(1)}, f32[5,72,256]{2,1,0:T(8,128)S(1)}, u32[]{:S(2)}, u32[]{:S(2)}) collective-permute-start(f32[5,72,256]{2,1,0:T(8,128)S(1)} %get-tuple-element.18), channel_id=1, source_target_pairs={{0,1},{1,0},{2,3},{3,2},{4,5},{5,4},{6,7},{7,6},{8,9},{9,8},{10,11... | collective-permute-start | bytes 1105928 | tf_op jit(solution)/shard_map/ppermute | solution.py:722
  7.1 7.4 %collective-permute-start = (f32[5,64,256]{2,1,0:T(8,128)S(1)}, f32[5,64,256]{2,1,0:T(8,128)S(1)}, u32[]{:S(2)}, u32[]{:S(2)}) collective-permute-start(f32[5,64,256]{2,1,0:T(8,128)S(1)} %get-tuple-element.13), channel_id=1, source_target_pairs={{4,1},{6,3},{1,4},{3,6},{8,5},{10,7},{5,8},{7,10},{12,9},{14,11},{... | collective-permute-start | bytes 983048 | tf_op jit(solution)/shard_map/ppermute | solution.py:686
  9.2 5.3 %collective-permute-start.1 = (f32[25,4,256]{2,1,0:T(4,128)S(1)}, f32[25,4,256]{2,1,0:T(4,128)S(1)}, u32[]{:S(2)}, u32[]{:S(2)}) collective-permute-start(f32[25,4,256]{2,1,0:T(4,128)S(1)} %get-tuple-element.14), channel_id=1, source_target_pairs={{0,2},{2,0},{1,3},{3,1},{4,6},{6,4},{5,7},{7,5},{8,10},{10,8},{9,1... | collective-permute-start | bytes 307208 | tf_op jit(solution)/shard_map/ppermute | solution.py:689
  10.7 3.8 %collective-permute-start.2 = (f32[5,4,256]{2,1,0:T(4,128)S(1)}, f32[5,4,256]{2,1,0:T(4,128)S(1)}, u32[]{:S(2)}, u32[]{:S(2)}) collective-permute-start(f32[5,4,256]{2,1,0:T(4,128)S(1)} %get-tuple-element.15), channel_id=1, source_target_pairs={{4,3},{6,1},{1,6},{3,4},{8,7},{10,5},{5,10},{7,8},{12,11},{14,9},{... | collective-permute-start | bytes 61448 | tf_op jit(solution)/shard_map/ppermute | solution.py:687
  15.7 6.0 %collective-permute-start.7 = (f32[3,72,256]{2,1,0:T(8,128)S(1)}, f32[3,72,256]{2,1,0:T(8,128)S(1)}, u32[]{:S(2)}, u32[]{:S(2)}) collective-permute-start(f32[3,72,256]{2,1,0:T(8,128)S(1)} %get-tuple-element.20.outgoing), channel_id=1, source_target_pairs={{4,1},{6,3},{1,4},{3,6},{8,5},{10,7},{5,8},{7,10},{12,9},{14,11},{... | collective-permute-start | bytes 663560 | tf_op jit(solution)/shard_map/ppermute | solution.py:748
  19.1 4.4 %collective-permute-start.6 = (f32[4,72,256]{2,1,0:T(8,128)S(1)}, f32[4,72,256]{2,1,0:T(8,128)S(1)}, u32[]{:S(2)}, u32[]{:S(2)}) collective-permute-start(f32[4,72,256]{2,1,0:T(8,128)S(1)} %shard_map.61.mine), channel_id=1, source_target_pairs={{0,1},{1,0},{2,3},{3,2},{4,5},{5,4},{6,7},{7,6},{8,9},{9,8},{10,11... | collective-permute-start | bytes 884744 | tf_op jit(solution)/shard_map/ppermute | solution.py:736
  21.7 3.1 %collective-permute-start.8 = (f32[3,72,256]{2,1,0:T(8,128)S(1)}, f32[3,72,256]{2,1,0:T(8,128)S(1)}, u32[]{:S(2)}, u32[]{:S(2)}) collective-permute-start(f32[3,72,256]{2,1,0:T(8,128)S(1)} %shard_map.64.ends), channel_id=1, source_target_pairs={{0,1},{1,0},{2,3},{3,2},{4,5},{5,4},{6,7},{7,6},{8,9},{9,8},{10,11... | collective-permute-start | bytes 663560 | tf_op jit(solution)/shard_map/ppermute | solution.py:760
  22.5 1.4 %collective-permute-start.5 = (f32[2,72,256]{2,1,0:T(8,128)S(1)}, f32[2,72,256]{2,1,0:T(8,128)S(1)}, u32[]{:S(2)}, u32[]{:S(2)}) collective-permute-start(f32[2,72,256]{2,1,0:T(8,128)S(1)} %get-tuple-element.19.own.first), channel_id=1, source_target_pairs={{0,1},{1,0},{2,3},{3,2},{4,5},{5,4},{6,7},{7,6},{8,9},{9,8},{10,11... | collective-permute-start | bytes 442376 | tf_op jit(solution)/shard_map/ppermute | solution.py:749

commit v7 on v6

--- a/solution.py
+++ b/solution.py
@@ -583,18 +583,16 @@
     side_rows(lax.axis_index("lc"), void, first, middle, ends, result, field, sums)
 
 
-def far_kernel(void, first, middle, ends, inner, near, gradient, field, sums, far, sems):
-    layers = void.shape[0]
+def gather_kernel(inner, near, far, gradient, sems):
+    layers = gradient.shape[0]
     core = lax.axis_index("lc")
     copies = [
         pltpu.make_async_copy(inner, gradient.at[pl.ds(3, layers - 6)], sems.at[0]),
         pltpu.make_async_copy(near, gradient.at[pl.ds(core * (layers - 3), 3)], sems.at[1]),
         pltpu.make_async_copy(far, gradient.at[pl.ds((1 - core) * (layers - 3), 3)], sems.at[2]),
     ]
-    for copy in copies[:2]:
+    for copy in copies:
         copy.start()
-    side_rows(1 - core, void, first, middle, ends, far, field, sums)
-    copies[2].start()
     for copy in copies:
         copy.wait()
 
@@ -722,17 +720,9 @@
     received = lax.ppermute(theirs, "lc", swap)
     scaling_rest = scaling(scaling_rest_kernel, layers - 4, *rests)
     (mine_rest,) = energy(
-        functools.partial(energy_rest_kernel, count),
-        layers - 3,
-        wide,
-        [],
-        [(layers - 4, wide, depth)],
-        *halos,
-        *rests,
+        functools.partial(energy_rest_kernel, count), layers - 3, wide, [], [(layers - 4, wide, depth)], *halos, *rests
     )
-    (crown,) = energy(
-        functools.partial(crown_kernel, count), 1, wide, [], [(1, wide, depth)], *halos
-    )
+    (crown,) = energy(functools.partial(crown_kernel, count), 1, wide, [], [(1, wide, depth)], *halos)
     received_rest = lax.ppermute(mine_rest, "lc", swap)
     scaling_first = scaling(scaling_first_kernel, 2, crossed, *rests, *corners)
     first, outgoing = call(
@@ -757,20 +747,12 @@
     (own_ends,) = call(ends_kernel, [(3, wide, depth)], [], [vmem()] * 4, 1 << 18)(
         scaling_first, crown, outgoing, beyond
     )
-    other_ends = lax.ppermute(own_ends, "lc", swap)
     held = [((7, wide, depth), real), ((7, 2, wide, depth), real)]
-    (near,) = call(near_kernel, [(3, rows, depth)], held, [vmem()] * 4, 1 << 21)(
-        void_mask, first, middle, own_ends
-    )
+    (near,) = call(near_kernel, [(3, rows, depth)], held, [vmem()] * 4, 1 << 21)(void_mask, first, middle, own_ends)
+    far = lax.ppermute(near, "lc", swap)
     (gradient,) = call(
-        far_kernel,
-        [(layers, rows, depth)],
-        held + [((3, rows, depth), real)],
-        [vmem()] * 6,
-        1 << 21,
-        out_specs=[hbm()],
-        sems=3,
-    )(void_mask, other, middle, other_ends, inner, near)
+        gather_kernel, [(layers, rows, depth)], [], [vmem()] * 3, 1 << 18, out_specs=[hbm()], sems=3
+    )(inner, near, far)
     return gradient
 
 

time: 26.1 us -> 30.3 us (1.16)
  waiting for transfers between devices: 6.74 us -> 12.7 us
  starting transfers between devices: 10.7 us -> 9.31 us
  Pallas kernels: 8.26 us -> 7.9 us
    ppermute x2, waiting for transfers between devices: 1.19 us -> 4.68 us  [shards(): lax.ppermute(a, 'gy', y_pairs(step))]
    ppermute x1, waiting for transfers between devices: 1.97 us -> 4 us  [shards(): beyond = lax.ppermute(outgoing, axes, crossing)]
    ppermute x1, starting transfers between devices: 2.08 us -> 0.98 us  [shards(): beyond = lax.ppermute(outgoing, axes, crossing)]
    ppermute x1, waiting for transfers between devices: 0.29 us -> 1.14 us  [shards(): other = lax.ppermute(first, 'lc', swap)]
    ppermute x1, starting transfers between devices: 0.77 us -> 0.24 us  [shards(): far = lax.ppermute(near, 'lc', swap)]
    ppermute x1, starting transfers between devices: 0.59 us -> 0.07 us  [shards(): received_rest = lax.ppermute(mine_rest, 'lc', swap)]
    ppermute x1, starting transfers between devices: 0.51 us -> 0.98 us  [shards(): lax.ppermute(a, axes, diagonal(step))]
    ppermute x1, waiting for transfers between devices: 3.28 us -> 2.87 us  [shards(): lax.ppermute(a, axes, diagonal(step))]
  transfers between devices with their start and end apart: 9 -> 9, of which waited for: 4 -> 5; matrix products, arithmetic and copies ran while one was open for 0% -> 0% of each run, Pallas kernels for 18% -> 16%
where the time goes in v7:
time: 30.3 us; the launch traced here: 30.1 us
  waiting for transfers between devices  12.7 us (42%)
  starting transfers between devices  9.31 us (31%)
  Pallas kernels  7.9 us (26%)
    ppermute x2, waiting for transfers between devices, shards(): lax.ppermute(a, 'gy', y_pairs(step))  4.68 us
    ppermute x2, starting transfers between devices, shards(): lax.ppermute(a, 'gy', y_pairs(step))  4.52 us
    ppermute x1, waiting for transfers between devices, shards(): beyond = lax.ppermute(outgoing, axes, crossing)  4 us
    ppermute x1, waiting for transfers between devices, shards(): lax.ppermute(a, axes, diagonal(step))  2.87 us
    pallas_call x4, Pallas kernels, energy(): call(kernel, outs, [((3, held, high, depth), real), ((held, 6, high, dept...  2.55 us
    ppermute x1, starting transfers between devices, shards(): crossed = lax.ppermute(crossing_out, axes, crossing)  2.11 us
    pallas_call x2, Pallas kernels, scaling(): call(functools.partial(kernel, count), [(held, wide, depth)], [((held + 4...  1.59 us
    pallas_call x1, Pallas kernels, shards(): call(functools.partial(prepare_kernel, sides), [(5, rows, depth)] + [(siz...  1.45 us
  transfers between devices with their start and end apart: 9, of which 5 were waited for; matrix products, arithmetic and copies ran while one was open for 0% of the time, Pallas kernels for 16%

profile of v7, /device:TPU:0, one launch (start us, length us, event | category | flops | bytes accessed | tf_op | source)
XLA Modules:
  0.0 30.1 jit_solution(14005764284958448101)
XLA Ops:
  0.0 1.4 %shard_map.55 = (f32[5,64,256]{2,1,0:T(8,128)S(1)}, f32[5,4,256]{2,1,0:T(4,128)S(1)}, f32[15,4,256]{2,1,0:T(4,128)S(1)}, f32[25,4,256]{2,1,0:T(4,128)S(1)}) custom-call(f32[1,3,8,64,256]{4,3,2,1,0:T(8,128)} %displacement.9, s32[8,64,256]{2,1,0:T(8,128)} %fixed.9, f32[8,64,256]{2,1,0:T(8,128)} %density.5, s32[8,64,256]{2,1,0:T(8,128)} %void.9), custom_call_target="tpu_custom_call" | custom-call | flops 262144 | bytes 1048576 | tf_op jit(solution)/shard_map/pallas_call | solution.py:674
  1.5 3.0 %collective-permute-start.3 = (f32[15,4,256]{2,1,0:T(4,128)S(1)}, f32[15,4,256]{2,1,0:T(4,128)S(1)}, u32[]{:S(2)}, u32[]{:S(2)}) collective-permute-start(f32[15,4,256]{2,1,0:T(4,128)S(1)} %get-tuple-element.16), channel_id=1, source_target_pairs={{0,2},{2,0},{1,3},{3,1},{4,6},{6,4},{5,7},{7,5},{8,10},{10,8},{9,1... | collective-permute-start | bytes 184328 | tf_op jit(solution)/shard_map/ppermute | solution.py:687
  4.5 0.1 copy.7.ratio
  4.6 0.9 %shard_map.57.bulk = f32[3,56,256]{2,1,0:T(8,128)S(1)} custom-call(f32[1,3,8,64,256]{4,3,2,1,0:T(8,128)S(1)} %copy-done, s32[8,64,256]{2,1,0:T(8,128)S(1)} %copy-done.2, s32[2,1]{1,0:T(2,128)S(1)} %copy.7.ratio), custom_call_target="tpu_custom_call" | custom-call | flops 8388608 | bytes 1048576 | tf_op jit(solution)/shard_map/pallas_call | solution.py:692
  5.5 1.2 %collective-permute-done.3.refs_0_ = f32[15,4,256]{2,1,0:T(4,128)S(1)} collective-permute-done((f32[15,4,256]{2,1,0:T(4,128)S(1)}, f32[15,4,256]{2,1,0:T(4,128)S(1)}, u32[]{:S(2)}, u32[]{:S(2)}) %collective-permute-start.3) | collective-permute-done | bytes 61472 | tf_op jit(solution)/shard_map/ppermute | solution.py:687
  6.7 0.3 %shard_map.58 = (f32[2,72,256]{2,1,0:T(8,128)S(1)}, f32[5,72,256]{2,1,0:T(8,128)S(1)}) custom-call(f32[1,3,8,64,256]{4,3,2,1,0:T(8,128)S(1)} %copy-done, s32[8,64,256]{2,1,0:T(8,128)S(1)} %copy-done.2, s32[2,1]{1,0:T(2,128)S(1)} %copy.7.ratio, f32[3,56,256]{2,1,0:T(8,128)S(1)} %shard_map.57.bulk, f32[15,4,256]{2,1,0:T(4,128)S(1)} %collective-permute-done.3.refs_0_), custom_call_target="tpu_custom_call" | custom-call | flops 8388608 | bytes 1048576 | tf_op jit(solution)/shard_map/pallas_call | solution.py:692
  7.0 0.1 collective-permute-start.4
  7.1 2.1 %collective-permute-start = (f32[5,64,256]{2,1,0:T(8,128)S(1)}, f32[5,64,256]{2,1,0:T(8,128)S(1)}, u32[]{:S(2)}, u32[]{:S(2)}) collective-permute-start(f32[5,64,256]{2,1,0:T(8,128)S(1)} %get-tuple-element.13), channel_id=1, source_target_pairs={{4,1},{6,3},{1,4},{3,6},{8,5},{10,7},{5,8},{7,10},{12,9},{14,11},{... | collective-permute-start | bytes 983048 | tf_op jit(solution)/shard_map/ppermute | solution.py:684
  9.2 1.5 %collective-permute-start.1 = (f32[25,4,256]{2,1,0:T(4,128)S(1)}, f32[25,4,256]{2,1,0:T(4,128)S(1)}, u32[]{:S(2)}, u32[]{:S(2)}) collective-permute-start(f32[25,4,256]{2,1,0:T(4,128)S(1)} %get-tuple-element.14), channel_id=1, source_target_pairs={{0,2},{2,0},{1,3},{3,1},{4,6},{6,4},{5,7},{7,5},{8,10},{10,8},{9,1... | collective-permute-start | bytes 307208 | tf_op jit(solution)/shard_map/ppermute | solution.py:687
  10.7 3.5 %collective-permute-done.1.refs_0_.refs_1_ = f32[25,4,256]{2,1,0:T(4,128)S(1)} collective-permute-done((f32[25,4,256]{2,1,0:T(4,128)S(1)}, f32[25,4,256]{2,1,0:T(4,128)S(1)}, u32[]{:S(2)}, u32[]{:S(2)}) %collective-permute-start.1) | collective-permute-done | bytes 102432 | tf_op jit(solution)/shard_map/ppermute | solution.py:687
  14.2 1.3 %shard_map.61.mine = f32[4,72,256]{2,1,0:T(8,128)S(1)} custom-call(f32[1,3,8,64,256]{4,3,2,1,0:T(8,128)S(1)} %copy-done, s32[8,64,256]{2,1,0:T(8,128)S(1)} %copy-done.2, s32[2,1]{1,0:T(2,128)S(1)} %copy.7.ratio, f32[15,4,256]{2,1,0:T(4,128)S(1)} %collective-permute-done.3.refs_0_, f32[25,4,256]{2,1,0:T(4,128)S(1)} %collective-permute-done.1.refs_0_.refs_1_), custom_call_target="tpu_custom_call" | custom-call | flops 8388608 | bytes 1048576 | tf_op jit(solution)/shard_map/pallas_call | solution.py:692
  15.6 1.0 %collective-permute-start.2 = (f32[5,4,256]{2,1,0:T(4,128)S(1)}, f32[5,4,256]{2,1,0:T(4,128)S(1)}, u32[]{:S(2)}, u32[]{:S(2)}) collective-permute-start(f32[5,4,256]{2,1,0:T(4,128)S(1)} %get-tuple-element.15), channel_id=1, source_target_pairs={{4,3},{6,1},{1,6},{3,4},{8,7},{10,5},{5,10},{7,8},{12,11},{14,9},{... | collective-permute-start | bytes 61448 | tf_op jit(solution)/shard_map/ppermute | solution.py:685
  16.6 2.9 %collective-permute-done.2.refs_1_.refs_0_ = f32[5,4,256]{2,1,0:T(4,128)S(1)} collective-permute-done((f32[5,4,256]{2,1,0:T(4,128)S(1)}, f32[5,4,256]{2,1,0:T(4,128)S(1)}, u32[]{:S(2)}, u32[]{:S(2)}) %collective-permute-start.2) | collective-permute-done | bytes 20512 | tf_op jit(solution)/shard_map/ppermute | solution.py:685
  19.5 0.6 %shard_map.56.scaling = f32[2,72,256]{2,1,0:T(8,128)S(1)} custom-call(f32[8,64,256]{2,1,0:T(8,128)S(1)} %copy-done.3, s32[8,64,256]{2,1,0:T(8,128)S(1)} %copy-done.1, f32[5,64,256]{2,1,0:T(8,128)S(1)} %collective-permute-done.beyond.crossed, f32[25,4,256]{2,1,0:T(4,128)S(1)} %collective-permute-done.1.refs_0_.refs_1_, ...), custom_call_target="tpu_custom_call" | custom-call | flops 2097152 | bytes 1048576 | tf_op jit(solution)/shard_map/pallas_call | solution.py:701
  20.2 0.5 %shard_map.59 = (f32[2,72,256]{2,1,0:T(8,128)S(1)}, f32[3,72,256]{2,1,0:T(8,128)S(1)}) custom-call(f32[2,72,256]{2,1,0:T(8,128)S(1)} %shard_map.56.scaling, f32[2,72,256]{2,1,0:T(8,128)S(1)} %get-tuple-element.17.mine, f32[5,72,256]{2,1,0:T(8,128)S(1)} %collective-permute-done.4.received, s32[2,1]{1,0:T(2,128)S(1)} %copy.7.ratio, ...), custom_call_target="tpu_custom_call" | custom-call | flops 4194304 | bytes 1048576 | tf_op jit(solution)/shard_map/pallas_call | solution.py:728
  20.6 1.0 %collective-permute-start.7 = (f32[3,72,256]{2,1,0:T(8,128)S(1)}, f32[3,72,256]{2,1,0:T(8,128)S(1)}, u32[]{:S(2)}, u32[]{:S(2)}) collective-permute-start(f32[3,72,256]{2,1,0:T(8,128)S(1)} %get-tuple-element.20.outgoing), channel_id=1, source_target_pairs={{4,1},{6,3},{1,4},{3,6},{8,5},{10,7},{5,8},{7,10},{12,9},{14,11},{... | collective-permute-start | bytes 663560 | tf_op jit(solution)/shard_map/ppermute | solution.py:738
  21.6 0.9 %shard_map.60.scaling = f32[4,72,256]{2,1,0:T(8,128)S(1)} custom-call(f32[8,64,256]{2,1,0:T(8,128)S(1)} %copy-done.3, s32[8,64,256]{2,1,0:T(8,128)S(1)} %copy-done.1, f32[25,4,256]{2,1,0:T(4,128)S(1)} %collective-permute-done.1.refs_0_.refs_1_), custom_call_target="tpu_custom_call" | custom-call | flops 2097152 | bytes 1048576 | tf_op jit(solution)/shard_map/pallas_call | solution.py:701
  22.6 4.0 %collective-permute-done.7.received = f32[3,72,256]{2,1,0:T(8,128)S(1)} collective-permute-done((f32[3,72,256]{2,1,0:T(8,128)S(1)}, f32[3,72,256]{2,1,0:T(8,128)S(1)}, u32[]{:S(2)}, u32[]{:S(2)}) %collective-permute-start.7) | collective-permute-done | bytes 221216 | tf_op jit(solution)/shard_map/ppermute | solution.py:738
  26.7 0.5 %shard_map.66.near = f32[3,64,256]{2,1,0:T(8,128)S(1)} custom-call(s32[8,64,256]{2,1,0:T(8,128)S(1)} %copy-done.1, f32[2,72,256]{2,1,0:T(8,128)S(1)} %get-tuple-element.19.own.first, f32[4,72,256]{2,1,0:T(8,128)S(1)} %shard_map.62.middle, f32[3,72,256]{2,1,0:T(8,128)S(1)} %shard_map.65.ends), custom_call_target="tpu_custom_call" | custom-call | flops 2097152 | bytes 1048576 | tf_op jit(solution)/shard_map/pallas_call | solution.py:751
  27.2 0.2 collective-permute-start.8
  27.4 0.3 %collective-permute-start.5 = (f32[2,72,256]{2,1,0:T(8,128)S(1)}, f32[2,72,256]{2,1,0:T(8,128)S(1)}, u32[]{:S(2)}, u32[]{:S(2)}) collective-permute-start(f32[2,72,256]{2,1,0:T(8,128)S(1)} %get-tuple-element.19.own.first), channel_id=1, source_target_pairs={{0,1},{1,0},{2,3},{3,2},{4,5},{5,4},{6,7},{7,6},{8,9},{9,8},{10,11... | collective-permute-start | bytes 442376 | tf_op jit(solution)/shard_map/ppermute | solution.py:739
  27.8 1.1 %collective-permute-done.5.other = f32[2,72,256]{2,1,0:T(8,128)S(1)} collective-permute-done((f32[2,72,256]{2,1,0:T(8,128)S(1)}, f32[2,72,256]{2,1,0:T(8,128)S(1)}, u32[]{:S(2)}, u32[]{:S(2)}) %collective-permute-start.5) | collective-permute-done | bytes 147488 | tf_op jit(solution)/shard_map/ppermute | solution.py:739
  28.9 0.4 %shard_map.63.inner = f32[2,64,256]{2,1,0:T(8,128)S(1)} custom-call(s32[8,64,256]{2,1,0:T(8,128)S(1)} %copy-done.1, f32[2,72,256]{2,1,0:T(8,128)S(1)} %get-tuple-element.19.own.first, f32[2,72,256]{2,1,0:T(8,128)S(1)} %collective-permute-done.5.other, f32[4,72,256]{2,1,0:T(8,128)S(1)} %shard_map.62.middle), custom_call_target="tpu_custom_call" | custom-call | flops 4194304 | bytes 1048576 | tf_op jit(solution)/shard_map/pallas_call | solution.py:740
  29.3 0.8 %shard_map.67 = f32[8,64,256]{2,1,0:T(8,128)} custom-call(f32[2,64,256]{2,1,0:T(8,128)S(1)} %shard_map.63.inner, f32[3,64,256]{2,1,0:T(8,128)S(1)} %shard_map.66.near, f32[3,64,256]{2,1,0:T(8,128)S(1)} %collective-permute-done.8.far), custom_call_target="tpu_custom_call" | custom-call | flops 262144 | bytes 1048576 | tf_op jit(solution)/shard_map/pallas_call | solution.py:753
  (18 shorter events, 0.2 us)
Async XLA Ops:
  0.0 4.6 %copy-start.2 = (s32[8,64,256]{2,1,0:T(8,128)S(1)}, s32[8,64,256]{2,1,0:T(8,128)}, u32[]{:S(2)}) copy-start(s32[8,64,256]{2,1,0:T(8,128)} %fixed.9) | copy-start | bytes 1572868
  0.0 4.6 %copy-start = (f32[1,3,8,64,256]{4,3,2,1,0:T(8,128)S(1)}, f32[1,3,8,64,256]{4,3,2,1,0:T(8,128)}, u32[]{:S(2)}) copy-start(f32[1,3,8,64,256]{4,3,2,1,0:T(8,128)} %displacement.9) | copy-start | bytes 4718596
  0.0 4.5 %copy-start.4 = (s32[2]{0:T(128)S(1)}, s32[2]{0:T(128)}, u32[]{:S(2)}) copy-start(s32[2]{0:T(128)} %param.9) | copy-start | bytes 28
  1.5 5.2 %collective-permute-start.3 = (f32[15,4,256]{2,1,0:T(4,128)S(1)}, f32[15,4,256]{2,1,0:T(4,128)S(1)}, u32[]{:S(2)}, u32[]{:S(2)}) collective-permute-start(f32[15,4,256]{2,1,0:T(4,128)S(1)} %get-tuple-element.16), channel_id=1, source_target_pairs={{0,2},{2,0},{1,3},{3,1},{4,6},{6,4},{5,7},{7,5},{8,10},{10,8},{9,1... | collective-permute-start | bytes 184328 | tf_op jit(solution)/shard_map/ppermute | solution.py:687
  7.0 12.5 %copy-start.1 = (s32[8,64,256]{2,1,0:T(8,128)S(1)}, s32[8,64,256]{2,1,0:T(8,128)}, u32[]{:S(2)}) copy-start(s32[8,64,256]{2,1,0:T(8,128)} %void.9) | copy-start | bytes 1572868
  7.0 12.4 %copy-start.3 = (f32[8,64,256]{2,1,0:T(8,128)S(1)}, f32[8,64,256]{2,1,0:T(8,128)}, u32[]{:S(2)}) copy-start(f32[8,64,256]{2,1,0:T(8,128)} %density.5) | copy-start | bytes 1572868
  7.0 13.1 %collective-permute-start.4 = (f32[5,72,256]{2,1,0:T(8,128)S(1)}, f32[5,72,256]{2,1,0:T(8,128)S(1)}, u32[]{:S(2)}, u32[]{:S(2)}) collective-permute-start(f32[5,72,256]{2,1,0:T(8,128)S(1)} %get-tuple-element.18), channel_id=1, source_target_pairs={{0,1},{1,0},{2,3},{3,2},{4,5},{5,4},{6,7},{7,6},{8,9},{9,8},{10,11... | collective-permute-start | bytes 1105928 | tf_op jit(solution)/shard_map/ppermute | solution.py:720
  7.1 12.3 %collective-permute-start = (f32[5,64,256]{2,1,0:T(8,128)S(1)}, f32[5,64,256]{2,1,0:T(8,128)S(1)}, u32[]{:S(2)}, u32[]{:S(2)}) collective-permute-start(f32[5,64,256]{2,1,0:T(8,128)S(1)} %get-tuple-element.13), channel_id=1, source_target_pairs={{4,1},{6,3},{1,4},{3,6},{8,5},{10,7},{5,8},{7,10},{12,9},{14,11},{... | collective-permute-start | bytes 983048 | tf_op jit(solution)/shard_map/ppermute | solution.py:684
  9.2 5.0 %collective-permute-start.1 = (f32[25,4,256]{2,1,0:T(4,128)S(1)}, f32[25,4,256]{2,1,0:T(4,128)S(1)}, u32[]{:S(2)}, u32[]{:S(2)}) collective-permute-start(f32[25,4,256]{2,1,0:T(4,128)S(1)} %get-tuple-element.14), channel_id=1, source_target_pairs={{0,2},{2,0},{1,3},{3,1},{4,6},{6,4},{5,7},{7,5},{8,10},{10,8},{9,1... | collective-permute-start | bytes 307208 | tf_op jit(solution)/shard_map/ppermute | solution.py:687
  15.5 7.0 %collective-permute-start.6 = (f32[4,72,256]{2,1,0:T(8,128)S(1)}, f32[4,72,256]{2,1,0:T(8,128)S(1)}, u32[]{:S(2)}, u32[]{:S(2)}) collective-permute-start(f32[4,72,256]{2,1,0:T(8,128)S(1)} %shard_map.61.mine), channel_id=1, source_target_pairs={{0,1},{1,0},{2,3},{3,2},{4,5},{5,4},{6,7},{7,6},{8,9},{9,8},{10,11... | collective-permute-start | bytes 884744 | tf_op jit(solution)/shard_map/ppermute | solution.py:726
  15.6 3.8 %collective-permute-start.2 = (f32[5,4,256]{2,1,0:T(4,128)S(1)}, f32[5,4,256]{2,1,0:T(4,128)S(1)}, u32[]{:S(2)}, u32[]{:S(2)}) collective-permute-start(f32[5,4,256]{2,1,0:T(4,128)S(1)} %get-tuple-element.15), channel_id=1, source_target_pairs={{4,3},{6,1},{1,6},{3,4},{8,7},{10,5},{5,10},{7,8},{12,11},{14,9},{... | collective-permute-start | bytes 61448 | tf_op jit(solution)/shard_map/ppermute | solution.py:685
  20.6 6.0 %collective-permute-start.7 = (f32[3,72,256]{2,1,0:T(8,128)S(1)}, f32[3,72,256]{2,1,0:T(8,128)S(1)}, u32[]{:S(2)}, u32[]{:S(2)}) collective-permute-start(f32[3,72,256]{2,1,0:T(8,128)S(1)} %get-tuple-element.20.outgoing), channel_id=1, source_target_pairs={{4,1},{6,3},{1,4},{3,6},{8,5},{10,7},{5,8},{7,10},{12,9},{14,11},{... | collective-permute-start | bytes 663560 | tf_op jit(solution)/shard_map/ppermute | solution.py:738
  27.2 2.1 %collective-permute-start.8 = (f32[3,64,256]{2,1,0:T(8,128)S(1)}, f32[3,64,256]{2,1,0:T(8,128)S(1)}, u32[]{:S(2)}, u32[]{:S(2)}) collective-permute-start(f32[3,64,256]{2,1,0:T(8,128)S(1)} %shard_map.66.near), channel_id=1, source_target_pairs={{0,1},{1,0},{2,3},{3,2},{4,5},{5,4},{6,7},{7,6},{8,9},{9,8},{10,11... | collective-permute-start | bytes 589832 | tf_op jit(solution)/shard_map/ppermute | solution.py:752
  27.4 1.5 %collective-permute-start.5 = (f32[2,72,256]{2,1,0:T(8,128)S(1)}, f32[2,72,256]{2,1,0:T(8,128)S(1)}, u32[]{:S(2)}, u32[]{:S(2)}) collective-permute-start(f32[2,72,256]{2,1,0:T(8,128)S(1)} %get-tuple-element.19.own.first), channel_id=1, source_target_pairs={{0,1},{1,0},{2,3},{3,2},{4,5},{5,4},{6,7},{7,6},{8,9},{9,8},{10,11... | collective-permute-start | bytes 442376 | tf_op jit(solution)/shard_map/ppermute | solution.py:739
